TPU v7x, 128 devices: a whole 4x4x4 slice. The times are simulated.
128 devices in a mesh: grp: 4 (over z), seq: 32 (over x, y, core).
Axes of the slice: x: 4, y: 4, z: 4, core: 2. Of those that a mesh axis runs over, the one named last changes fastest.
Arguments:
- hidden_in: bfloat16 [96, 4096], P(None, ('grp', 'seq')), may hold values from -6 to 6
- norm_gain: float32 [4096], replicated, may hold values from 0.5 to 1.5
- w_ssm_in: bfloat16 [4096, 8192], P(None, ('grp', 'seq')), may hold values from -0.09375 to 0.09375
- w_ssm_gate: bfloat16 [4096, 8192], P(None, ('grp', 'seq')), may hold values from -0.09375 to 0.09375
- conv_weight: float32 [4, 8192], P(None, ('grp', 'seq')), may hold values from -3 to 3
- conv_bias: float32 [8192], P(('grp', 'seq')), may hold values from -0.5 to 0.5
- conv_state: bfloat16 [96, 3, 8192], P(None, None, ('grp', 'seq')), may hold values from -6 to 6
- w_state_proj: bfloat16 [8192, 288], P(('grp', 'seq')), may hold values from -0.0625 to 0.0625
- w_step: bfloat16 [256, 8192], P(None, ('grp', 'seq')), may hold values from -0.375 to 0.375
- step_bias: float32 [8192], P(('grp', 'seq')), may hold values from -4 to -1
- log_decay: float32 [16, 8192], P(None, ('grp', 'seq')), may hold values from 0 to 2.7
- skip_gain: float32 [8192], P(('grp', 'seq')), may hold values from 0.5 to 1.5
- ssm_state: float32 [96, 16, 8192], P(None, None, ('grp', 'seq')), may hold values from -6 to 6
- w_ssm_out: bfloat16 [8192, 4096], P(('grp', 'seq')), may hold values from -0.25 to 0.25
- w_query: bfloat16 [4096, 2048], P(None, 'grp'), may hold values from -6 to 6
- key_projection: bfloat16 [4096, 1024], P(None, 'grp'), may hold values from -0.09375 to 0.09375
- value_projection: bfloat16 [4096, 1024], P(None, 'grp'), may hold values from -0.09375 to 0.09375
- w_attn_out: bfloat16 [2048, 4096], P('grp', 'seq'), may hold values from -0.125 to 0.125
- w_mlp_gate: bfloat16 [4096, 14336], P(None, ('grp', 'seq')), may hold values from -0.09375 to 0.09375
- w_mlp_up: bfloat16 [4096, 14336], P(None, ('grp', 'seq')), may hold values from -0.09375 to 0.09375
- w_mlp_down: bfloat16 [14336, 4096], P(('grp', 'seq')), may hold values from -0.1875 to 0.1875
- cached_inputs: bfloat16 [96, 512, 4096], P('seq'), may hold values from -6 to 6
- window_lengths: int32 [96], replicated, may hold values from 1 to 512, as said below
Outputs:
- hidden_out: bfloat16 [96, 4096], P(None, ('grp', 'seq'))
- state_out: float32 [96, 16, 8192], P(None, None, ('grp', 'seq'))
Inputs may be any that keep to these rules, and one draw needn't show every extreme that they name: `window_lengths`: every sequence has at least one valid cached position, and some sequence fills the whole window of 512.
All inputs are finite; a program needn't handle non-finite values.
Results may differ from a plain program's by a relative error of at most 0.012.
The roundings to bfloat16 on the way count: a program that leaves them out, or rounds other values in their place, can miss the bound.
Values may be sent and summed in bfloat16 or wider, within the bound.
No kernel may reach another device: no remote copies, remote signals or barrier semaphores. Data moves between devices by JAX's collectives and lax.ppermute only.
A program may use at most 128 MiB of HBM per device.

v0:
```python
import functools

import jax
import jax.numpy as jnp
import numpy as np
from jax import lax
from jax.experimental import pallas as pl
from jax.experimental.pallas import tpu as pltpu
from jax.sharding import Mesh
from jax.sharding import PartitionSpec as P


HEAD_SIZE = 128
GRP_SEQ = ("grp", "seq_0", "seq_1", "seq_2")
SEQ = ("seq_0", "seq_1", "seq_2")
CHIPS = ("grp", "seq_0", "seq_1")
EPSILON = 1e-05
ROPE_BASE = 10000.0
F32 = jnp.float32
BF16 = jnp.bfloat16
NT = (((1,), (1,)), ((), ()))
TN = (((0,), (0,)), ((), ()))
RING = 4
ROWS = 144
SLOT = 16


def rotary_tables(count):
    half = HEAD_SIZE // 2
    frequency = np.float32(ROPE_BASE) ** (
        -(np.arange(half, dtype=np.float32) * np.float32(2.0)) / np.float32(HEAD_SIZE)
    )
    angles = np.arange(count, dtype=np.float32)[:, None] * frequency.astype(np.float32)
    cosine = np.cos(angles.astype(np.float64)).astype(np.float32)
    sine = np.sin(angles.astype(np.float64)).astype(np.float32)
    return (
        np.concatenate([cosine, cosine], axis=1),
        np.concatenate([-sine, sine], axis=1),
    )


def shifted(value, axis, step):
    size = lax.axis_size(axis)
    return lax.ppermute(value, axis, [(i, (i + step) % size) for i in range(size)])


def from_ring(value, axis):
    arrived = [value]
    for step in (1, 3, 2):
        arrived.append(shifted(value, axis, step))
    return [arrived[0], arrived[1], arrived[3], arrived[2]]


def dot(a, b):
    return jnp.dot(a, b, preferred_element_type=F32)


def here():
    return tuple(lax.axis_index(a).astype(jnp.int32) for a in GRP_SEQ)


def own_seq():
    _, x, y, c = here()
    return (x * RING + y) * 2 + c


def in_vmem(value):
    return pltpu.with_memory_space_constraint(value, pltpu.VMEM)


def vmem_call(kernel, outs, operands, lengths=None, scratch=(), limit=12 << 20):
    smem = pl.BlockSpec(memory_space=pltpu.SMEM)
    vmem = pl.BlockSpec(memory_space=pltpu.VMEM)
    scalars = () if lengths is None else (lengths,)
    return pl.pallas_call(
        kernel,
        out_shape=tuple(pltpu.VMEM(shape, dtype) if inner else jax.ShapeDtypeStruct(shape, dtype) for shape, dtype, inner in outs),
        in_specs=[smem] * len(scalars) + [vmem] * len(operands),
        out_specs=tuple(vmem for _ in outs),
        scratch_shapes=list(scratch),
        compiler_params=pltpu.CompilerParams(vmem_limit_bytes=limit),
    )(*scalars, *(in_vmem(v) for v in operands))


def window_kernel(lengths, rows, w_key, w_value, cosines, sines, key_out, value_out, *, chunk):
    step = pl.program_id(0)
    per_seq = 512 // chunk
    start = (step % per_seq) * chunk
    length = lengths[own_seq() * 3 + step // per_seq]

    @pl.when(start < length)
    def _():
        block = rows[0]
        keys = dot(block, w_key[...])
        begin = pl.multiple_of(start, chunk)
        cos = cosines[pl.ds(begin, chunk), :]
        sin = sines[pl.ds(begin, chunk), :]
        for head in range(keys.shape[1] // HEAD_SIZE):
            part = keys[:, head * HEAD_SIZE : (head + 1) * HEAD_SIZE]
            turned = part * cos + pltpu.roll(part, HEAD_SIZE // 2, 1) * sin
            key_out[0, :, head * HEAD_SIZE : (head + 1) * HEAD_SIZE] = turned.astype(BF16)
        value_out[0] = dot(block, w_value[...]).astype(BF16)

    @pl.when(start >= length)
    def _():
        key_out[...] = jnp.zeros_like(key_out)
        value_out[...] = jnp.zeros_like(value_out)


def window_rows(lengths, cached, w_key, w_value, cosines, sines, chunk=256):
    seqs, window, width = cached.shape
    per_seq = window // chunk
    columns = w_key.shape[1]
    whole = pl.BlockSpec(memory_space=pltpu.VMEM)
    out = jax.ShapeDtypeStruct((seqs, window, columns), BF16)

    def block_at(i, _):
        return (i // per_seq, i % per_seq, 0)

    return pl.pallas_call(
        functools.partial(window_kernel, chunk=chunk),
        out_shape=(out, out),
        grid_spec=pltpu.PrefetchScalarGridSpec(
            num_scalar_prefetch=1,
            grid=(seqs * per_seq,),
            in_specs=[pl.BlockSpec((1, chunk, width), block_at), whole, whole, whole, whole],
            out_specs=[
                pl.BlockSpec((1, chunk, columns), block_at),
                pl.BlockSpec((1, chunk, columns), block_at),
            ],
        ),
        compiler_params=pltpu.CompilerParams(vmem_limit_bytes=24 << 20),
    )(
        lengths,
        pltpu.with_memory_space_constraint(cached, pltpu.HBM),
        *(in_vmem(v) for v in (w_key, w_value, cosines, sines)),
    )


def inner_kernel(near, far, gain, w_in, w_proj, past, taps, bias, normed_out, conv_out, low_out):
    c = lax.axis_index("seq_2").astype(jnp.int32)
    rows, batch = near.shape[1], near.shape[2]
    total = jnp.zeros((rows, batch), F32)
    for slot in range(near.shape[0]):
        a = near[slot].astype(F32)
        b = far[slot].astype(F32)
        total = total + a * a + b * b
    width = gain.shape[0] * gain.shape[1]
    mean = jnp.sum(total, axis=0, keepdims=True) * (1.0 / width)
    scale = lax.rsqrt(mean + EPSILON)
    gains = gain[...].T
    mine = c == 0
    per_gain = gain.shape[1] // rows
    for slot in range(near.shape[0]):
        a = near[slot].astype(F32)
        b = far[slot].astype(F32)
        pair = (jnp.where(mine, a, b), jnp.where(mine, b, a))
        for k in range(2):
            j = 2 * slot + k
            at = (j % per_gain) * rows
            column = gains[at : at + rows, j // per_gain : j // per_gain + 1]
            normed_out[j * rows : (j + 1) * rows, :] = (pair[k] * scale * column).astype(BF16)
    fresh = dot(w_in[...], normed_out[...]).astype(BF16).astype(F32)
    params = jnp.concatenate([taps[...], bias[...], jnp.zeros((3, taps.shape[1]), F32)], axis=0).T
    mixed = params[:, 4:5] + params[:, 3:4] * fresh
    for k in range(past.shape[0]):
        mixed = mixed + past[k].astype(F32) * params[:, k : k + 1]
    conv = jax.nn.silu(mixed)
    conv_out[...] = conv
    low = lax.dot_general(w_proj[...], conv.astype(BF16), TN, preferred_element_type=F32)
    low = jnp.concatenate([low, jnp.zeros((low.shape[0], 128 - batch), F32)], axis=1)
    low_out[c] = low[0:ROWS]
    low_out[1 - c] = low[ROWS:]


def gate_kernel(normed, w_gate, w_mlp_gate, w_mlp_up, gate_out, act_out):
    gate_out[...] = jax.nn.silu(dot(w_gate[...], normed[...]))
    act = jax.nn.silu(dot(w_mlp_gate[...], normed[...])) * dot(w_mlp_up[...], normed[...])
    act_out[...] = act.astype(BF16)


def down_kernel(act, w_mlp_down, term_out):
    term_out[...] = lax.dot_general(act[...], w_mlp_down[...], TN, preferred_element_type=F32)


def attention_kernel(
    lengths, normed, w_query, w_key, w_value, keys, values, cosines, sines, out
):
    seqs, window = keys.shape[0], keys.shape[1]
    kv_heads = keys.shape[2] // HEAD_SIZE
    group = w_query.shape[1] // keys.shape[2]
    batch = normed.shape[1]
    first = own_seq() * seqs
    row = lax.broadcasted_iota(jnp.int32, (8, batch), 0)
    column = lax.broadcasted_iota(jnp.int32, (8, batch), 1)
    pick = jnp.where((column == first + row) & (row < seqs), 1.0, 0.0).astype(BF16)
    own = lax.dot_general(pick, normed[...], NT, preferred_element_type=F32).astype(BF16)
    query = dot(own, w_query[...])
    fresh_key = dot(own, w_key[...])
    fresh_value = dot(own, w_value[...]).astype(BF16).astype(F32)
    scale = HEAD_SIZE ** (-0.5)
    slot_ids = lax.broadcasted_iota(jnp.int32, (1, window), 1)
    out[...] = jnp.zeros((SLOT, HEAD_SIZE), F32)

    def turned(part, cos, sin):
        return (part * cos + pltpu.roll(part, HEAD_SIZE // 2, 1) * sin).astype(BF16)

    for b in range(seqs):
        length = lengths[first + b]
        cos = cosines[pl.ds(length, 1), :]
        sin = sines[pl.ds(length, 1), :]
        valid = slot_ids < length
        for g in range(kv_heads):
            lanes = slice(g * HEAD_SIZE, (g + 1) * HEAD_SIZE)
            heads = [
                query[b : b + 1, (g * group + i) * HEAD_SIZE : (g * group + i + 1) * HEAD_SIZE]
                for i in range(group)
            ]
            stacked = jnp.concatenate(heads + [jnp.zeros((8 - group, HEAD_SIZE), F32)], axis=0)
            q = turned(stacked, cos, sin)
            k_new = turned(jnp.broadcast_to(fresh_key[b : b + 1, lanes], (8, HEAD_SIZE)), cos, sin)
            scores = (
                lax.dot_general(q, keys[b, :, lanes], NT, preferred_element_type=F32) * scale
            )
            fresh = (
                jnp.sum(q.astype(F32) * k_new.astype(F32), axis=1, keepdims=True) * scale
            )
            scores = jnp.where(valid, scores, -1e30)
            top = jnp.maximum(jnp.max(scores, axis=1, keepdims=True), fresh)
            weights = jnp.where(valid, jnp.exp(scores - top), 0.0)
            weight_new = jnp.exp(fresh - top)
            denominator = jnp.sum(weights, axis=1, keepdims=True) + weight_new
            summed = dot(weights.astype(BF16), values[b, :, lanes])
            summed = summed + weight_new * fresh_value[b : b + 1, lanes]
            result = (summed / denominator).astype(BF16).astype(F32)
            at = (b * kv_heads + g) * group
            out[at : at + group, :] = result[0:group, :]


def pack_kernel(s0, s1, s2, s3, attended, out):
    out[0:ROWS, :] = (s0[...] + s1[...]) + (s2[...] + s3[...])
    out[ROWS:, :] = attended[...]


def combine_kernel(p0, p1, p2, p3, out):
    out[0:ROWS, :] = (p0[0:ROWS] + p1[0:ROWS]) + (p2[0:ROWS] + p3[0:ROWS])
    size = p0.shape[0] - ROWS
    for k, part in enumerate((p0, p1, p2, p3)):
        out[ROWS + k * size : ROWS + (k + 1) * size, :] = part[ROWS:, :]


def outer_kernel(
    near, far, w_step, log_decay, step_bias, skip, conv, gate, state, w_out, term, w_attn,
    state_out, keep_out, send_out, total,
):
    _, x, y, c = here()
    seq = own_seq()
    batch = conv.shape[1]
    mine = c == 0
    near_low = near[0:ROWS, 0:batch]
    far_low = far[0:ROWS, 0:batch]
    low = jnp.concatenate(
        [jnp.where(mine, near_low, far_low), jnp.where(mine, far_low, near_low)], axis=0
    )
    rank = w_step.shape[1]
    states = state.shape[0]
    params = jnp.concatenate(
        [jnp.exp(log_decay[...]), step_bias[...], skip[...], jnp.zeros((6, conv.shape[0]), F32)],
        axis=0,
    ).T
    step = jax.nn.softplus(
        dot(w_step[...], low[0:rank].astype(BF16)) + params[:, states : states + 1]
    )
    conv_value = conv[...]
    driven = step * conv_value
    mixed = params[:, states + 1 : states + 2] * conv_value
    for n in range(states):
        decay = jnp.exp(-step * params[:, n : n + 1])
        fresh = decay * state[n] + driven * low[rank + n : rank + n + 1]
        state_out[n] = fresh
        mixed = mixed + fresh * low[rank + states + n : rank + states + n + 1]
    gated = (mixed * gate[...]).astype(BF16)
    total[...] = term[...] + lax.dot_general(gated, w_out[...], TN, preferred_element_type=F32)

    slots = near.shape[0] - ROWS
    attended = jnp.concatenate([near[ROWS:, :], far[ROWS:, :]], axis=0).astype(BF16)
    seqs = 3
    heads = w_attn.shape[0] // HEAD_SIZE
    token = lax.broadcasted_iota(jnp.int32, (batch, 2 * slots), 0)
    source = lax.broadcasted_iota(jnp.int32, (batch, 2 * slots), 1)
    owner = token // seqs
    kx = lax.rem(x - owner // 8 + RING, RING)
    ky = lax.rem(y - (owner // 2) % 4 + RING, RING)
    kc = jnp.where(owner % 2 == c, 0, 1)
    at = kc * slots + (ky * RING + kx) * SLOT + (token % seqs) * heads
    attn = jnp.zeros((batch, w_attn.shape[1]), F32)
    for h in range(heads):
        pick = jnp.where(source == at + h, 1.0, 0.0).astype(BF16)
        rows = dot(pick, attended).astype(BF16)
        attn = attn + dot(rows, w_attn[h * HEAD_SIZE : (h + 1) * HEAD_SIZE, :])
    start = pl.multiple_of(seq * HEAD_SIZE, HEAD_SIZE)
    total[:, pl.ds(start, HEAD_SIZE)] = total[:, pl.ds(start, HEAD_SIZE)] + attn

    rows = keep_out.shape[1]
    for i in range(total.shape[1] // HEAD_SIZE):
        block = total[:, i * HEAD_SIZE : (i + 1) * HEAD_SIZE].T.astype(BF16)
        for q in range(0, HEAD_SIZE // rows, 2):
            slot = (i * (HEAD_SIZE // rows) + q) // 2
            even = block[q * rows : (q + 1) * rows, :]
            odd = block[(q + 1) * rows : (q + 2) * rows, :]
            keep_out[slot] = jnp.where(mine, even, odd)
            send_out[slot] = jnp.where(mine, odd, even)


def block(
    hidden_in,
    norm_gain,
    w_ssm_in,
    w_ssm_gate,
    conv_weight,
    conv_bias,
    conv_state,
    w_state_proj,
    w_step,
    step_bias,
    log_decay,
    skip_gain,
    ssm_state,
    w_ssm_out,
    w_query,
    key_projection,
    value_projection,
    w_attn_out,
    w_mlp_gate,
    w_mlp_up,
    w_mlp_down,
    cached_inputs,
    window_lengths,
):
    batch, features = hidden_in.shape
    width = norm_gain.shape[0]
    channels = w_ssm_in.shape[1]
    window = cached_inputs.shape[1]
    states = log_decay.shape[0]
    cosines, sines = (jnp.asarray(t) for t in rotary_tables(window + 8))

    hidden = hidden_in.T
    copies = jnp.broadcast_to(hidden[None], (64, features, batch))
    held = lax.all_to_all(copies, CHIPS, 0, 0, tiled=True)
    other = shifted(held, "seq_2", 1)

    keys, values = window_rows(
        window_lengths, cached_inputs, key_projection, value_projection, cosines, sines
    )

    normed, conv, low = vmem_call(
        inner_kernel,
        (
            ((width, batch), BF16, True),
            ((channels, batch), F32, True),
            ((2, ROWS, 128), F32, True),
        ),
        (
            held, other, norm_gain.reshape(-1, 128), w_ssm_in.T, w_state_proj,
            jnp.transpose(conv_state, (1, 2, 0)), conv_weight, conv_bias[None],
        ),
    )
    half = low[0] + shifted(low[1], "seq_2", 1)
    arrived = from_ring(half, "grp")
    (attended,) = vmem_call(
        attention_kernel,
        (((SLOT, HEAD_SIZE), F32, True),),
        (normed, w_query, key_projection, value_projection, keys, values, cosines, sines),
        lengths=window_lengths,
    )
    gate, act = vmem_call(
        gate_kernel,
        (((channels, batch), F32, True), ((w_mlp_up.shape[1], batch), BF16, True)),
        (normed, w_ssm_gate.T, w_mlp_gate.T, w_mlp_up.T),
    )
    (term,) = vmem_call(down_kernel, (((batch, width), F32, True),), (act, w_mlp_down))
    (packed,) = vmem_call(
        pack_kernel, (((ROWS + SLOT, HEAD_SIZE), F32, True),), (*arrived, attended)
    )
    for axis in ("seq_0", "seq_1"):
        parts = from_ring(packed, axis)
        size = ROWS + RING * (packed.shape[0] - ROWS)
        (packed,) = vmem_call(combine_kernel, (((size, HEAD_SIZE), F32, True),), parts)
    packed_other = shifted(packed, "seq_2", 1)

    piece = ((64, features, batch), BF16, True)
    state_new, keep, send = vmem_call(
        outer_kernel,
        (((states, channels, batch), F32, False), piece, piece),
        (
            packed, packed_other, w_step.T, log_decay, step_bias[None], skip_gain[None], conv, gate,
            jnp.transpose(ssm_state, (1, 2, 0)), w_ssm_out, term, w_attn_out,
        ),
        scratch=(pltpu.VMEM((batch, width), F32),),
    )
    came = shifted(send, "seq_2", 1)
    summed = (keep.astype(F32) + came.astype(F32)).astype(BF16)
    arrived = lax.all_to_all(summed, CHIPS, 0, 0, tiled=True)
    total = jnp.sum(arrived.astype(F32), axis=0)
    hidden_out = (hidden.astype(F32) + total).astype(BF16).T
    return (hidden_out, jnp.transpose(state_new, (2, 0, 1)))


def solution(mesh):
    torus = Mesh(
        mesh.devices.reshape(mesh.shape["grp"], 4, 4, 2), ("grp", "seq_0", "seq_1", "seq_2")
    )
    placed = (
        P(None, GRP_SEQ),
        P(),
        P(None, GRP_SEQ),
        P(None, GRP_SEQ),
        P(None, GRP_SEQ),
        P(GRP_SEQ),
        P(None, None, GRP_SEQ),
        P(GRP_SEQ, None),
        P(None, GRP_SEQ),
        P(GRP_SEQ),
        P(None, GRP_SEQ),
        P(GRP_SEQ),
        P(None, None, GRP_SEQ),
        P(GRP_SEQ, None),
        P(None, "grp"),
        P(None, "grp"),
        P(None, "grp"),
        P("grp", SEQ),
        P(None, GRP_SEQ),
        P(None, GRP_SEQ),
        P(GRP_SEQ, None),
        P(SEQ, None, None),
        P(),
    )
    return jax.shard_map(
        block,
        mesh=torus,
        in_specs=placed,
        out_specs=(P(None, GRP_SEQ), P(None, None, GRP_SEQ)),
        check_vma=False,
    )
```

profile of v0, /device:TPU:0, one launch (start us, length us, event | category | flops | bytes accessed | tf_op | source)
XLA Modules:
  0.0 100.2 jit_solution(13495910066897719540)
XLA Ops:
  0.7 0.9 broadcast_in_dim.15
  1.6 24.6 %all_to_all.10.near = bf16[64,32,96]{2,1,0:T(8,128)(2,1)S(1)} all-to-all(bf16[64,32,96]{2,1,0:T(8,128)(2,1)S(1)} %broadcast_in_dim.15), channel_id=1, replica_groups=mesh['grp'=4,'seq_0'=4,'seq_1'=4,'seq_2'=2] {'grp','seq_0','seq_1'}, dimensions={0} | all-to-all | bytes 786432 | tf_op jit(solution)/shard_map/all_to_all | solution.py:349
  26.2 1.9 %collective-permute-done.far = bf16[64,32,96]{2,1,0:T(8,128)(2,1)S(1)} collective-permute-done((bf16[64,32,96]{2,1,0:T(8,128)(2,1)S(1)}, bf16[64,32,96]{2,1,0:T(8,128)(2,1)S(1)}, u32[]{:S(2)}, u32[]{:S(2)}) %collective-permute-start) | collective-permute-done | bytes 393248 | tf_op jit(solution)/shard_map/ppermute | solution.py:44
  28.1 1.0 %copy-done.8 = bf16[4096,64]{0,1:T(8,128)(2,1)S(1)} copy-done((bf16[4096,64]{0,1:T(8,128)(2,1)S(1)}, bf16[4096,64]{0,1:T(8,128)(2,1)}, u32[]{:S(2)}) %copy-start.8) | copy-done | bytes 524312
  29.1 0.8 copy-done.13
  29.9 0.8 copy-done.14
  32.8 1.3 %shard_map.248 = (bf16[4096,96]{1,0:T(8,128)(2,1)S(1)}, f32[64,96]{1,0:T(8,128)S(1)}, f32[2,144,128]{2,1,0:T(8,128)S(1)}) custom-call(bf16[64,32,96]{2,1,0:T(8,128)(2,1)S(1)} %all_to_all.10.near, bf16[64,32,96]{2,1,0:T(8,128)(2,1)S(1)} %collective-permute-done.far, f32[32,128]{1,0:T(8,128)S(1)} %bitcast.28, bf16[64,4096]{1,0:T(8,128)(2,1)S(1)} %bitcast.23, ...), custom_call_target="tpu_custom_call" | custom-call | tf_op jit(solution)/shard_map/pallas_call | solution.py:75
  34.4 1.1 %collective-permute-done.1 = f32[144,128]{1,0:T(8,128)S(1)} collective-permute-done((f32[144,128]{1,0:T(8,128)S(1)}, f32[144,128]{1,0:T(8,128)S(1)}, u32[]{:S(2)}, u32[]{:S(2)}) %collective-permute-start.1) | collective-permute-done | bytes 73760 | tf_op jit(solution)/shard_map/ppermute | solution.py:44
  35.7 2.1 %collective-permute-start.3 = (f32[144,128]{1,0:T(8,128)S(1)}, f32[144,128]{1,0:T(8,128)S(1)}, u32[]{:S(2)}, u32[]{:S(2)}) collective-permute-start(f32[144,128]{1,0:T(8,128)S(1)} %bitcast_add_fusion.s0), channel_id=1, source_target_pairs={{0,64},{32,96},{64,0},{96,32},{1,65},{33,97},{65,1},{97,33},{2,66}... | collective-permute-start | bytes 221192 | tf_op jit(solution)/shard_map/ppermute | solution.py:44
  37.8 1.1 %collective-permute-start.4 = (f32[144,128]{1,0:T(8,128)S(1)}, f32[144,128]{1,0:T(8,128)S(1)}, u32[]{:S(2)}, u32[]{:S(2)}) collective-permute-start(f32[144,128]{1,0:T(8,128)S(1)} %bitcast_add_fusion.s0), channel_id=1, source_target_pairs={{0,96},{32,0},{64,32},{96,64},{1,97},{33,1},{65,33},{97,65},{2,98}... | collective-permute-start | bytes 221192 | tf_op jit(solution)/shard_map/ppermute | solution.py:44
  38.9 1.6 %copy-done.1 = bf16[4096,256]{1,0:T(8,128)(2,1)S(1)} copy-done((bf16[4096,256]{1,0:T(8,128)(2,1)S(1)}, bf16[4096,256]{1,0:T(8,128)(2,1)}, u32[]{:S(2)}) %copy-start.1) | copy-done | bytes 2097176
  41.1 11.2 %shard_map.249 = (bf16[3,512,256]{2,1,0:T(8,128)(2,1)S(1)}, bf16[3,512,256]{2,1,0:T(8,128)(2,1)S(1)}) custom-call(s32[96]{0:T(128)S(1)} %copy-done.18, bf16[3,512,4096]{2,1,0:T(8,128)(2,1)} %rows.1, bf16[4096,256]{1,0:T(8,128)(2,1)S(1)} %copy-done, bf16[4096,256]{1,0:T(8,128)(2,1)S(1)} %copy-done.1, f32[520,128]{1,0:T(8,128)S(1)} %copy-done.3, ...), custom_call_target="tpu_custom_call" | custom-call | tf_op jit(solution)/shard_map/pallas_call | solution.py:120
  52.4 3.5 %shard_map.250.attended = f32[16,128]{1,0:T(8,128)S(1)} custom-call(s32[96]{0:T(128)S(1)} %copy-done.18, bf16[4096,96]{1,0:T(8,128)(2,1)S(1)} %get-tuple-element.13.normed, bf16[4096,512]{1,0:T(8,128)(2,1)S(1)} %copy-done.2, bf16[4096,256]{1,0:T(8,128)(2,1)S(1)} %copy-done, bf16[4096,256]{1,0:T(8,128)(2,1)S(1)} %copy-done.1, ...), custom_call_target="tpu_custom_call" | custom-call | tf_op jit(solution)/shard_map/pallas_call | solution.py:75
  56.0 1.7 %collective-permute-start.6 = (f32[160,128]{1,0:T(8,128)S(1)}, f32[160,128]{1,0:T(8,128)S(1)}, u32[]{:S(2)}, u32[]{:S(2)}) collective-permute-start(f32[160,128]{1,0:T(8,128)S(1)} %shard_map.251.p0), channel_id=1, source_target_pairs={{0,16},{8,24},{16,0},{24,8},{1,17},{9,25},{17,1},{25,9},{2,18},{10... | collective-permute-start | bytes 245768 | tf_op jit(solution)/shard_map/ppermute | solution.py:44
  57.7 2.5 %collective-permute-start.7 = (f32[160,128]{1,0:T(8,128)S(1)}, f32[160,128]{1,0:T(8,128)S(1)}, u32[]{:S(2)}, u32[]{:S(2)}) collective-permute-start(f32[160,128]{1,0:T(8,128)S(1)} %shard_map.251.p0), channel_id=1, source_target_pairs={{0,24},{8,0},{16,8},{24,16},{1,25},{9,1},{17,9},{25,17},{2,26},{10... | collective-permute-start | bytes 245768 | tf_op jit(solution)/shard_map/ppermute | solution.py:44
  60.2 2.6 %collective-permute-done.5.p1 = f32[160,128]{1,0:T(8,128)S(1)} collective-permute-done((f32[160,128]{1,0:T(8,128)S(1)}, f32[160,128]{1,0:T(8,128)S(1)}, u32[]{:S(2)}, u32[]{:S(2)}) %collective-permute-start.5) | collective-permute-done | bytes 81952 | tf_op jit(solution)/shard_map/ppermute | solution.py:44
  63.5 1.4 %collective-permute-start.10 = (f32[208,128]{1,0:T(8,128)S(1)}, f32[208,128]{1,0:T(8,128)S(1)}, u32[]{:S(2)}, u32[]{:S(2)}) collective-permute-start(f32[208,128]{1,0:T(8,128)S(1)} %shard_map.252.p0), channel_id=1, source_target_pairs={{0,6},{2,0},{4,2},{6,4},{1,7},{3,1},{5,3},{7,5},{8,14},{10,8},{12,... | collective-permute-start | bytes 319496 | tf_op jit(solution)/shard_map/ppermute | solution.py:44
  65.6 1.2 %collective-permute-start.9 = (f32[208,128]{1,0:T(8,128)S(1)}, f32[208,128]{1,0:T(8,128)S(1)}, u32[]{:S(2)}, u32[]{:S(2)}) collective-permute-start(f32[208,128]{1,0:T(8,128)S(1)} %shard_map.252.p0), channel_id=1, source_target_pairs={{0,4},{2,6},{4,0},{6,2},{1,5},{3,7},{5,1},{7,3},{8,12},{10,14},{12... | collective-permute-start | bytes 319496 | tf_op jit(solution)/shard_map/ppermute | solution.py:44
  66.8 1.4 %collective-permute-done.10.p3 = f32[208,128]{1,0:T(8,128)S(1)} collective-permute-done((f32[208,128]{1,0:T(8,128)S(1)}, f32[208,128]{1,0:T(8,128)S(1)}, u32[]{:S(2)}, u32[]{:S(2)}) %collective-permute-start.10) | collective-permute-done | bytes 106528 | tf_op jit(solution)/shard_map/ppermute | solution.py:44
  68.3 4.3 %collective-permute-done.8.p1 = f32[208,128]{1,0:T(8,128)S(1)} collective-permute-done((f32[208,128]{1,0:T(8,128)S(1)}, f32[208,128]{1,0:T(8,128)S(1)}, u32[]{:S(2)}, u32[]{:S(2)}) %collective-permute-start.8) | collective-permute-done | bytes 106528 | tf_op jit(solution)/shard_map/ppermute | solution.py:44
  72.7 0.8 shard_map.254
  74.8 1.7 %shard_map.256 = (f32[16,64,96]{2,1,0:T(8,128)}, bf16[64,32,96]{2,1,0:T(8,128)(2,1)S(1)}, bf16[64,32,96]{2,1,0:T(8,128)(2,1)S(1)}) custom-call(f32[400,128]{1,0:T(8,128)S(1)} %shard_map.253.near, f32[400,128]{1,0:T(8,128)S(1)} %collective-permute-done.11.far, bf16[64,256]{1,0:T(8,128)(2,1)S(1)} %bitcast.27, f32[16,64]{1,0:T(8,128)S(1)} %copy-done.17, ...), custom_call_target="tpu_custom_call" | custom-call | tf_op jit(solution)/shard_map/pallas_call | solution.py:75
  77.0 1.5 %collective-permute-done.12 = bf16[64,32,96]{2,1,0:T(8,128)(2,1)S(1)} collective-permute-done((bf16[64,32,96]{2,1,0:T(8,128)(2,1)S(1)}, bf16[64,32,96]{2,1,0:T(8,128)(2,1)S(1)}, u32[]{:S(2)}, u32[]{:S(2)}) %collective-permute-start.12) | collective-permute-done | bytes 393248 | tf_op jit(solution)/shard_map/ppermute | solution.py:44
  78.7 20.8 %all_to_all.11 = bf16[64,32,96]{2,1,0:T(8,128)(2,1)S(1)} all-to-all(bf16[64,32,96]{2,1,0:T(8,128)(2,1)S(1)} %add_convert_fusion), channel_id=1, replica_groups=mesh['grp'=4,'seq_0'=4,'seq_1'=4,'seq_2'=2] {'grp','seq_0','seq_1'}, dimensions={0} | all-to-all | bytes 786432 | tf_op jit(solution)/shard_map/all_to_all | solution.py:403
  (67 shorter events, 7.3 us)
Async XLA Ops:
  0.6 38.2 %copy-start.3 = (f32[520,128]{1,0:T(8,128)S(1)}, f32[520,128]{1,0:T(8,128)}, u32[]{:S(2)}) copy-start(f32[520,128]{1,0:T(8,128)} %constant.6.clone.cosines) | copy-start | bytes 798724
  0.6 38.2 %copy-start.4 = (f32[520,128]{1,0:T(8,128)S(1)}, f32[520,128]{1,0:T(8,128)}, u32[]{:S(2)}) copy-start(f32[520,128]{1,0:T(8,128)} %constant.7.clone.sines) | copy-start | bytes 798724
  0.7 38.2 %copy-start = (bf16[4096,256]{1,0:T(8,128)(2,1)S(1)}, bf16[4096,256]{1,0:T(8,128)(2,1)}, u32[]{:S(2)}) copy-start(bf16[4096,256]{1,0:T(8,128)(2,1)} %w_key.3) | copy-start | bytes 6291460
  26.2 1.9 %collective-permute-start = (bf16[64,32,96]{2,1,0:T(8,128)(2,1)S(1)}, bf16[64,32,96]{2,1,0:T(8,128)(2,1)S(1)}, u32[]{:S(2)}, u32[]{:S(2)}) collective-permute-start(bf16[64,32,96]{2,1,0:T(8,128)(2,1)S(1)} %all_to_all.10.near), channel_id=1, source_target_pairs={{0,1},{1,0},{2,3},{3,2},{4,5},{5,4},{6,7},{7,6},{8,9},{9,8},{10,11... | collective-permute-start | bytes 1179656 | tf_op jit(solution)/shard_map/ppermute | solution.py:44
  34.2 1.3 %collective-permute-start.1 = (f32[144,128]{1,0:T(8,128)S(1)}, f32[144,128]{1,0:T(8,128)S(1)}, u32[]{:S(2)}, u32[]{:S(2)}) collective-permute-start(f32[144,128]{1,0:T(8,128)S(1)} %slice_bitcast_fusion), channel_id=1, source_target_pairs={{0,1},{1,0},{2,3},{3,2},{4,5},{5,4},{6,7},{7,6},{8,9},{9,8},{10,11... | collective-permute-start | bytes 221192 | tf_op jit(solution)/shard_map/ppermute | solution.py:44
  35.5 20.3 %collective-permute-start.2 = (f32[144,128]{1,0:T(8,128)S(1)}, f32[144,128]{1,0:T(8,128)S(1)}, u32[]{:S(2)}, u32[]{:S(2)}) collective-permute-start(f32[144,128]{1,0:T(8,128)S(1)} %bitcast_add_fusion.s0), channel_id=1, source_target_pairs={{0,32},{32,64},{64,96},{96,0},{1,33},{33,65},{65,97},{97,1},{2,34}... | collective-permute-start | bytes 221192 | tf_op jit(solution)/shard_map/ppermute | solution.py:44
  35.7 20.1 %collective-permute-start.3 = (f32[144,128]{1,0:T(8,128)S(1)}, f32[144,128]{1,0:T(8,128)S(1)}, u32[]{:S(2)}, u32[]{:S(2)}) collective-permute-start(f32[144,128]{1,0:T(8,128)S(1)} %bitcast_add_fusion.s0), channel_id=1, source_target_pairs={{0,64},{32,96},{64,0},{96,32},{1,65},{33,97},{65,1},{97,33},{2,66}... | collective-permute-start | bytes 221192 | tf_op jit(solution)/shard_map/ppermute | solution.py:44
  37.8 18.1 %collective-permute-start.4 = (f32[144,128]{1,0:T(8,128)S(1)}, f32[144,128]{1,0:T(8,128)S(1)}, u32[]{:S(2)}, u32[]{:S(2)}) collective-permute-start(f32[144,128]{1,0:T(8,128)S(1)} %bitcast_add_fusion.s0), channel_id=1, source_target_pairs={{0,96},{32,0},{64,32},{96,64},{1,97},{33,1},{65,33},{97,65},{2,98}... | collective-permute-start | bytes 221192 | tf_op jit(solution)/shard_map/ppermute | solution.py:44
  38.9 1.6 %copy-start.1 = (bf16[4096,256]{1,0:T(8,128)(2,1)S(1)}, bf16[4096,256]{1,0:T(8,128)(2,1)}, u32[]{:S(2)}) copy-start(bf16[4096,256]{1,0:T(8,128)(2,1)} %w_value.3) | copy-start | bytes 6291460
  41.1 11.2 %copy-start.2 = (bf16[4096,512]{1,0:T(8,128)(2,1)S(1)}, bf16[4096,512]{1,0:T(8,128)(2,1)}, u32[]{:S(2)}) copy-start(bf16[4096,512]{1,0:T(8,128)(2,1)} %w_query.1) | copy-start | bytes 12582916
  52.3 20.3 %copy-start.6 = (bf16[4096,112]{0,1:T(8,128)(2,1)S(1)}, bf16[4096,112]{0,1:T(8,128)(2,1)}, u32[]{:S(2)}) copy-start(bf16[4096,112]{0,1:T(8,128)(2,1)} %param.43) | copy-start | bytes 2752516
  52.3 20.3 %copy-start.7 = (bf16[4096,112]{0,1:T(8,128)(2,1)S(1)}, bf16[4096,112]{0,1:T(8,128)(2,1)}, u32[]{:S(2)}) copy-start(bf16[4096,112]{0,1:T(8,128)(2,1)} %param.44) | copy-start | bytes 2752516
  52.4 20.3 %copy-start.9 = (bf16[4096,64]{0,1:T(8,128)(2,1)S(1)}, bf16[4096,64]{0,1:T(8,128)(2,1)}, u32[]{:S(2)}) copy-start(bf16[4096,64]{0,1:T(8,128)(2,1)} %param.28) | copy-start | bytes 1572868
  55.9 7.0 %collective-permute-start.5 = (f32[160,128]{1,0:T(8,128)S(1)}, f32[160,128]{1,0:T(8,128)S(1)}, u32[]{:S(2)}, u32[]{:S(2)}) collective-permute-start(f32[160,128]{1,0:T(8,128)S(1)} %shard_map.251.p0), channel_id=1, source_target_pairs={{0,8},{8,16},{16,24},{24,0},{1,9},{9,17},{17,25},{25,1},{2,10},{10... | collective-permute-start | bytes 245768 | tf_op jit(solution)/shard_map/ppermute | solution.py:44
  56.0 6.9 %collective-permute-start.6 = (f32[160,128]{1,0:T(8,128)S(1)}, f32[160,128]{1,0:T(8,128)S(1)}, u32[]{:S(2)}, u32[]{:S(2)}) collective-permute-start(f32[160,128]{1,0:T(8,128)S(1)} %shard_map.251.p0), channel_id=1, source_target_pairs={{0,16},{8,24},{16,0},{24,8},{1,17},{9,25},{17,1},{25,9},{2,18},{10... | collective-permute-start | bytes 245768 | tf_op jit(solution)/shard_map/ppermute | solution.py:44
  57.7 5.8 %collective-permute-start.7 = (f32[160,128]{1,0:T(8,128)S(1)}, f32[160,128]{1,0:T(8,128)S(1)}, u32[]{:S(2)}, u32[]{:S(2)}) collective-permute-start(f32[160,128]{1,0:T(8,128)S(1)} %shard_map.251.p0), channel_id=1, source_target_pairs={{0,24},{8,0},{16,8},{24,16},{1,25},{9,1},{17,9},{25,17},{2,26},{10... | collective-permute-start | bytes 245768 | tf_op jit(solution)/shard_map/ppermute | solution.py:44
  63.5 10.1 %copy-start.5 = (bf16[112,4096]{1,0:T(8,128)(2,1)S(1)}, bf16[112,4096]{1,0:T(8,128)(2,1)}, u32[]{:S(2)}) copy-start(bf16[112,4096]{1,0:T(8,128)(2,1)} %w_mlp_down.1) | copy-start | bytes 2752516
  63.5 4.8 %collective-permute-start.10 = (f32[208,128]{1,0:T(8,128)S(1)}, f32[208,128]{1,0:T(8,128)S(1)}, u32[]{:S(2)}, u32[]{:S(2)}) collective-permute-start(f32[208,128]{1,0:T(8,128)S(1)} %shard_map.252.p0), channel_id=1, source_target_pairs={{0,6},{2,0},{4,2},{6,4},{1,7},{3,1},{5,3},{7,5},{8,14},{10,8},{12,... | collective-permute-start | bytes 319496 | tf_op jit(solution)/shard_map/ppermute | solution.py:44
  64.9 7.6 %collective-permute-start.8 = (f32[208,128]{1,0:T(8,128)S(1)}, f32[208,128]{1,0:T(8,128)S(1)}, u32[]{:S(2)}, u32[]{:S(2)}) collective-permute-start(f32[208,128]{1,0:T(8,128)S(1)} %shard_map.252.p0), channel_id=1, source_target_pairs={{0,2},{2,4},{4,6},{6,0},{1,3},{3,5},{5,7},{7,1},{8,10},{10,12},{12... | collective-permute-start | bytes 319496 | tf_op jit(solution)/shard_map/ppermute | solution.py:44
  65.6 6.9 %collective-permute-start.9 = (f32[208,128]{1,0:T(8,128)S(1)}, f32[208,128]{1,0:T(8,128)S(1)}, u32[]{:S(2)}, u32[]{:S(2)}) collective-permute-start(f32[208,128]{1,0:T(8,128)S(1)} %shard_map.252.p0), channel_id=1, source_target_pairs={{0,4},{2,6},{4,0},{6,2},{1,5},{3,7},{5,1},{7,3},{8,12},{10,14},{12... | collective-permute-start | bytes 319496 | tf_op jit(solution)/shard_map/ppermute | solution.py:44
  72.6 1.5 %collective-permute-start.11 = (f32[400,128]{1,0:T(8,128)S(1)}, f32[400,128]{1,0:T(8,128)S(1)}, u32[]{:S(2)}, u32[]{:S(2)}) collective-permute-start(f32[400,128]{1,0:T(8,128)S(1)} %shard_map.253.near), channel_id=1, source_target_pairs={{0,1},{1,0},{2,3},{3,2},{4,5},{5,4},{6,7},{7,6},{8,9},{9,8},{10,11... | collective-permute-start | bytes 614408 | tf_op jit(solution)/shard_map/ppermute | solution.py:44
  73.5 1.2 %copy-start.12 = (bf16[512,128]{1,0:T(8,128)(2,1)S(1)}, bf16[512,128]{1,0:T(8,128)(2,1)}, u32[]{:S(2)}) copy-start(bf16[512,128]{1,0:T(8,128)(2,1)} %w_attn.1) | copy-start | bytes 393220
  76.4 23.2 %copy-start.23 = (bf16[96,32]{0,1:T(8,128)(2,1)S(1)}, bf16[96,32]{0,1:T(8,128)(2,1)}, u32[]{:S(2)}) copy-start(bf16[96,32]{0,1:T(8,128)(2,1)} %param.25) | copy-start | bytes 18436
  76.4 2.1 %collective-permute-start.12 = (bf16[64,32,96]{2,1,0:T(8,128)(2,1)S(1)}, bf16[64,32,96]{2,1,0:T(8,128)(2,1)S(1)}, u32[]{:S(2)}, u32[]{:S(2)}) collective-permute-start(bf16[64,32,96]{2,1,0:T(8,128)(2,1)S(1)} %get-tuple-element.20), channel_id=1, source_target_pairs={{0,1},{1,0},{2,3},{3,2},{4,5},{5,4},{6,7},{7,6},{8,9},{9,8},{10,11... | collective-permute-start | bytes 1179656 | tf_op jit(solution)/shard_map/ppermute | solution.py:44
  (13 other events, 12.3 us)
where the time goes:
time: 101 us; the launch traced here: 100 us
  blocking collectives  45.4 us (45%)
  Pallas kernels  19 us (19%)
  waiting for transfers between devices  13.6 us (13%)
  starting transfers between devices  11.9 us (12%)
  local copies, waits for them, and re-layouts  8.59 us (9%)
    all_to_all x1, blocking collectives, block(): held = lax.all_to_all(copies, CHIPS, 0, 0, tiled=True)  24.6 us
    all_to_all x1, blocking collectives, block(): arrived = lax.all_to_all(summed, CHIPS, 0, 0, tiled=True)  20.8 us
    ppermute x13, waiting for transfers between devices, shifted(): lax.ppermute(value, axis, [(i, (i + step) % size) for i in range(size)])  13.6 us
    ppermute x13, starting transfers between devices, shifted(): lax.ppermute(value, axis, [(i, (i + step) % size) for i in range(size)])  11.9 us
    pallas_call x1, Pallas kernels, window_rows(): pl.pallas_call(functools.partial(window_kernel, chunk=chunk), out_shape=(...  11.2 us
    pallas_call x8, Pallas kernels, vmem_call(): pl.pallas_call(kernel, out_shape=tuple((pltpu.VMEM(shape, dtype) if inner...  7.76 us
    unnamed x48, local copies, waits for them, and re-layouts  7.67 us
  transfers between devices with their start and end apart: 13, of which 8 were waited for; matrix products, arithmetic and copies ran while one was open for 0% of the time, Pallas kernels for 16%

commit v1 on v0

--- a/solution.py
+++ b/solution.py
@@ -1,5 +1,3 @@
-import functools
-
 import jax
 import jax.numpy as jnp
 import numpy as np
@@ -23,6 +21,7 @@
 RING = 4
 ROWS = 144
 SLOT = 16
+WEIGHT_PIECES = 4
 
 
 def rotary_tables(count):
@@ -64,80 +63,135 @@
     return (x * RING + y) * 2 + c
 
 
+def in_hbm(value):
+    return pltpu.with_memory_space_constraint(value, pltpu.HBM)
+
+
 def in_vmem(value):
     return pltpu.with_memory_space_constraint(value, pltpu.VMEM)
 
 
-def vmem_call(kernel, outs, operands, lengths=None, scratch=(), limit=12 << 20):
-    smem = pl.BlockSpec(memory_space=pltpu.SMEM)
+def vmem_call(kernel, outs, operands, fetched=(), scratch=(), limit=12 << 20):
     vmem = pl.BlockSpec(memory_space=pltpu.VMEM)
-    scalars = () if lengths is None else (lengths,)
+    anywhere = pl.BlockSpec(memory_space=pl.ANY)
     return pl.pallas_call(
         kernel,
         out_shape=tuple(pltpu.VMEM(shape, dtype) if inner else jax.ShapeDtypeStruct(shape, dtype) for shape, dtype, inner in outs),
-        in_specs=[smem] * len(scalars) + [vmem] * len(operands),
+        in_specs=[anywhere if k in fetched else vmem for k in range(len(operands))],
         out_specs=tuple(vmem for _ in outs),
         scratch_shapes=list(scratch),
         compiler_params=pltpu.CompilerParams(vmem_limit_bytes=limit),
-    )(*scalars, *(in_vmem(v) for v in operands))
-
-
-def window_kernel(lengths, rows, w_key, w_value, cosines, sines, key_out, value_out, *, chunk):
-    step = pl.program_id(0)
-    per_seq = 512 // chunk
-    start = (step % per_seq) * chunk
-    length = lengths[own_seq() * 3 + step // per_seq]
-
-    @pl.when(start < length)
-    def _():
-        block = rows[0]
-        keys = dot(block, w_key[...])
-        begin = pl.multiple_of(start, chunk)
-        cos = cosines[pl.ds(begin, chunk), :]
-        sin = sines[pl.ds(begin, chunk), :]
-        for head in range(keys.shape[1] // HEAD_SIZE):
-            part = keys[:, head * HEAD_SIZE : (head + 1) * HEAD_SIZE]
-            turned = part * cos + pltpu.roll(part, HEAD_SIZE // 2, 1) * sin
-            key_out[0, :, head * HEAD_SIZE : (head + 1) * HEAD_SIZE] = turned.astype(BF16)
-        value_out[0] = dot(block, w_value[...]).astype(BF16)
-
-    @pl.when(start >= length)
-    def _():
-        key_out[...] = jnp.zeros_like(key_out)
-        value_out[...] = jnp.zeros_like(value_out)
-
-
-def window_rows(lengths, cached, w_key, w_value, cosines, sines, chunk=256):
+    )(*((in_hbm if k in fetched else in_vmem)(v) for k, v in enumerate(operands)))
+
+
+def window_kernel(
+    lengths, cached, w_key, w_value, cosines, sines, key_out, value_out,
+    rows, weights, cos, sin, turned, plain, row_sem, first_sem, key_sem, value_sem, table_sem, out_sem,
+):
     seqs, window, width = cached.shape
-    per_seq = window // chunk
     columns = w_key.shape[1]
-    whole = pl.BlockSpec(memory_space=pltpu.VMEM)
-    out = jax.ShapeDtypeStruct((seqs, window, columns), BF16)
-
-    def block_at(i, _):
-        return (i // per_seq, i % per_seq, 0)
-
+    first = own_seq() * seqs
+    pieces = WEIGHT_PIECES
+    step = width // pieces
+
+    def piece_copies(p):
+        span = pl.ds(p * step, step)
+        return (
+            pltpu.make_async_copy(
+                w_key.at[span], weights.at[span, pl.ds(0, columns)], key_sem.at[p]
+            ),
+            pltpu.make_async_copy(
+                w_value.at[span], weights.at[span, pl.ds(columns, columns)], value_sem.at[p]
+            ),
+            pltpu.make_async_copy(cached.at[0, :, span], rows.at[0, :, span], first_sem.at[p]),
+        )
+
+    tables = (
+        pltpu.make_async_copy(cosines.at[pl.ds(0, window)], cos, table_sem.at[0]),
+        pltpu.make_async_copy(sines.at[pl.ds(0, window)], sin, table_sem.at[1]),
+    )
+    later = [
+        pltpu.make_async_copy(cached.at[b], rows.at[b], row_sem.at[b]) for b in range(1, seqs)
+    ]
+    for p in range(pieces):
+        for copy in piece_copies(p):
+            copy.start()
+    for copy in tables:
+        copy.start()
+    for copy in later:
+        copy.start()
+
+    def finish(b, both):
+        for head in range(columns // HEAD_SIZE):
+            lanes = slice(head * HEAD_SIZE, (head + 1) * HEAD_SIZE)
+            part = both[:, lanes]
+            turned[b, :, lanes] = (
+                part * cos[...] + pltpu.roll(part, HEAD_SIZE // 2, 1) * sin[...]
+            ).astype(BF16)
+        plain[b] = both[:, columns:].astype(BF16)
+
+    def out_copies(b):
+        return (
+            pltpu.make_async_copy(turned.at[b], key_out.at[b], out_sem.at[0, b]),
+            pltpu.make_async_copy(plain.at[b], value_out.at[b], out_sem.at[1, b]),
+        )
+
+    total = None
+    for p in range(pieces):
+        for copy in piece_copies(p):
+            copy.wait()
+        span = slice(p * step, (p + 1) * step)
+        part = dot(rows[0, :, span], weights[span, :])
+        total = part if total is None else total + part
+    for copy in tables:
+        copy.wait()
+    finish(0, total)
+    for copy in out_copies(0):
+        copy.start()
+    for b in range(1, seqs):
+        later[b - 1].wait()
+        finish(b, dot(rows[b], weights[...]))
+        for copy in out_copies(b):
+            copy.start()
+    for b in range(seqs):
+        for copy in out_copies(b):
+            copy.wait()
+
+
+def window_rows(lengths, cached, w_key, w_value, cosines, sines):
+    seqs, window, width = cached.shape
+    columns = w_key.shape[1]
+    anywhere = pl.BlockSpec(memory_space=pl.ANY)
+    out = pltpu.HBM((seqs, window, columns), BF16)
+    dma = pltpu.SemaphoreType.DMA
     return pl.pallas_call(
-        functools.partial(window_kernel, chunk=chunk),
+        window_kernel,
         out_shape=(out, out),
-        grid_spec=pltpu.PrefetchScalarGridSpec(
-            num_scalar_prefetch=1,
-            grid=(seqs * per_seq,),
-            in_specs=[pl.BlockSpec((1, chunk, width), block_at), whole, whole, whole, whole],
-            out_specs=[
-                pl.BlockSpec((1, chunk, columns), block_at),
-                pl.BlockSpec((1, chunk, columns), block_at),
-            ],
-        ),
-        compiler_params=pltpu.CompilerParams(vmem_limit_bytes=24 << 20),
-    )(
-        lengths,
-        pltpu.with_memory_space_constraint(cached, pltpu.HBM),
-        *(in_vmem(v) for v in (w_key, w_value, cosines, sines)),
-    )
-
-
-def inner_kernel(near, far, gain, w_in, w_proj, past, taps, bias, normed_out, conv_out, low_out):
+        in_specs=[pl.BlockSpec(memory_space=pltpu.SMEM)] + [anywhere] * 5,
+        out_specs=(anywhere, anywhere),
+        scratch_shapes=[
+            pltpu.VMEM((seqs, window, width), BF16),
+            pltpu.VMEM((width, 2 * columns), BF16),
+            pltpu.VMEM((window, HEAD_SIZE), F32),
+            pltpu.VMEM((window, HEAD_SIZE), F32),
+            pltpu.VMEM((seqs, window, columns), BF16),
+            pltpu.VMEM((seqs, window, columns), BF16),
+            dma((seqs,)),
+            dma((WEIGHT_PIECES,)),
+            dma((WEIGHT_PIECES,)),
+            dma((WEIGHT_PIECES,)),
+            dma((2,)),
+            dma((2, seqs)),
+        ],
+        compiler_params=pltpu.CompilerParams(vmem_limit_bytes=40 << 20),
+    )(lengths, *(in_hbm(v) for v in (cached, w_key, w_value, cosines, sines)))
+
+
+def inner_kernel(
+    near, far, gain, w_in_hbm, w_proj, past, taps, bias, normed_out, conv_out, low_out, w_in, w_sem,
+):
+    fetch = pltpu.make_async_copy(w_in_hbm, w_in, w_sem)
+    fetch.start()
     c = lax.axis_index("seq_2").astype(jnp.int32)
     rows, batch = near.shape[1], near.shape[2]
     total = jnp.zeros((rows, batch), F32)
@@ -160,6 +214,7 @@
             at = (j % per_gain) * rows
             column = gains[at : at + rows, j // per_gain : j // per_gain + 1]
             normed_out[j * rows : (j + 1) * rows, :] = (pair[k] * scale * column).astype(BF16)
+    fetch.wait()
     fresh = dot(w_in[...], normed_out[...]).astype(BF16).astype(F32)
     params = jnp.concatenate([taps[...], bias[...], jnp.zeros((3, taps.shape[1]), F32)], axis=0).T
     mixed = params[:, 4:5] + params[:, 3:4] * fresh
@@ -184,20 +239,69 @@
 
 
 def attention_kernel(
-    lengths, normed, w_query, w_key, w_value, keys, values, cosines, sines, out
+    lengths, normed, w_query, w_key, w_value, key_rows, value_rows, cosines, sines, out,
+    weights, keys, values, cos_rows, sin_rows, weight_sem, row_sem, table_sem,
 ):
     seqs, window = keys.shape[0], keys.shape[1]
-    kv_heads = keys.shape[2] // HEAD_SIZE
-    group = w_query.shape[1] // keys.shape[2]
-    batch = normed.shape[1]
+    columns = keys.shape[2]
+    queries = w_query.shape[1]
+    kv_heads = columns // HEAD_SIZE
+    group = queries // columns
+    width, batch = normed.shape
     first = own_seq() * seqs
+    pieces = WEIGHT_PIECES
+    step = width // pieces
+
+    def piece_copies(p):
+        span = pl.ds(p * step, step)
+        return (
+            pltpu.make_async_copy(
+                w_query.at[span], weights.at[span, pl.ds(0, queries)], weight_sem.at[0, p]
+            ),
+            pltpu.make_async_copy(
+                w_key.at[span], weights.at[span, pl.ds(queries, columns)], weight_sem.at[1, p]
+            ),
+            pltpu.make_async_copy(
+                w_value.at[span],
+                weights.at[span, pl.ds(queries + columns, columns)],
+                weight_sem.at[2, p],
+            ),
+        )
+
+    row_copies = (
+        pltpu.make_async_copy(key_rows, keys, row_sem.at[0]),
+        pltpu.make_async_copy(value_rows, values, row_sem.at[1]),
+    )
+    table_copies = []
+    for b in range(seqs):
+        at = pl.ds(lengths[first + b], 1)
+        table_copies.append(
+            pltpu.make_async_copy(cosines.at[at], cos_rows.at[pl.ds(b, 1)], table_sem.at[0, b])
+        )
+        table_copies.append(
+            pltpu.make_async_copy(sines.at[at], sin_rows.at[pl.ds(b, 1)], table_sem.at[1, b])
+        )
+    for p in range(pieces):
+        for copy in piece_copies(p):
+            copy.start()
+    for copy in (*table_copies, *row_copies):
+        copy.start()
     row = lax.broadcasted_iota(jnp.int32, (8, batch), 0)
     column = lax.broadcasted_iota(jnp.int32, (8, batch), 1)
     pick = jnp.where((column == first + row) & (row < seqs), 1.0, 0.0).astype(BF16)
     own = lax.dot_general(pick, normed[...], NT, preferred_element_type=F32).astype(BF16)
-    query = dot(own, w_query[...])
-    fresh_key = dot(own, w_key[...])
-    fresh_value = dot(own, w_value[...]).astype(BF16).astype(F32)
+    projected = None
+    for p in range(pieces):
+        for copy in piece_copies(p):
+            copy.wait()
+        span = slice(p * step, (p + 1) * step)
+        part = dot(own[:, span], weights[span, :])
+        projected = part if projected is None else projected + part
+    query = projected[:, 0:queries]
+    fresh_key = projected[:, queries : queries + columns]
+    fresh_value = projected[:, queries + columns :].astype(BF16).astype(F32)
+    for copy in (*table_copies, *row_copies):
+        copy.wait()
     scale = HEAD_SIZE ** (-0.5)
     slot_ids = lax.broadcasted_iota(jnp.int32, (1, window), 1)
     out[...] = jnp.zeros((SLOT, HEAD_SIZE), F32)
@@ -207,8 +311,8 @@
 
     for b in range(seqs):
         length = lengths[first + b]
-        cos = cosines[pl.ds(length, 1), :]
-        sin = sines[pl.ds(length, 1), :]
+        cos = cos_rows[b : b + 1, :]
+        sin = sin_rows[b : b + 1, :]
         valid = slot_ids < length
         for g in range(kv_heads):
             lanes = slice(g * HEAD_SIZE, (g + 1) * HEAD_SIZE)
@@ -235,6 +339,34 @@
             result = (summed / denominator).astype(BF16).astype(F32)
             at = (b * kv_heads + g) * group
             out[at : at + group, :] = result[0:group, :]
+
+
+def attended_rows(lengths, normed, w_query, w_key, w_value, keys, values, cosines, sines):
+    anywhere = pl.BlockSpec(memory_space=pl.ANY)
+    vmem = pl.BlockSpec(memory_space=pltpu.VMEM)
+    dma = pltpu.SemaphoreType.DMA
+    width = normed.shape[0]
+    return pl.pallas_call(
+        attention_kernel,
+        out_shape=pltpu.VMEM((SLOT, HEAD_SIZE), F32),
+        in_specs=[pl.BlockSpec(memory_space=pltpu.SMEM), vmem] + [anywhere] * 7,
+        out_specs=vmem,
+        scratch_shapes=[
+            pltpu.VMEM((width, w_query.shape[1] + 2 * w_key.shape[1]), BF16),
+            pltpu.VMEM(keys.shape, BF16),
+            pltpu.VMEM(values.shape, BF16),
+            pltpu.VMEM((8, HEAD_SIZE), F32),
+            pltpu.VMEM((8, HEAD_SIZE), F32),
+            dma((3, WEIGHT_PIECES)),
+            dma((2,)),
+            dma((2, keys.shape[0])),
+        ],
+        compiler_params=pltpu.CompilerParams(vmem_limit_bytes=20 << 20),
+    )(
+        lengths,
+        in_vmem(normed),
+        *(in_hbm(v) for v in (w_query, w_key, w_value, keys, values, cosines, sines)),
+    )
 
 
 def pack_kernel(s0, s1, s2, s3, attended, out):
@@ -364,14 +496,14 @@
             held, other, norm_gain.reshape(-1, 128), w_ssm_in.T, w_state_proj,
             jnp.transpose(conv_state, (1, 2, 0)), conv_weight, conv_bias[None],
         ),
+        fetched=(3,),
+        scratch=(pltpu.VMEM((channels, width), BF16), pltpu.SemaphoreType.DMA),
     )
     half = low[0] + shifted(low[1], "seq_2", 1)
     arrived = from_ring(half, "grp")
-    (attended,) = vmem_call(
-        attention_kernel,
-        (((SLOT, HEAD_SIZE), F32, True),),
-        (normed, w_query, key_projection, value_projection, keys, values, cosines, sines),
-        lengths=window_lengths,
+    attended = attended_rows(
+        window_lengths, normed, w_query, key_projection, value_projection, keys, values,
+        cosines, sines,
     )
     gate, act = vmem_call(
         gate_kernel,

time: 101 us -> 102 us (level)
  Pallas kernels: 19 us -> 23 us
  local copies, waits for them, and re-layouts: 8.59 us -> 5.15 us
    pallas_call x1 -> x2, Pallas kernels: 11.2 us -> 18.5 us  [the longest x1 11.9 us: window_rows(): pl.pallas_call(window_kernel, out_shape=(out, out), in_specs=[pl.BlockSpe...]
    unnamed x48 -> x36, local copies, waits for them, and re-layouts: 7.67 us -> 4.37 us
    pallas_call x8 -> x7, Pallas kernels: 7.76 us -> 4.52 us  [vmem_call(): pl.pallas_call(kernel, out_shape=tuple((pltpu.VMEM(shape, dtype) if inner...]
  transfers between devices with their start and end apart: 13 -> 13, of which waited for: 8 -> 8; matrix products, arithmetic and copies ran while one was open for 0% -> 0% of each run, Pallas kernels for 16% -> 19%
where the time goes in v1:
time: 102 us; the launch traced here: 101 us
  blocking collectives  46.3 us (45%)
  Pallas kernels  23 us (23%)
  waiting for transfers between devices  13.1 us (13%)
  starting transfers between devices  11.9 us (12%)
  local copies, waits for them, and re-layouts  5.15 us (5%)
    all_to_all x1, blocking collectives, block(): held = lax.all_to_all(copies, CHIPS, 0, 0, tiled=True)  24.6 us
    all_to_all x1, blocking collectives, block(): arrived = lax.all_to_all(summed, CHIPS, 0, 0, tiled=True)  21.7 us
    ppermute x13, waiting for transfers between devices, shifted(): lax.ppermute(value, axis, [(i, (i + step) % size) for i in range(size)])  13.1 us
    pallas_call x1, Pallas kernels, window_rows(): pl.pallas_call(window_kernel, out_shape=(out, out), in_specs=[pl.BlockSpe...  11.9 us
    ppermute x13, starting transfers between devices, shifted(): lax.ppermute(value, axis, [(i, (i + step) % size) for i in range(size)])  11.9 us
    pallas_call x1, Pallas kernels, attended_rows(): pl.pallas_call(attention_kernel, out_shape=pltpu.VMEM((SLOT, HEAD_SIZE),...  6.57 us
    pallas_call x7, Pallas kernels, vmem_call(): pl.pallas_call(kernel, out_shape=tuple((pltpu.VMEM(shape, dtype) if inner...  4.52 us
    unnamed x36, local copies, waits for them, and re-layouts  4.37 us
  transfers between devices with their start and end apart: 13, of which 8 were waited for; matrix products, arithmetic and copies ran while one was open for 0% of the time, Pallas kernels for 19%

profile of v1, /device:TPU:0, one launch (start us, length us, event | category | flops | bytes accessed | tf_op | source)
XLA Modules:
  0.0 101.3 jit_solution(2901117080413076290)
XLA Ops:
  0.6 0.8 broadcast_in_dim.15
  1.4 24.6 %all_to_all.10.near = bf16[64,32,96]{2,1,0:T(8,128)(2,1)S(1)} all-to-all(bf16[64,32,96]{2,1,0:T(8,128)(2,1)S(1)} %broadcast_in_dim.15), channel_id=1, replica_groups=mesh['grp'=4,'seq_0'=4,'seq_1'=4,'seq_2'=2] {'grp','seq_0','seq_1'}, dimensions={0} | all-to-all | bytes 786432 | tf_op jit(solution)/shard_map/all_to_all | solution.py:481
  26.0 1.9 %collective-permute-done.far = bf16[64,32,96]{2,1,0:T(8,128)(2,1)S(1)} collective-permute-done((bf16[64,32,96]{2,1,0:T(8,128)(2,1)S(1)}, bf16[64,32,96]{2,1,0:T(8,128)(2,1)S(1)}, u32[]{:S(2)}, u32[]{:S(2)}) %collective-permute-start) | collective-permute-done | bytes 393248 | tf_op jit(solution)/shard_map/ppermute | solution.py:43
  27.9 0.8 copy-done.7
  28.7 0.8 copy-done.8
  29.5 0.7 copy-done.10
  30.2 0.7 copy-done.13
  31.6 1.5 %shard_map.248 = (bf16[4096,96]{1,0:T(8,128)(2,1)S(1)}, f32[64,96]{1,0:T(8,128)S(1)}, f32[2,144,128]{2,1,0:T(8,128)S(1)}) custom-call(bf16[64,32,96]{2,1,0:T(8,128)(2,1)S(1)} %all_to_all.10.near, bf16[64,32,96]{2,1,0:T(8,128)(2,1)S(1)} %collective-permute-done.far, f32[32,128]{1,0:T(8,128)S(1)} %bitcast.27, bf16[64,4096]{1,0:T(8,128)(2,1)} %bitcast.31, ...), custom_call_target="tpu_custom_call" | custom-call | tf_op jit(solution)/shard_map/pallas_call | solution.py:77
  33.4 1.1 %collective-permute-done.1 = f32[144,128]{1,0:T(8,128)S(1)} collective-permute-done((f32[144,128]{1,0:T(8,128)S(1)}, f32[144,128]{1,0:T(8,128)S(1)}, u32[]{:S(2)}, u32[]{:S(2)}) %collective-permute-start.1) | collective-permute-done | bytes 73760 | tf_op jit(solution)/shard_map/ppermute | solution.py:43
  34.7 2.1 %collective-permute-start.3 = (f32[144,128]{1,0:T(8,128)S(1)}, f32[144,128]{1,0:T(8,128)S(1)}, u32[]{:S(2)}, u32[]{:S(2)}) collective-permute-start(f32[144,128]{1,0:T(8,128)S(1)} %bitcast_add_fusion.s0), channel_id=1, source_target_pairs={{0,64},{32,96},{64,0},{96,32},{1,65},{33,97},{65,1},{97,33},{2,66}... | collective-permute-start | bytes 221192 | tf_op jit(solution)/shard_map/ppermute | solution.py:43
  36.8 1.1 %collective-permute-start.4 = (f32[144,128]{1,0:T(8,128)S(1)}, f32[144,128]{1,0:T(8,128)S(1)}, u32[]{:S(2)}, u32[]{:S(2)}) collective-permute-start(f32[144,128]{1,0:T(8,128)S(1)} %bitcast_add_fusion.s0), channel_id=1, source_target_pairs={{0,96},{32,0},{64,32},{96,64},{1,97},{33,1},{65,33},{97,65},{2,98}... | collective-permute-start | bytes 221192 | tf_op jit(solution)/shard_map/ppermute | solution.py:43
  37.9 11.9 %shard_map.249 = (bf16[3,512,256]{2,1,0:T(8,128)(2,1)}, bf16[3,512,256]{2,1,0:T(8,128)(2,1)}) custom-call(s32[96]{0:T(128)S(1)} %copy-done.12, bf16[3,512,4096]{2,1,0:T(8,128)(2,1)} %cached.1, bf16[4096,256]{1,0:T(8,128)(2,1)} %w_key.3, bf16[4096,256]{1,0:T(8,128)(2,1)} %w_value.3, f32[520,128]{1,0:T(8,128)} %constant.6.clone.cosines, ...), custom_call_target="tpu_custom_call" | custom-call | tf_op jit(solution)/shard_map/pallas_call | solution.py:167
  49.8 6.6 %shard_map.250.attended = f32[16,128]{1,0:T(8,128)S(1)} custom-call(s32[96]{0:T(128)S(1)} %copy-done.12, bf16[4096,96]{1,0:T(8,128)(2,1)S(1)} %get-tuple-element.13.normed, bf16[4096,512]{1,0:T(8,128)(2,1)} %w_query.1, bf16[4096,256]{1,0:T(8,128)(2,1)} %w_key.3, bf16[4096,256]{1,0:T(8,128)(2,1)} %w_value.3, bf16[3,512,256]{2,1,0:T(8,128)(2,1)} %get-tuple-element.14.key_rows, ...), custom_call_target="tpu_custom_call" | custom-call | tf_op jit(solution)/shard_map/pallas_call | solution.py:349
  57.1 2.4 %collective-permute-start.6 = (f32[160,128]{1,0:T(8,128)S(1)}, f32[160,128]{1,0:T(8,128)S(1)}, u32[]{:S(2)}, u32[]{:S(2)}) collective-permute-start(f32[160,128]{1,0:T(8,128)S(1)} %shard_map.251.p0), channel_id=1, source_target_pairs={{0,16},{8,24},{16,0},{24,8},{1,17},{9,25},{17,1},{25,9},{2,18},{10... | collective-permute-start | bytes 245768 | tf_op jit(solution)/shard_map/ppermute | solution.py:43
  59.5 1.3 %collective-permute-start.7 = (f32[160,128]{1,0:T(8,128)S(1)}, f32[160,128]{1,0:T(8,128)S(1)}, u32[]{:S(2)}, u32[]{:S(2)}) collective-permute-start(f32[160,128]{1,0:T(8,128)S(1)} %shard_map.251.p0), channel_id=1, source_target_pairs={{0,24},{8,0},{16,8},{24,16},{1,25},{9,1},{17,9},{25,17},{2,26},{10... | collective-permute-start | bytes 245768 | tf_op jit(solution)/shard_map/ppermute | solution.py:43
  60.9 2.6 %collective-permute-done.5.p1 = f32[160,128]{1,0:T(8,128)S(1)} collective-permute-done((f32[160,128]{1,0:T(8,128)S(1)}, f32[160,128]{1,0:T(8,128)S(1)}, u32[]{:S(2)}, u32[]{:S(2)}) %collective-permute-start.5) | collective-permute-done | bytes 81952 | tf_op jit(solution)/shard_map/ppermute | solution.py:43
  64.0 1.6 %collective-permute-start.10 = (f32[208,128]{1,0:T(8,128)S(1)}, f32[208,128]{1,0:T(8,128)S(1)}, u32[]{:S(2)}, u32[]{:S(2)}) collective-permute-start(f32[208,128]{1,0:T(8,128)S(1)} %shard_map.252.p0), channel_id=1, source_target_pairs={{0,6},{2,0},{4,2},{6,4},{1,7},{3,1},{5,3},{7,5},{8,14},{10,8},{12,... | collective-permute-start | bytes 319496 | tf_op jit(solution)/shard_map/ppermute | solution.py:43
  66.1 1.3 %collective-permute-start.9 = (f32[208,128]{1,0:T(8,128)S(1)}, f32[208,128]{1,0:T(8,128)S(1)}, u32[]{:S(2)}, u32[]{:S(2)}) collective-permute-start(f32[208,128]{1,0:T(8,128)S(1)} %shard_map.252.p0), channel_id=1, source_target_pairs={{0,4},{2,6},{4,0},{6,2},{1,5},{3,7},{5,1},{7,3},{8,12},{10,14},{12... | collective-permute-start | bytes 319496 | tf_op jit(solution)/shard_map/ppermute | solution.py:43
  67.4 2.3 %collective-permute-done.10.p3 = f32[208,128]{1,0:T(8,128)S(1)} collective-permute-done((f32[208,128]{1,0:T(8,128)S(1)}, f32[208,128]{1,0:T(8,128)S(1)}, u32[]{:S(2)}, u32[]{:S(2)}) %collective-permute-start.10) | collective-permute-done | bytes 106528 | tf_op jit(solution)/shard_map/ppermute | solution.py:43
  69.7 3.1 %collective-permute-done.8.p1 = f32[208,128]{1,0:T(8,128)S(1)} collective-permute-done((f32[208,128]{1,0:T(8,128)S(1)}, f32[208,128]{1,0:T(8,128)S(1)}, u32[]{:S(2)}, u32[]{:S(2)}) %collective-permute-start.8) | collective-permute-done | bytes 106528 | tf_op jit(solution)/shard_map/ppermute | solution.py:43
  72.9 0.8 shard_map.254
  75.0 1.7 %shard_map.256 = (f32[16,64,96]{2,1,0:T(8,128)}, bf16[64,32,96]{2,1,0:T(8,128)(2,1)S(1)}, bf16[64,32,96]{2,1,0:T(8,128)(2,1)S(1)}) custom-call(f32[400,128]{1,0:T(8,128)S(1)} %shard_map.253.near, f32[400,128]{1,0:T(8,128)S(1)} %collective-permute-done.11.far, bf16[64,256]{1,0:T(8,128)(2,1)S(1)} %bitcast.26, f32[16,64]{1,0:T(8,128)S(1)} %copy-done.11, ...), custom_call_target="tpu_custom_call" | custom-call | tf_op jit(solution)/shard_map/pallas_call | solution.py:77
  77.2 1.5 %collective-permute-done.12 = bf16[64,32,96]{2,1,0:T(8,128)(2,1)S(1)} collective-permute-done((bf16[64,32,96]{2,1,0:T(8,128)(2,1)S(1)}, bf16[64,32,96]{2,1,0:T(8,128)(2,1)S(1)}, u32[]{:S(2)}, u32[]{:S(2)}) %collective-permute-start.12) | collective-permute-done | bytes 393248 | tf_op jit(solution)/shard_map/ppermute | solution.py:43
  78.9 21.7 %all_to_all.11 = bf16[64,32,96]{2,1,0:T(8,128)(2,1)S(1)} all-to-all(bf16[64,32,96]{2,1,0:T(8,128)(2,1)S(1)} %add_convert_fusion), channel_id=1, replica_groups=mesh['grp'=4,'seq_0'=4,'seq_1'=4,'seq_2'=2] {'grp','seq_0','seq_1'}, dimensions={0} | all-to-all | bytes 786432 | tf_op jit(solution)/shard_map/all_to_all | solution.py:535
  (55 shorter events, 5.6 us)
Async XLA Ops:
  0.6 37.2 %copy-start.12 = (s32[96]{0:T(128)S(1)}, s32[96]{0:T(128)}, u32[]{:S(2)}) copy-start(s32[96]{0:T(128)} %lengths.3) | copy-start | bytes 1156
  26.0 1.9 %collective-permute-start = (bf16[64,32,96]{2,1,0:T(8,128)(2,1)S(1)}, bf16[64,32,96]{2,1,0:T(8,128)(2,1)S(1)}, u32[]{:S(2)}, u32[]{:S(2)}) collective-permute-start(bf16[64,32,96]{2,1,0:T(8,128)(2,1)S(1)} %all_to_all.10.near), channel_id=1, source_target_pairs={{0,1},{1,0},{2,3},{3,2},{4,5},{5,4},{6,7},{7,6},{8,9},{9,8},{10,11... | collective-permute-start | bytes 1179656 | tf_op jit(solution)/shard_map/ppermute | solution.py:43
  33.1 1.3 %collective-permute-start.1 = (f32[144,128]{1,0:T(8,128)S(1)}, f32[144,128]{1,0:T(8,128)S(1)}, u32[]{:S(2)}, u32[]{:S(2)}) collective-permute-start(f32[144,128]{1,0:T(8,128)S(1)} %slice_bitcast_fusion), channel_id=1, source_target_pairs={{0,1},{1,0},{2,3},{3,2},{4,5},{5,4},{6,7},{7,6},{8,9},{9,8},{10,11... | collective-permute-start | bytes 221192 | tf_op jit(solution)/shard_map/ppermute | solution.py:43
  34.5 21.9 %collective-permute-start.2 = (f32[144,128]{1,0:T(8,128)S(1)}, f32[144,128]{1,0:T(8,128)S(1)}, u32[]{:S(2)}, u32[]{:S(2)}) collective-permute-start(f32[144,128]{1,0:T(8,128)S(1)} %bitcast_add_fusion.s0), channel_id=1, source_target_pairs={{0,32},{32,64},{64,96},{96,0},{1,33},{33,65},{65,97},{97,1},{2,34}... | collective-permute-start | bytes 221192 | tf_op jit(solution)/shard_map/ppermute | solution.py:43
  34.7 21.7 %collective-permute-start.3 = (f32[144,128]{1,0:T(8,128)S(1)}, f32[144,128]{1,0:T(8,128)S(1)}, u32[]{:S(2)}, u32[]{:S(2)}) collective-permute-start(f32[144,128]{1,0:T(8,128)S(1)} %bitcast_add_fusion.s0), channel_id=1, source_target_pairs={{0,64},{32,96},{64,0},{96,32},{1,65},{33,97},{65,1},{97,33},{2,66}... | collective-permute-start | bytes 221192 | tf_op jit(solution)/shard_map/ppermute | solution.py:43
  36.8 19.7 %collective-permute-start.4 = (f32[144,128]{1,0:T(8,128)S(1)}, f32[144,128]{1,0:T(8,128)S(1)}, u32[]{:S(2)}, u32[]{:S(2)}) collective-permute-start(f32[144,128]{1,0:T(8,128)S(1)} %bitcast_add_fusion.s0), channel_id=1, source_target_pairs={{0,96},{32,0},{64,32},{96,64},{1,97},{33,1},{65,33},{97,65},{2,98}... | collective-permute-start | bytes 221192 | tf_op jit(solution)/shard_map/ppermute | solution.py:43
  49.8 23.1 %copy-start.1 = (bf16[4096,112]{0,1:T(8,128)(2,1)S(1)}, bf16[4096,112]{0,1:T(8,128)(2,1)}, u32[]{:S(2)}) copy-start(bf16[4096,112]{0,1:T(8,128)(2,1)} %param.43) | copy-start | bytes 2752516
  49.8 23.1 %copy-start.2 = (bf16[4096,112]{0,1:T(8,128)(2,1)S(1)}, bf16[4096,112]{0,1:T(8,128)(2,1)}, u32[]{:S(2)}) copy-start(bf16[4096,112]{0,1:T(8,128)(2,1)} %param.44) | copy-start | bytes 2752516
  49.8 23.0 %copy-start.3 = (bf16[4096,64]{0,1:T(8,128)(2,1)S(1)}, bf16[4096,64]{0,1:T(8,128)(2,1)}, u32[]{:S(2)}) copy-start(bf16[4096,64]{0,1:T(8,128)(2,1)} %param.28) | copy-start | bytes 1572868
  56.5 6.9 %collective-permute-start.5 = (f32[160,128]{1,0:T(8,128)S(1)}, f32[160,128]{1,0:T(8,128)S(1)}, u32[]{:S(2)}, u32[]{:S(2)}) collective-permute-start(f32[160,128]{1,0:T(8,128)S(1)} %shard_map.251.p0), channel_id=1, source_target_pairs={{0,8},{8,16},{16,24},{24,0},{1,9},{9,17},{17,25},{25,1},{2,10},{10... | collective-permute-start | bytes 245768 | tf_op jit(solution)/shard_map/ppermute | solution.py:43
  57.1 6.3 %collective-permute-start.6 = (f32[160,128]{1,0:T(8,128)S(1)}, f32[160,128]{1,0:T(8,128)S(1)}, u32[]{:S(2)}, u32[]{:S(2)}) collective-permute-start(f32[160,128]{1,0:T(8,128)S(1)} %shard_map.251.p0), channel_id=1, source_target_pairs={{0,16},{8,24},{16,0},{24,8},{1,17},{9,25},{17,1},{25,9},{2,18},{10... | collective-permute-start | bytes 245768 | tf_op jit(solution)/shard_map/ppermute | solution.py:43
  59.5 4.5 %collective-permute-start.7 = (f32[160,128]{1,0:T(8,128)S(1)}, f32[160,128]{1,0:T(8,128)S(1)}, u32[]{:S(2)}, u32[]{:S(2)}) collective-permute-start(f32[160,128]{1,0:T(8,128)S(1)} %shard_map.251.p0), channel_id=1, source_target_pairs={{0,24},{8,0},{16,8},{24,16},{1,25},{9,1},{17,9},{25,17},{2,26},{10... | collective-permute-start | bytes 245768 | tf_op jit(solution)/shard_map/ppermute | solution.py:43
  64.0 9.8 %copy-start = (bf16[112,4096]{1,0:T(8,128)(2,1)S(1)}, bf16[112,4096]{1,0:T(8,128)(2,1)}, u32[]{:S(2)}) copy-start(bf16[112,4096]{1,0:T(8,128)(2,1)} %w_mlp_down.1) | copy-start | bytes 2752516
  64.0 5.6 %collective-permute-start.10 = (f32[208,128]{1,0:T(8,128)S(1)}, f32[208,128]{1,0:T(8,128)S(1)}, u32[]{:S(2)}, u32[]{:S(2)}) collective-permute-start(f32[208,128]{1,0:T(8,128)S(1)} %shard_map.252.p0), channel_id=1, source_target_pairs={{0,6},{2,0},{4,2},{6,4},{1,7},{3,1},{5,3},{7,5},{8,14},{10,8},{12,... | collective-permute-start | bytes 319496 | tf_op jit(solution)/shard_map/ppermute | solution.py:43
  65.7 7.1 %collective-permute-start.8 = (f32[208,128]{1,0:T(8,128)S(1)}, f32[208,128]{1,0:T(8,128)S(1)}, u32[]{:S(2)}, u32[]{:S(2)}) collective-permute-start(f32[208,128]{1,0:T(8,128)S(1)} %shard_map.252.p0), channel_id=1, source_target_pairs={{0,2},{2,4},{4,6},{6,0},{1,3},{3,5},{5,7},{7,1},{8,10},{10,12},{12... | collective-permute-start | bytes 319496 | tf_op jit(solution)/shard_map/ppermute | solution.py:43
  66.1 6.6 %collective-permute-start.9 = (f32[208,128]{1,0:T(8,128)S(1)}, f32[208,128]{1,0:T(8,128)S(1)}, u32[]{:S(2)}, u32[]{:S(2)}) collective-permute-start(f32[208,128]{1,0:T(8,128)S(1)} %shard_map.252.p0), channel_id=1, source_target_pairs={{0,4},{2,6},{4,0},{6,2},{1,5},{3,7},{5,1},{7,3},{8,12},{10,14},{12... | collective-permute-start | bytes 319496 | tf_op jit(solution)/shard_map/ppermute | solution.py:43
  72.8 1.5 %collective-permute-start.11 = (f32[400,128]{1,0:T(8,128)S(1)}, f32[400,128]{1,0:T(8,128)S(1)}, u32[]{:S(2)}, u32[]{:S(2)}) collective-permute-start(f32[400,128]{1,0:T(8,128)S(1)} %shard_map.253.near), channel_id=1, source_target_pairs={{0,1},{1,0},{2,3},{3,2},{4,5},{5,4},{6,7},{7,6},{8,9},{9,8},{10,11... | collective-permute-start | bytes 614408 | tf_op jit(solution)/shard_map/ppermute | solution.py:43
  73.7 1.2 %copy-start.5 = (bf16[64,4096]{1,0:T(8,128)(2,1)S(1)}, bf16[64,4096]{1,0:T(8,128)(2,1)}, u32[]{:S(2)}) copy-start(bf16[64,4096]{1,0:T(8,128)(2,1)} %w_out.1) | copy-start | bytes 1572868
  73.7 1.2 %copy-start.6 = (bf16[512,128]{1,0:T(8,128)(2,1)S(1)}, bf16[512,128]{1,0:T(8,128)(2,1)}, u32[]{:S(2)}) copy-start(bf16[512,128]{1,0:T(8,128)(2,1)} %w_attn.1) | copy-start | bytes 393220
  73.8 1.2 %copy-start.9 = (bf16[256,64]{0,1:T(8,128)(2,1)S(1)}, bf16[256,64]{0,1:T(8,128)(2,1)}, u32[]{:S(2)}) copy-start(bf16[256,64]{0,1:T(8,128)(2,1)} %param.33) | copy-start | bytes 98308
  73.8 1.2 %copy-start.11 = (f32[16,64]{1,0:T(8,128)S(1)}, f32[16,64]{1,0:T(8,128)}, u32[]{:S(2)}) copy-start(f32[16,64]{1,0:T(8,128)} %log_decay.1) | copy-start | bytes 12292
  73.8 1.2 %copy-start.15 = (f32[64]{0:T(128)S(1)}, f32[64]{0:T(128)}, u32[]{:S(2)}) copy-start(f32[64]{0:T(128)} %param.34) | copy-start | bytes 772
  76.6 24.1 %copy-start.17 = (bf16[96,32]{0,1:T(8,128)(2,1)S(1)}, bf16[96,32]{0,1:T(8,128)(2,1)}, u32[]{:S(2)}) copy-start(bf16[96,32]{0,1:T(8,128)(2,1)} %param.25) | copy-start | bytes 18436
  76.6 2.1 %collective-permute-start.12 = (bf16[64,32,96]{2,1,0:T(8,128)(2,1)S(1)}, bf16[64,32,96]{2,1,0:T(8,128)(2,1)S(1)}, u32[]{:S(2)}, u32[]{:S(2)}) collective-permute-start(bf16[64,32,96]{2,1,0:T(8,128)(2,1)S(1)} %get-tuple-element.20), channel_id=1, source_target_pairs={{0,1},{1,0},{2,3},{3,2},{4,5},{5,4},{6,7},{7,6},{8,9},{9,8},{10,11... | collective-permute-start | bytes 1179656 | tf_op jit(solution)/shard_map/ppermute | solution.py:43
  (7 other events, 5.9 us)

commit v2 on v1

--- a/solution.py
+++ b/solution.py
@@ -12,6 +12,7 @@
 GRP_SEQ = ("grp", "seq_0", "seq_1", "seq_2")
 SEQ = ("seq_0", "seq_1", "seq_2")
 CHIPS = ("grp", "seq_0", "seq_1")
+PLANE = ("seq_0", "seq_1")
 EPSILON = 1e-05
 ROPE_BASE = 10000.0
 F32 = jnp.float32
@@ -303,42 +304,67 @@
     for copy in (*table_copies, *row_copies):
         copy.wait()
     scale = HEAD_SIZE ** (-0.5)
-    slot_ids = lax.broadcasted_iota(jnp.int32, (1, window), 1)
+    blocks = [(b, g) for b in range(seqs) for g in range(kv_heads)]
+    height = len(blocks) * 8
+    spare = jnp.zeros((8 - group, HEAD_SIZE), F32)
+    stacked, cos, sin, new_key, new_value = [], [], [], [], []
+    for b, g in blocks:
+        lanes = slice(g * HEAD_SIZE, (g + 1) * HEAD_SIZE)
+        for i in range(group):
+            head = g * group + i
+            stacked.append(query[b : b + 1, head * HEAD_SIZE : (head + 1) * HEAD_SIZE])
+        stacked.append(spare)
+        cos.append(jnp.broadcast_to(cos_rows[b : b + 1, :], (8, HEAD_SIZE)))
+        sin.append(jnp.broadcast_to(sin_rows[b : b + 1, :], (8, HEAD_SIZE)))
+        new_key.append(jnp.broadcast_to(fresh_key[b : b + 1, lanes], (8, HEAD_SIZE)))
+        new_value.append(jnp.broadcast_to(fresh_value[b : b + 1, lanes], (8, HEAD_SIZE)))
+    cos = jnp.concatenate(cos, axis=0)
+    sin = jnp.concatenate(sin, axis=0)
+
+    def turned(part):
+        return (part * cos + pltpu.roll(part, HEAD_SIZE // 2, 1) * sin).astype(BF16)
+
+    q = turned(jnp.concatenate(stacked, axis=0))
+    k_new = turned(jnp.concatenate(new_key, axis=0))
+    scores = jnp.concatenate(
+        [
+            lax.dot_general(
+                q[n * 8 : n * 8 + 8],
+                keys[b, :, g * HEAD_SIZE : (g + 1) * HEAD_SIZE],
+                NT,
+                preferred_element_type=F32,
+            )
+            for n, (b, g) in enumerate(blocks)
+        ],
+        axis=0,
+    ) * scale
+    fresh = jnp.sum(q.astype(F32) * k_new.astype(F32), axis=1, keepdims=True) * scale
+    slot_ids = lax.broadcasted_iota(jnp.int32, (height, window), 1)
+    owner = lax.broadcasted_iota(jnp.int32, (height, window), 0) // (8 * kv_heads)
+    length = jnp.where(
+        owner == 0,
+        lengths[first],
+        jnp.where(owner == 1, lengths[first + 1], lengths[first + 2]),
+    )
+    valid = slot_ids < length
+    scores = jnp.where(valid, scores, -1e30)
+    top = jnp.maximum(jnp.max(scores, axis=1, keepdims=True), fresh)
+    shares = jnp.where(valid, jnp.exp(scores - top), 0.0)
+    share_new = jnp.exp(fresh - top)
+    denominator = jnp.sum(shares, axis=1, keepdims=True) + share_new
+    rounded = shares.astype(BF16)
+    summed = jnp.concatenate(
+        [
+            dot(rounded[n * 8 : n * 8 + 8], values[b, :, g * HEAD_SIZE : (g + 1) * HEAD_SIZE])
+            for n, (b, g) in enumerate(blocks)
+        ],
+        axis=0,
+    )
+    result = (summed + share_new * jnp.concatenate(new_value, axis=0)) / denominator
+    result = result.astype(BF16).astype(F32)
     out[...] = jnp.zeros((SLOT, HEAD_SIZE), F32)
-
-    def turned(part, cos, sin):
-        return (part * cos + pltpu.roll(part, HEAD_SIZE // 2, 1) * sin).astype(BF16)
-
-    for b in range(seqs):
-        length = lengths[first + b]
-        cos = cos_rows[b : b + 1, :]
-        sin = sin_rows[b : b + 1, :]
-        valid = slot_ids < length
-        for g in range(kv_heads):
-            lanes = slice(g * HEAD_SIZE, (g + 1) * HEAD_SIZE)
-            heads = [
-                query[b : b + 1, (g * group + i) * HEAD_SIZE : (g * group + i + 1) * HEAD_SIZE]
-                for i in range(group)
-            ]
-            stacked = jnp.concatenate(heads + [jnp.zeros((8 - group, HEAD_SIZE), F32)], axis=0)
-            q = turned(stacked, cos, sin)
-            k_new = turned(jnp.broadcast_to(fresh_key[b : b + 1, lanes], (8, HEAD_SIZE)), cos, sin)
-            scores = (
-                lax.dot_general(q, keys[b, :, lanes], NT, preferred_element_type=F32) * scale
-            )
-            fresh = (
-                jnp.sum(q.astype(F32) * k_new.astype(F32), axis=1, keepdims=True) * scale
-            )
-            scores = jnp.where(valid, scores, -1e30)
-            top = jnp.maximum(jnp.max(scores, axis=1, keepdims=True), fresh)
-            weights = jnp.where(valid, jnp.exp(scores - top), 0.0)
-            weight_new = jnp.exp(fresh - top)
-            denominator = jnp.sum(weights, axis=1, keepdims=True) + weight_new
-            summed = dot(weights.astype(BF16), values[b, :, lanes])
-            summed = summed + weight_new * fresh_value[b : b + 1, lanes]
-            result = (summed / denominator).astype(BF16).astype(F32)
-            at = (b * kv_heads + g) * group
-            out[at : at + group, :] = result[0:group, :]
+    for n in range(len(blocks)):
+        out[n * group : (n + 1) * group, :] = result[n * 8 : n * 8 + group, :]
 
 
 def attended_rows(lengths, normed, w_query, w_key, w_value, keys, values, cosines, sines):
@@ -370,27 +396,32 @@
 
 
 def pack_kernel(s0, s1, s2, s3, attended, out):
-    out[0:ROWS, :] = (s0[...] + s1[...]) + (s2[...] + s3[...])
-    out[ROWS:, :] = attended[...]
-
-
-def combine_kernel(p0, p1, p2, p3, out):
-    out[0:ROWS, :] = (p0[0:ROWS] + p1[0:ROWS]) + (p2[0:ROWS] + p3[0:ROWS])
-    size = p0.shape[0] - ROWS
-    for k, part in enumerate((p0, p1, p2, p3)):
-        out[ROWS + k * size : ROWS + (k + 1) * size, :] = part[ROWS:, :]
+    low = ((s0[...] + s1[...]) + (s2[...] + s3[...])).astype(BF16)
+    rows = attended[...].astype(BF16)
+    for k in range(out.shape[0]):
+        out[k, 0:ROWS, :] = low
+        out[k, ROWS:, :] = rows
+
+
+def combine_kernel(arrived, low_out, rows_out):
+    total = arrived[0, 0:ROWS, :].astype(F32)
+    rows_out[0:SLOT, :] = arrived[0, ROWS:, :]
+    for k in range(1, arrived.shape[0]):
+        total = total + arrived[k, 0:ROWS, :].astype(F32)
+        rows_out[k * SLOT : (k + 1) * SLOT, :] = arrived[k, ROWS:, :]
+    low_out[...] = total
 
 
 def outer_kernel(
-    near, far, w_step, log_decay, step_bias, skip, conv, gate, state, w_out, term, w_attn,
+    near, far, near_rows, far_rows, w_step, log_decay, step_bias, skip, conv, gate, state, w_out, term, w_attn,
     state_out, keep_out, send_out, total,
 ):
-    _, x, y, c = here()
+    c = lax.axis_index("seq_2").astype(jnp.int32)
     seq = own_seq()
     batch = conv.shape[1]
     mine = c == 0
-    near_low = near[0:ROWS, 0:batch]
-    far_low = far[0:ROWS, 0:batch]
+    near_low = near[:, 0:batch]
+    far_low = far[:, 0:batch]
     low = jnp.concatenate(
         [jnp.where(mine, near_low, far_low), jnp.where(mine, far_low, near_low)], axis=0
     )
@@ -414,17 +445,15 @@
     gated = (mixed * gate[...]).astype(BF16)
     total[...] = term[...] + lax.dot_general(gated, w_out[...], TN, preferred_element_type=F32)
 
-    slots = near.shape[0] - ROWS
-    attended = jnp.concatenate([near[ROWS:, :], far[ROWS:, :]], axis=0).astype(BF16)
+    slots = near_rows.shape[0]
+    attended = jnp.concatenate([near_rows[...], far_rows[...]], axis=0)
     seqs = 3
     heads = w_attn.shape[0] // HEAD_SIZE
     token = lax.broadcasted_iota(jnp.int32, (batch, 2 * slots), 0)
     source = lax.broadcasted_iota(jnp.int32, (batch, 2 * slots), 1)
     owner = token // seqs
-    kx = lax.rem(x - owner // 8 + RING, RING)
-    ky = lax.rem(y - (owner // 2) % 4 + RING, RING)
-    kc = jnp.where(owner % 2 == c, 0, 1)
-    at = kc * slots + (ky * RING + kx) * SLOT + (token % seqs) * heads
+    other_core = jnp.where(owner % 2 == c, 0, 1)
+    at = other_core * slots + (owner // 2) * SLOT + (token % seqs) * heads
     attn = jnp.zeros((batch, w_attn.shape[1]), F32)
     for h in range(heads):
         pick = jnp.where(source == at + h, 1.0, 0.0).astype(BF16)
@@ -499,7 +528,8 @@
         fetched=(3,),
         scratch=(pltpu.VMEM((channels, width), BF16), pltpu.SemaphoreType.DMA),
     )
-    half = low[0] + shifted(low[1], "seq_2", 1)
+    paired = shifted(low[1], "seq_2", 1)
+    half = low[0] + paired
     arrived = from_ring(half, "grp")
     attended = attended_rows(
         window_lengths, normed, w_query, key_projection, value_projection, keys, values,
@@ -512,20 +542,23 @@
     )
     (term,) = vmem_call(down_kernel, (((batch, width), F32, True),), (act, w_mlp_down))
     (packed,) = vmem_call(
-        pack_kernel, (((ROWS + SLOT, HEAD_SIZE), F32, True),), (*arrived, attended)
-    )
-    for axis in ("seq_0", "seq_1"):
-        parts = from_ring(packed, axis)
-        size = ROWS + RING * (packed.shape[0] - ROWS)
-        (packed,) = vmem_call(combine_kernel, (((size, HEAD_SIZE), F32, True),), parts)
-    packed_other = shifted(packed, "seq_2", 1)
+        pack_kernel, (((16, ROWS + SLOT, HEAD_SIZE), BF16, True),), (*arrived, attended)
+    )
+    packed = lax.all_to_all(packed, PLANE, 0, 0, tiled=True)
+    near_low, near_rows = vmem_call(
+        combine_kernel,
+        (((ROWS, HEAD_SIZE), F32, True), ((16 * SLOT, HEAD_SIZE), BF16, True)),
+        (packed,),
+    )
+    far_low = shifted(near_low, "seq_2", 1)
+    far_rows = shifted(near_rows, "seq_2", 1)
 
     piece = ((64, features, batch), BF16, True)
     state_new, keep, send = vmem_call(
         outer_kernel,
         (((states, channels, batch), F32, False), piece, piece),
         (
-            packed, packed_other, w_step.T, log_decay, step_bias[None], skip_gain[None], conv, gate,
+            near_low, far_low, near_rows, far_rows, w_step.T, log_decay, step_bias[None], skip_gain[None], conv, gate,
             jnp.transpose(ssm_state, (1, 2, 0)), w_ssm_out, term, w_attn_out,
         ),
         scratch=(pltpu.VMEM((batch, width), F32),),

time: 102 us -> 99 us (0.971)
  blocking collectives: 46.3 us -> 60.3 us
  waiting for transfers between devices: 13.1 us -> 4.69 us
  starting transfers between devices: 11.9 us -> 4.41 us
    all_to_all x0 -> x1, blocking collectives: none -> 16 us  [block(): packed = lax.all_to_all(packed, PLANE, 0, 0, tiled=True)]
    ppermute x13 -> x8, waiting for transfers between devices: 13.1 us -> 4.69 us  [shifted(): lax.ppermute(value, axis, [(i, (i + step) % size) for i in range(size)])]
    ppermute x13 -> x8, starting transfers between devices: 11.9 us -> 4.41 us  [shifted(): lax.ppermute(value, axis, [(i, (i + step) % size) for i in range(size)])]
    all_to_all x1, blocking collectives: 21.7 us -> 19.7 us  [block(): arrived = lax.all_to_all(summed, CHIPS, 0, 0, tiled=True)]
    pallas_call x7 -> x6, Pallas kernels: 4.52 us -> 4.59 us  [vmem_call(): pl.pallas_call(kernel, out_shape=tuple((pltpu.VMEM(shape, dtype) if inner...]
  transfers between devices with their start and end apart: 13 -> 8, of which waited for: 8 -> 3; matrix products, arithmetic and copies ran while one was open for 0% -> 0% of each run, Pallas kernels for 19% -> 19%
where the time goes in v2:
time: 99 us; the launch traced here: 98.4 us
  blocking collectives  60.3 us (61%)
  Pallas kernels  22.1 us (22%)
  local copies, waits for them, and re-layouts  5.2 us (5%)
  waiting for transfers between devices  4.69 us (5%)
  starting transfers between devices  4.41 us (4%)
    all_to_all x1, blocking collectives, block(): held = lax.all_to_all(copies, CHIPS, 0, 0, tiled=True)  24.6 us
    all_to_all x1, blocking collectives, block(): arrived = lax.all_to_all(summed, CHIPS, 0, 0, tiled=True)  19.7 us
    all_to_all x1, blocking collectives, block(): packed = lax.all_to_all(packed, PLANE, 0, 0, tiled=True)  16 us
    pallas_call x1, Pallas kernels, window_rows(): pl.pallas_call(window_kernel, out_shape=(out, out), in_specs=[pl.BlockSpe...  11.9 us
    pallas_call x1, Pallas kernels, attended_rows(): pl.pallas_call(attention_kernel, out_shape=pltpu.VMEM((SLOT, HEAD_SIZE),...  5.57 us
    ppermute x8, waiting for transfers between devices, shifted(): lax.ppermute(value, axis, [(i, (i + step) % size) for i in range(size)])  4.69 us
    pallas_call x6, Pallas kernels, vmem_call(): pl.pallas_call(kernel, out_shape=tuple((pltpu.VMEM(shape, dtype) if inner...  4.59 us
    unnamed x36, local copies, waits for them, and re-layouts  4.42 us
  transfers between devices with their start and end apart: 8, of which 3 were waited for; matrix products, arithmetic and copies ran while one was open for 0% of the time, Pallas kernels for 19%

profile of v2, /device:TPU:0, one launch (start us, length us, event | category | flops | bytes accessed | tf_op | source)
XLA Modules:
  0.0 98.4 jit_solution(11770293380303164286)
XLA Ops:
  0.6 0.8 broadcast_in_dim.15
  1.4 24.6 %all_to_all.15.near = bf16[64,32,96]{2,1,0:T(8,128)(2,1)S(1)} all-to-all(bf16[64,32,96]{2,1,0:T(8,128)(2,1)S(1)} %broadcast_in_dim.15), channel_id=1, replica_groups=mesh['grp'=4,'seq_0'=4,'seq_1'=4,'seq_2'=2] {'grp','seq_0','seq_1'}, dimensions={0} | all-to-all | bytes 786432 | tf_op jit(solution)/shard_map/all_to_all | solution.py:510
  26.0 1.9 %collective-permute-done.far = bf16[64,32,96]{2,1,0:T(8,128)(2,1)S(1)} collective-permute-done((bf16[64,32,96]{2,1,0:T(8,128)(2,1)S(1)}, bf16[64,32,96]{2,1,0:T(8,128)(2,1)S(1)}, u32[]{:S(2)}, u32[]{:S(2)}) %collective-permute-start) | collective-permute-done | bytes 393248 | tf_op jit(solution)/shard_map/ppermute | solution.py:44
  27.9 0.8 copy-done.7
  28.7 0.8 copy-done.8
  29.5 0.7 copy-done.10
  30.2 0.7 copy-done.13
  30.9 0.7 copy-done.14
  31.6 1.5 %shard_map.248 = (bf16[4096,96]{1,0:T(8,128)(2,1)S(1)}, f32[64,96]{1,0:T(8,128)S(1)}, f32[2,144,128]{2,1,0:T(8,128)S(1)}) custom-call(bf16[64,32,96]{2,1,0:T(8,128)(2,1)S(1)} %all_to_all.15.near, bf16[64,32,96]{2,1,0:T(8,128)(2,1)S(1)} %collective-permute-done.far, f32[32,128]{1,0:T(8,128)S(1)} %bitcast.27, bf16[64,4096]{1,0:T(8,128)(2,1)} %bitcast.31, ...), custom_call_target="tpu_custom_call" | custom-call | tf_op jit(solution)/shard_map/pallas_call | solution.py:78
  33.4 1.1 %collective-permute-done.1 = f32[144,128]{1,0:T(8,128)S(1)} collective-permute-done((f32[144,128]{1,0:T(8,128)S(1)}, f32[144,128]{1,0:T(8,128)S(1)}, u32[]{:S(2)}, u32[]{:S(2)}) %collective-permute-start.1) | collective-permute-done | bytes 73760 | tf_op jit(solution)/shard_map/ppermute | solution.py:44
  34.7 2.1 %collective-permute-start.3 = (f32[144,128]{1,0:T(8,128)S(1)}, f32[144,128]{1,0:T(8,128)S(1)}, u32[]{:S(2)}, u32[]{:S(2)}) collective-permute-start(f32[144,128]{1,0:T(8,128)S(1)} %bitcast_add_fusion.s0), channel_id=1, source_target_pairs={{0,64},{32,96},{64,0},{96,32},{1,65},{33,97},{65,1},{97,33},{2,66}... | collective-permute-start | bytes 221192 | tf_op jit(solution)/shard_map/ppermute | solution.py:44
  36.8 1.1 %collective-permute-start.4 = (f32[144,128]{1,0:T(8,128)S(1)}, f32[144,128]{1,0:T(8,128)S(1)}, u32[]{:S(2)}, u32[]{:S(2)}) collective-permute-start(f32[144,128]{1,0:T(8,128)S(1)} %bitcast_add_fusion.s0), channel_id=1, source_target_pairs={{0,96},{32,0},{64,32},{96,64},{1,97},{33,1},{65,33},{97,65},{2,98}... | collective-permute-start | bytes 221192 | tf_op jit(solution)/shard_map/ppermute | solution.py:44
  37.9 11.9 %shard_map.249 = (bf16[3,512,256]{2,1,0:T(8,128)(2,1)}, bf16[3,512,256]{2,1,0:T(8,128)(2,1)}) custom-call(s32[96]{0:T(128)S(1)} %copy-done.12, bf16[3,512,4096]{2,1,0:T(8,128)(2,1)} %cached.1, bf16[4096,256]{1,0:T(8,128)(2,1)} %w_key.3, bf16[4096,256]{1,0:T(8,128)(2,1)} %w_value.3, f32[520,128]{1,0:T(8,128)} %constant.6.clone.cosines, ...), custom_call_target="tpu_custom_call" | custom-call | tf_op jit(solution)/shard_map/pallas_call | solution.py:168
  49.8 5.6 %shard_map.250.attended = f32[16,128]{1,0:T(8,128)S(1)} custom-call(s32[96]{0:T(128)S(1)} %copy-done.12, bf16[4096,96]{1,0:T(8,128)(2,1)S(1)} %get-tuple-element.15.normed, bf16[4096,512]{1,0:T(8,128)(2,1)} %w_query.1, bf16[4096,256]{1,0:T(8,128)(2,1)} %w_key.3, bf16[4096,256]{1,0:T(8,128)(2,1)} %w_value.3, bf16[3,512,256]{2,1,0:T(8,128)(2,1)} %get-tuple-element.16.key_rows, ...), custom_call_target="tpu_custom_call" | custom-call | tf_op jit(solution)/shard_map/pallas_call | solution.py:375
  55.5 16.0 %all_to_all.16.arrived = bf16[16,160,128]{2,1,0:T(8,128)(2,1)S(1)} all-to-all(bf16[16,160,128]{2,1,0:T(8,128)(2,1)S(1)} %shard_map.251), channel_id=1, replica_groups=mesh['grp'=4,'seq_0'=4,'seq_1'=4,'seq_2'=2] {'seq_0','seq_1'}, dimensions={0} | all-to-all | bytes 1310720 | tf_op jit(solution)/shard_map/all_to_all | solution.py:547
  71.7 0.5 collective-permute-start.6
  72.2 0.8 shard_map.253
  73.1 0.4 shard_map.254.term
  73.5 0.5 copy-done.4
  74.3 1.7 %shard_map.255 = (f32[16,64,96]{2,1,0:T(8,128)}, bf16[64,32,96]{2,1,0:T(8,128)(2,1)S(1)}, bf16[64,32,96]{2,1,0:T(8,128)(2,1)S(1)}) custom-call(f32[144,128]{1,0:T(8,128)S(1)} %get-tuple-element.18.near, f32[144,128]{1,0:T(8,128)S(1)} %collective-permute-done.5.far, bf16[256,128]{1,0:T(8,128)(2,1)S(1)} %get-tuple-element.19.near_rows, ...), custom_call_target="tpu_custom_call" | custom-call | tf_op jit(solution)/shard_map/pallas_call | solution.py:78
  75.9 0.3 collective-permute-start.7
  76.2 1.6 %collective-permute-done.7 = bf16[64,32,96]{2,1,0:T(8,128)(2,1)S(1)} collective-permute-done((bf16[64,32,96]{2,1,0:T(8,128)(2,1)S(1)}, bf16[64,32,96]{2,1,0:T(8,128)(2,1)S(1)}, u32[]{:S(2)}, u32[]{:S(2)}) %collective-permute-start.7) | collective-permute-done | bytes 393248 | tf_op jit(solution)/shard_map/ppermute | solution.py:44
  78.0 19.7 %all_to_all.17 = bf16[64,32,96]{2,1,0:T(8,128)(2,1)S(1)} all-to-all(bf16[64,32,96]{2,1,0:T(8,128)(2,1)S(1)} %add_convert_fusion), channel_id=1, replica_groups=mesh['grp'=4,'seq_0'=4,'seq_1'=4,'seq_2'=2] {'grp','seq_0','seq_1'}, dimensions={0} | all-to-all | bytes 786432 | tf_op jit(solution)/shard_map/all_to_all | solution.py:568
  97.8 0.6 fusion
  (45 shorter events, 1.2 us)
Async XLA Ops:
  0.6 37.2 %copy-start.12 = (s32[96]{0:T(128)S(1)}, s32[96]{0:T(128)}, u32[]{:S(2)}) copy-start(s32[96]{0:T(128)} %lengths.3) | copy-start | bytes 1156
  26.0 1.9 %collective-permute-start = (bf16[64,32,96]{2,1,0:T(8,128)(2,1)S(1)}, bf16[64,32,96]{2,1,0:T(8,128)(2,1)S(1)}, u32[]{:S(2)}, u32[]{:S(2)}) collective-permute-start(bf16[64,32,96]{2,1,0:T(8,128)(2,1)S(1)} %all_to_all.15.near), channel_id=1, source_target_pairs={{0,1},{1,0},{2,3},{3,2},{4,5},{5,4},{6,7},{7,6},{8,9},{9,8},{10,11... | collective-permute-start | bytes 1179656 | tf_op jit(solution)/shard_map/ppermute | solution.py:44
  27.9 0.8 copy-start.7
  28.7 0.8 copy-start.8
  29.5 0.7 copy-start.10
  33.1 1.3 %collective-permute-start.1 = (f32[144,128]{1,0:T(8,128)S(1)}, f32[144,128]{1,0:T(8,128)S(1)}, u32[]{:S(2)}, u32[]{:S(2)}) collective-permute-start(f32[144,128]{1,0:T(8,128)S(1)} %slice_bitcast_fusion), channel_id=1, source_target_pairs={{0,1},{1,0},{2,3},{3,2},{4,5},{5,4},{6,7},{7,6},{8,9},{9,8},{10,11... | collective-permute-start | bytes 221192 | tf_op jit(solution)/shard_map/ppermute | solution.py:44
  34.5 20.9 %collective-permute-start.2 = (f32[144,128]{1,0:T(8,128)S(1)}, f32[144,128]{1,0:T(8,128)S(1)}, u32[]{:S(2)}, u32[]{:S(2)}) collective-permute-start(f32[144,128]{1,0:T(8,128)S(1)} %bitcast_add_fusion.s0), channel_id=1, source_target_pairs={{0,32},{32,64},{64,96},{96,0},{1,33},{33,65},{65,97},{97,1},{2,34}... | collective-permute-start | bytes 221192 | tf_op jit(solution)/shard_map/ppermute | solution.py:44
  34.7 20.7 %collective-permute-start.3 = (f32[144,128]{1,0:T(8,128)S(1)}, f32[144,128]{1,0:T(8,128)S(1)}, u32[]{:S(2)}, u32[]{:S(2)}) collective-permute-start(f32[144,128]{1,0:T(8,128)S(1)} %bitcast_add_fusion.s0), channel_id=1, source_target_pairs={{0,64},{32,96},{64,0},{96,32},{1,65},{33,97},{65,1},{97,33},{2,66}... | collective-permute-start | bytes 221192 | tf_op jit(solution)/shard_map/ppermute | solution.py:44
  36.8 18.6 %collective-permute-start.4 = (f32[144,128]{1,0:T(8,128)S(1)}, f32[144,128]{1,0:T(8,128)S(1)}, u32[]{:S(2)}, u32[]{:S(2)}) collective-permute-start(f32[144,128]{1,0:T(8,128)S(1)} %bitcast_add_fusion.s0), channel_id=1, source_target_pairs={{0,96},{32,0},{64,32},{96,64},{1,97},{33,1},{65,33},{97,65},{2,98}... | collective-permute-start | bytes 221192 | tf_op jit(solution)/shard_map/ppermute | solution.py:44
  55.4 16.8 %copy-start.1 = (bf16[4096,112]{0,1:T(8,128)(2,1)S(1)}, bf16[4096,112]{0,1:T(8,128)(2,1)}, u32[]{:S(2)}) copy-start(bf16[4096,112]{0,1:T(8,128)(2,1)} %param.43) | copy-start | bytes 2752516
  55.4 16.8 %copy-start.2 = (bf16[4096,112]{0,1:T(8,128)(2,1)S(1)}, bf16[4096,112]{0,1:T(8,128)(2,1)}, u32[]{:S(2)}) copy-start(bf16[4096,112]{0,1:T(8,128)(2,1)} %param.44) | copy-start | bytes 2752516
  55.4 16.8 %copy-start.3 = (bf16[4096,64]{0,1:T(8,128)(2,1)S(1)}, bf16[4096,64]{0,1:T(8,128)(2,1)}, u32[]{:S(2)}) copy-start(bf16[4096,64]{0,1:T(8,128)(2,1)} %param.28) | copy-start | bytes 1572868
  71.5 1.6 %copy-start = (bf16[112,4096]{1,0:T(8,128)(2,1)S(1)}, bf16[112,4096]{1,0:T(8,128)(2,1)}, u32[]{:S(2)}) copy-start(bf16[112,4096]{1,0:T(8,128)(2,1)} %w_mlp_down.1) | copy-start | bytes 2752516
  71.6 1.9 %collective-permute-start.5 = (f32[144,128]{1,0:T(8,128)S(1)}, f32[144,128]{1,0:T(8,128)S(1)}, u32[]{:S(2)}, u32[]{:S(2)}) collective-permute-start(f32[144,128]{1,0:T(8,128)S(1)} %get-tuple-element.18.near), channel_id=1, source_target_pairs={{0,1},{1,0},{2,3},{3,2},{4,5},{5,4},{6,7},{7,6},{8,9},{9,8},{10,11... | collective-permute-start | bytes 221192 | tf_op jit(solution)/shard_map/ppermute | solution.py:44
  71.7 1.8 %collective-permute-start.6 = (bf16[256,128]{1,0:T(8,128)(2,1)S(1)}, bf16[256,128]{1,0:T(8,128)(2,1)S(1)}, u32[]{:S(2)}, u32[]{:S(2)}) collective-permute-start(bf16[256,128]{1,0:T(8,128)(2,1)S(1)} %get-tuple-element.19.near_rows), channel_id=1, source_target_pairs={{0,1},{1,0},{2,3},{3,2},{4,5},{5,4},{6,7},{7,6},{8,9},{9,8},{10,11... | collective-permute-start | bytes 196616 | tf_op jit(solution)/shard_map/ppermute | solution.py:44
  73.0 1.0 %copy-start.4 = (f32[96,16,64]{0,2,1:T(8,128)S(1)}, f32[96,16,64]{0,2,1:T(8,128)}, u32[]{:S(2)}) copy-start(f32[96,16,64]{0,2,1:T(8,128)} %param.37) | copy-start | bytes 1179652
  73.0 1.2 %copy-start.5 = (bf16[64,4096]{1,0:T(8,128)(2,1)S(1)}, bf16[64,4096]{1,0:T(8,128)(2,1)}, u32[]{:S(2)}) copy-start(bf16[64,4096]{1,0:T(8,128)(2,1)} %w_out.1) | copy-start | bytes 1572868
  73.0 1.2 %copy-start.6 = (bf16[512,128]{1,0:T(8,128)(2,1)S(1)}, bf16[512,128]{1,0:T(8,128)(2,1)}, u32[]{:S(2)}) copy-start(bf16[512,128]{1,0:T(8,128)(2,1)} %w_attn.1) | copy-start | bytes 393220
  73.1 1.2 %copy-start.9 = (bf16[256,64]{0,1:T(8,128)(2,1)S(1)}, bf16[256,64]{0,1:T(8,128)(2,1)}, u32[]{:S(2)}) copy-start(bf16[256,64]{0,1:T(8,128)(2,1)} %param.33) | copy-start | bytes 98308
  73.1 1.2 %copy-start.11 = (f32[16,64]{1,0:T(8,128)S(1)}, f32[16,64]{1,0:T(8,128)}, u32[]{:S(2)}) copy-start(f32[16,64]{1,0:T(8,128)} %log_decay.1) | copy-start | bytes 12292
  73.1 1.2 %copy-start.15 = (f32[64]{0:T(128)S(1)}, f32[64]{0:T(128)}, u32[]{:S(2)}) copy-start(f32[64]{0:T(128)} %param.34) | copy-start | bytes 772
  73.1 1.2 %copy-start.16 = (f32[64]{0:T(128)S(1)}, f32[64]{0:T(128)}, u32[]{:S(2)}) copy-start(f32[64]{0:T(128)} %param.36) | copy-start | bytes 772
  75.9 21.9 %copy-start.17 = (bf16[96,32]{0,1:T(8,128)(2,1)S(1)}, bf16[96,32]{0,1:T(8,128)(2,1)}, u32[]{:S(2)}) copy-start(bf16[96,32]{0,1:T(8,128)(2,1)} %param.25) | copy-start | bytes 18436
  75.9 1.9 %collective-permute-start.7 = (bf16[64,32,96]{2,1,0:T(8,128)(2,1)S(1)}, bf16[64,32,96]{2,1,0:T(8,128)(2,1)S(1)}, u32[]{:S(2)}, u32[]{:S(2)}) collective-permute-start(bf16[64,32,96]{2,1,0:T(8,128)(2,1)S(1)} %get-tuple-element.24), channel_id=1, source_target_pairs={{0,1},{1,0},{2,3},{3,2},{4,5},{5,4},{6,7},{7,6},{8,9},{9,8},{10,11... | collective-permute-start | bytes 1179656 | tf_op jit(solution)/shard_map/ppermute | solution.py:44
  (2 other events, 1.3 us)

commit v3 on v2

--- a/solution.py
+++ b/solution.py
@@ -1,3 +1,5 @@
+import functools
+
 import jax
 import jax.numpy as jnp
 import numpy as np
@@ -12,7 +14,6 @@
 GRP_SEQ = ("grp", "seq_0", "seq_1", "seq_2")
 SEQ = ("seq_0", "seq_1", "seq_2")
 CHIPS = ("grp", "seq_0", "seq_1")
-PLANE = ("seq_0", "seq_1")
 EPSILON = 1e-05
 ROPE_BASE = 10000.0
 F32 = jnp.float32
@@ -20,8 +21,8 @@
 NT = (((1,), (1,)), ((), ()))
 TN = (((0,), (0,)), ((), ()))
 RING = 4
-ROWS = 144
 SLOT = 16
+PIECE = 4
 WEIGHT_PIECES = 4
 
 
@@ -44,23 +45,12 @@
     return lax.ppermute(value, axis, [(i, (i + step) % size) for i in range(size)])
 
 
-def from_ring(value, axis):
-    arrived = [value]
-    for step in (1, 3, 2):
-        arrived.append(shifted(value, axis, step))
-    return [arrived[0], arrived[1], arrived[3], arrived[2]]
-
-
 def dot(a, b):
     return jnp.dot(a, b, preferred_element_type=F32)
 
 
-def here():
-    return tuple(lax.axis_index(a).astype(jnp.int32) for a in GRP_SEQ)
-
-
 def own_seq():
-    _, x, y, c = here()
+    x, y, c = (lax.axis_index(a).astype(jnp.int32) for a in SEQ)
     return (x * RING + y) * 2 + c
 
 
@@ -72,26 +62,26 @@
     return pltpu.with_memory_space_constraint(value, pltpu.VMEM)
 
 
-def vmem_call(kernel, outs, operands, fetched=(), scratch=(), limit=12 << 20):
+def vmem_call(kernel, outs, operands, fetched=(), stored=(), scratch=(), limit=12 << 20):
     vmem = pl.BlockSpec(memory_space=pltpu.VMEM)
     anywhere = pl.BlockSpec(memory_space=pl.ANY)
     return pl.pallas_call(
         kernel,
-        out_shape=tuple(pltpu.VMEM(shape, dtype) if inner else jax.ShapeDtypeStruct(shape, dtype) for shape, dtype, inner in outs),
+        out_shape=tuple((pltpu.VMEM if inner else pltpu.HBM)(shape, dtype) for shape, dtype, inner in outs),
         in_specs=[anywhere if k in fetched else vmem for k in range(len(operands))],
-        out_specs=tuple(vmem for _ in outs),
+        out_specs=tuple(anywhere if k in stored else vmem for k in range(len(outs))),
         scratch_shapes=list(scratch),
         compiler_params=pltpu.CompilerParams(vmem_limit_bytes=limit),
     )(*((in_hbm if k in fetched else in_vmem)(v) for k, v in enumerate(operands)))
 
 
 def window_kernel(
-    lengths, cached, w_key, w_value, cosines, sines, key_out, value_out,
+    cached, w_key, w_value, cosines, sines, key_out, value_out,
     rows, weights, cos, sin, turned, plain, row_sem, first_sem, key_sem, value_sem, table_sem, out_sem,
+    *, begin,
 ):
-    seqs, window, width = cached.shape
-    columns = w_key.shape[1]
-    first = own_seq() * seqs
+    seqs, window = key_out.shape[0], key_out.shape[1]
+    width, columns = w_key.shape
     pieces = WEIGHT_PIECES
     step = width // pieces
 
@@ -104,7 +94,7 @@
             pltpu.make_async_copy(
                 w_value.at[span], weights.at[span, pl.ds(columns, columns)], value_sem.at[p]
             ),
-            pltpu.make_async_copy(cached.at[0, :, span], rows.at[0, :, span], first_sem.at[p]),
+            pltpu.make_async_copy(cached.at[begin, :, span], rows.at[0, :, span], first_sem.at[p]),
         )
 
     tables = (
@@ -112,7 +102,7 @@
         pltpu.make_async_copy(sines.at[pl.ds(0, window)], sin, table_sem.at[1]),
     )
     later = [
-        pltpu.make_async_copy(cached.at[b], rows.at[b], row_sem.at[b]) for b in range(1, seqs)
+        pltpu.make_async_copy(cached.at[begin + b], rows.at[b], row_sem.at[b]) for b in range(1, seqs)
     ]
     for p in range(pieces):
         for copy in piece_copies(p):
@@ -159,16 +149,16 @@
             copy.wait()
 
 
-def window_rows(lengths, cached, w_key, w_value, cosines, sines):
-    seqs, window, width = cached.shape
+def window_rows(begin, seqs, cached, w_key, w_value, cosines, sines):
+    _, window, width = cached.shape
     columns = w_key.shape[1]
     anywhere = pl.BlockSpec(memory_space=pl.ANY)
     out = pltpu.HBM((seqs, window, columns), BF16)
     dma = pltpu.SemaphoreType.DMA
     return pl.pallas_call(
-        window_kernel,
+        functools.partial(window_kernel, begin=begin),
         out_shape=(out, out),
-        in_specs=[pl.BlockSpec(memory_space=pltpu.SMEM)] + [anywhere] * 5,
+        in_specs=[anywhere] * 5,
         out_specs=(anywhere, anywhere),
         scratch_shapes=[
             pltpu.VMEM((seqs, window, width), BF16),
@@ -185,11 +175,12 @@
             dma((2, seqs)),
         ],
         compiler_params=pltpu.CompilerParams(vmem_limit_bytes=40 << 20),
-    )(lengths, *(in_hbm(v) for v in (cached, w_key, w_value, cosines, sines)))
+    )(*(in_hbm(v) for v in (cached, w_key, w_value, cosines, sines)))
 
 
 def inner_kernel(
-    near, far, gain, w_in_hbm, w_proj, past, taps, bias, normed_out, conv_out, low_out, w_in, w_sem,
+    near, far, gain, w_in_hbm, w_proj, past, taps, bias, normed_hbm, conv_out, low_out,
+    normed_out, w_in, w_sem, normed_sem,
 ):
     fetch = pltpu.make_async_copy(w_in_hbm, w_in, w_sem)
     fetch.start()
@@ -215,6 +206,8 @@
             at = (j % per_gain) * rows
             column = gains[at : at + rows, j // per_gain : j // per_gain + 1]
             normed_out[j * rows : (j + 1) * rows, :] = (pair[k] * scale * column).astype(BF16)
+    keep = pltpu.make_async_copy(normed_out, normed_hbm, normed_sem)
+    keep.start()
     fetch.wait()
     fresh = dot(w_in[...], normed_out[...]).astype(BF16).astype(F32)
     params = jnp.concatenate([taps[...], bias[...], jnp.zeros((3, taps.shape[1]), F32)], axis=0).T
@@ -225,8 +218,12 @@
     conv_out[...] = conv
     low = lax.dot_general(w_proj[...], conv.astype(BF16), TN, preferred_element_type=F32)
     low = jnp.concatenate([low, jnp.zeros((low.shape[0], 128 - batch), F32)], axis=1)
-    low_out[c] = low[0:ROWS]
-    low_out[1 - c] = low[ROWS:]
+    for k in range(low_out.shape[0]):
+        if k < low.shape[0] // PIECE:
+            low_out[k] = low[k * PIECE : (k + 1) * PIECE]
+        else:
+            low_out[k] = jnp.zeros((PIECE, 128), F32)
+    keep.wait()
 
 
 def gate_kernel(normed, w_gate, w_mlp_gate, w_mlp_up, gate_out, act_out):
@@ -240,8 +237,8 @@
 
 
 def attention_kernel(
-    lengths, normed, w_query, w_key, w_value, key_rows, value_rows, cosines, sines, out,
-    weights, keys, values, cos_rows, sin_rows, weight_sem, row_sem, table_sem,
+    lengths, normed_hbm, w_query, w_key, w_value, first_keys, first_values, later_keys,
+    later_values, cosines, sines, out, normed, normed_sem, weights, keys, values, cos_rows, sin_rows, weight_sem, row_sem, table_sem,
 ):
     seqs, window = keys.shape[0], keys.shape[1]
     columns = keys.shape[2]
@@ -270,9 +267,13 @@
         )
 
     row_copies = (
-        pltpu.make_async_copy(key_rows, keys, row_sem.at[0]),
-        pltpu.make_async_copy(value_rows, values, row_sem.at[1]),
-    )
+        pltpu.make_async_copy(first_keys, keys.at[pl.ds(0, 1)], row_sem.at[0]),
+        pltpu.make_async_copy(first_values, values.at[pl.ds(0, 1)], row_sem.at[1]),
+        pltpu.make_async_copy(later_keys, keys.at[pl.ds(1, seqs - 1)], row_sem.at[2]),
+        pltpu.make_async_copy(later_values, values.at[pl.ds(1, seqs - 1)], row_sem.at[3]),
+    )
+    fetch = pltpu.make_async_copy(normed_hbm, normed, normed_sem)
+    fetch.start()
     table_copies = []
     for b in range(seqs):
         at = pl.ds(lengths[first + b], 1)
@@ -287,6 +288,7 @@
             copy.start()
     for copy in (*table_copies, *row_copies):
         copy.start()
+    fetch.wait()
     row = lax.broadcasted_iota(jnp.int32, (8, batch), 0)
     column = lax.broadcasted_iota(jnp.int32, (8, batch), 1)
     pick = jnp.where((column == first + row) & (row < seqs), 1.0, 0.0).astype(BF16)
@@ -367,70 +369,76 @@
         out[n * group : (n + 1) * group, :] = result[n * 8 : n * 8 + group, :]
 
 
-def attended_rows(lengths, normed, w_query, w_key, w_value, keys, values, cosines, sines):
+def attended_rows(lengths, *operands):
+    normed, w_query, w_key, _, first_keys, _, later_keys = operands[:7]
     anywhere = pl.BlockSpec(memory_space=pl.ANY)
-    vmem = pl.BlockSpec(memory_space=pltpu.VMEM)
     dma = pltpu.SemaphoreType.DMA
-    width = normed.shape[0]
+    seqs = first_keys.shape[0] + later_keys.shape[0]
+    held = pltpu.VMEM((seqs, *first_keys.shape[1:]), BF16)
     return pl.pallas_call(
         attention_kernel,
         out_shape=pltpu.VMEM((SLOT, HEAD_SIZE), F32),
-        in_specs=[pl.BlockSpec(memory_space=pltpu.SMEM), vmem] + [anywhere] * 7,
-        out_specs=vmem,
+        in_specs=[pl.BlockSpec(memory_space=pltpu.SMEM)] + [anywhere] * len(operands),
+        out_specs=pl.BlockSpec(memory_space=pltpu.VMEM),
         scratch_shapes=[
-            pltpu.VMEM((width, w_query.shape[1] + 2 * w_key.shape[1]), BF16),
-            pltpu.VMEM(keys.shape, BF16),
-            pltpu.VMEM(values.shape, BF16),
+            pltpu.VMEM(normed.shape, BF16),
+            dma,
+            pltpu.VMEM((normed.shape[0], w_query.shape[1] + 2 * w_key.shape[1]), BF16),
+            held,
+            held,
             pltpu.VMEM((8, HEAD_SIZE), F32),
             pltpu.VMEM((8, HEAD_SIZE), F32),
             dma((3, WEIGHT_PIECES)),
-            dma((2,)),
-            dma((2, keys.shape[0])),
+            dma((4,)),
+            dma((2, seqs)),
         ],
-        compiler_params=pltpu.CompilerParams(vmem_limit_bytes=20 << 20),
-    )(
-        lengths,
-        in_vmem(normed),
-        *(in_hbm(v) for v in (w_query, w_key, w_value, keys, values, cosines, sines)),
-    )
-
-
-def pack_kernel(s0, s1, s2, s3, attended, out):
-    low = ((s0[...] + s1[...]) + (s2[...] + s3[...])).astype(BF16)
-    rows = attended[...].astype(BF16)
+        compiler_params=pltpu.CompilerParams(vmem_limit_bytes=24 << 20),
+    )(lengths, *(in_hbm(v) for v in operands))
+
+
+def pack_kernel(arrived, attended, out):
+    total = arrived[0]
+    for k in range(1, arrived.shape[0]):
+        total = total + arrived[k]
+    block = jnp.concatenate([attended[0 : SLOT - PIECE, :], total], axis=0).astype(BF16)
     for k in range(out.shape[0]):
-        out[k, 0:ROWS, :] = low
-        out[k, ROWS:, :] = rows
-
-
-def combine_kernel(arrived, low_out, rows_out):
-    total = arrived[0, 0:ROWS, :].astype(F32)
-    rows_out[0:SLOT, :] = arrived[0, ROWS:, :]
-    for k in range(1, arrived.shape[0]):
-        total = total + arrived[k, 0:ROWS, :].astype(F32)
-        rows_out[k * SLOT : (k + 1) * SLOT, :] = arrived[k, ROWS:, :]
-    low_out[...] = total
+        out[k] = block
 
 
 def outer_kernel(
-    near, far, near_rows, far_rows, w_step, log_decay, step_bias, skip, conv, gate, state, w_out, term, w_attn,
-    state_out, keep_out, send_out, total,
+    packed, w_step_hbm, log_decay, step_bias, skip, conv_hbm, gate_hbm, state, w_out_hbm, term,
+    w_attn_hbm, state_out, keep_out, send_out, total, w_step, conv, gate, w_out, w_attn, sems,
 ):
+    fetches = [
+        pltpu.make_async_copy(source, target, sems.at[k])
+        for k, (source, target) in enumerate(
+            (
+                (w_step_hbm, w_step),
+                (conv_hbm, conv),
+                (gate_hbm, gate),
+                (w_out_hbm, w_out),
+                (w_attn_hbm, w_attn),
+            )
+        )
+    ]
+    for fetch in fetches:
+        fetch.start()
     c = lax.axis_index("seq_2").astype(jnp.int32)
     seq = own_seq()
     batch = conv.shape[1]
     mine = c == 0
-    near_low = near[:, 0:batch]
-    far_low = far[:, 0:batch]
+    states = state.shape[0]
+    pieces = (w_step.shape[1] + 2 * states) // PIECE
     low = jnp.concatenate(
-        [jnp.where(mine, near_low, far_low), jnp.where(mine, far_low, near_low)], axis=0
+        [packed[k].astype(F32)[SLOT - PIECE :, 0:batch] for k in range(pieces)], axis=0
     )
     rank = w_step.shape[1]
-    states = state.shape[0]
     params = jnp.concatenate(
         [jnp.exp(log_decay[...]), step_bias[...], skip[...], jnp.zeros((6, conv.shape[0]), F32)],
         axis=0,
     ).T
+    for fetch in fetches:
+        fetch.wait()
     step = jax.nn.softplus(
         dot(w_step[...], low[0:rank].astype(BF16)) + params[:, states : states + 1]
     )
@@ -445,15 +453,14 @@
     gated = (mixed * gate[...]).astype(BF16)
     total[...] = term[...] + lax.dot_general(gated, w_out[...], TN, preferred_element_type=F32)
 
-    slots = near_rows.shape[0]
-    attended = jnp.concatenate([near_rows[...], far_rows[...]], axis=0)
-    seqs = 3
+    group = lax.axis_index("grp").astype(jnp.int32)
+    members = packed.shape[0] // RING
+    attended = packed[pl.ds(group * members, members)].reshape(members * SLOT, HEAD_SIZE)
+    seqs = batch // members
     heads = w_attn.shape[0] // HEAD_SIZE
-    token = lax.broadcasted_iota(jnp.int32, (batch, 2 * slots), 0)
-    source = lax.broadcasted_iota(jnp.int32, (batch, 2 * slots), 1)
-    owner = token // seqs
-    other_core = jnp.where(owner % 2 == c, 0, 1)
-    at = other_core * slots + (owner // 2) * SLOT + (token % seqs) * heads
+    token = lax.broadcasted_iota(jnp.int32, (batch, members * SLOT), 0)
+    source = lax.broadcasted_iota(jnp.int32, (batch, members * SLOT), 1)
+    at = (token // seqs) * SLOT + (token % seqs) * heads
     attn = jnp.zeros((batch, w_attn.shape[1]), F32)
     for h in range(heads):
         pick = jnp.where(source == at + h, 1.0, 0.0).astype(BF16)
@@ -510,58 +517,65 @@
     held = lax.all_to_all(copies, CHIPS, 0, 0, tiled=True)
     other = shifted(held, "seq_2", 1)
 
-    keys, values = window_rows(
-        window_lengths, cached_inputs, key_projection, value_projection, cosines, sines
-    )
-
+    tables = (key_projection, value_projection, cosines, sines)
+    first_rows = window_rows(0, 1, cached_inputs, *tables)
+
+    devices = 64 * 2
     normed, conv, low = vmem_call(
         inner_kernel,
         (
-            ((width, batch), BF16, True),
-            ((channels, batch), F32, True),
-            ((2, ROWS, 128), F32, True),
+            ((width, batch), BF16, False),
+            ((channels, batch), F32, False),
+            ((devices, PIECE, 128), F32, False),
         ),
         (
             held, other, norm_gain.reshape(-1, 128), w_ssm_in.T, w_state_proj,
             jnp.transpose(conv_state, (1, 2, 0)), conv_weight, conv_bias[None],
         ),
         fetched=(3,),
-        scratch=(pltpu.VMEM((channels, width), BF16), pltpu.SemaphoreType.DMA),
-    )
-    paired = shifted(low[1], "seq_2", 1)
-    half = low[0] + paired
-    arrived = from_ring(half, "grp")
-    attended = attended_rows(
-        window_lengths, normed, w_query, key_projection, value_projection, keys, values,
-        cosines, sines,
-    )
+        stored=(0,),
+        scratch=(
+            pltpu.VMEM((width, batch), BF16),
+            pltpu.VMEM((channels, width), BF16),
+            pltpu.SemaphoreType.DMA,
+            pltpu.SemaphoreType.DMA,
+        ),
+    )
+    low = lax.all_to_all(low, GRP_SEQ, 0, 0, tiled=True)
+    later_rows = window_rows(1, cached_inputs.shape[0] - 1, cached_inputs, *tables)
     gate, act = vmem_call(
         gate_kernel,
-        (((channels, batch), F32, True), ((w_mlp_up.shape[1], batch), BF16, True)),
+        (((channels, batch), F32, False), ((w_mlp_up.shape[1], batch), BF16, False)),
         (normed, w_ssm_gate.T, w_mlp_gate.T, w_mlp_up.T),
     )
+    attended = attended_rows(
+        window_lengths, normed, w_query, key_projection, value_projection, *first_rows,
+        *later_rows, cosines, sines,
+    )
+    (packed,) = vmem_call(
+        pack_kernel, (((devices, SLOT, HEAD_SIZE), BF16, True),), (low, attended)
+    )
+    packed = lax.all_to_all(packed, GRP_SEQ, 0, 0, tiled=True)
     (term,) = vmem_call(down_kernel, (((batch, width), F32, True),), (act, w_mlp_down))
-    (packed,) = vmem_call(
-        pack_kernel, (((16, ROWS + SLOT, HEAD_SIZE), BF16, True),), (*arrived, attended)
-    )
-    packed = lax.all_to_all(packed, PLANE, 0, 0, tiled=True)
-    near_low, near_rows = vmem_call(
-        combine_kernel,
-        (((ROWS, HEAD_SIZE), F32, True), ((16 * SLOT, HEAD_SIZE), BF16, True)),
-        (packed,),
-    )
-    far_low = shifted(near_low, "seq_2", 1)
-    far_rows = shifted(near_rows, "seq_2", 1)
 
     piece = ((64, features, batch), BF16, True)
     state_new, keep, send = vmem_call(
         outer_kernel,
         (((states, channels, batch), F32, False), piece, piece),
         (
-            near_low, far_low, near_rows, far_rows, w_step.T, log_decay, step_bias[None], skip_gain[None], conv, gate,
+            packed, w_step.T, log_decay, step_bias[None], skip_gain[None], conv, gate,
             jnp.transpose(ssm_state, (1, 2, 0)), w_ssm_out, term, w_attn_out,
         ),
-        scratch=(pltpu.VMEM((batch, width), F32),),
+        fetched=(1, 5, 6, 8, 10),
+        scratch=(
+            pltpu.VMEM((batch, width), F32),
+            pltpu.VMEM((channels, w_step.shape[0]), BF16),
+            pltpu.VMEM((channels, batch), F32),
+            pltpu.VMEM((channels, batch), F32),
+            pltpu.VMEM(w_ssm_out.shape, BF16),
+            pltpu.VMEM(w_attn_out.shape, BF16),
+            pltpu.SemaphoreType.DMA((5,)),
+        ),
     )
     came = shifted(send, "seq_2", 1)
     summed = (keep.astype(F32) + came.astype(F32)).astype(BF16)

time: 99 us -> 109 us (1.10)
  blocking collectives: 60.3 us -> 42.9 us
  starting transfers between devices: 4.41 us -> 14.6 us
  waiting for transfers between devices: 4.69 us -> 12.1 us
  Pallas kernels: 22.1 us -> 29.1 us
  local copies, waits for them, and re-layouts: 5.2 us -> 7.62 us
    all_to_all x1 -> x0, blocking collectives: 16 us -> none  [block(): packed = lax.all_to_all(packed, PLANE, 0, 0, tiled=True)]
    all_to_all x0 -> x2, starting transfers between devices: none -> 14.6 us  [the longest x1 9.94 us: block(): packed = lax.all_to_all(packed, GRP_SEQ, 0, 0, tiled=True)]
    all_to_all x0 -> x2, waiting for transfers between devices: none -> 8.31 us  [the longest x1 8.31 us: block(): packed = lax.all_to_all(packed, GRP_SEQ, 0, 0, tiled=True)]
    pallas_call x7, Pallas kernels: 16.5 us -> 22.1 us  [the longest x2 14.2 us: window_rows(): pl.pallas_call(functools.partial(window_kernel, begin=begin), out_shape=(...]
    ppermute x8 -> x2, starting transfers between devices: 4.41 us -> 0.09 us  [shifted(): lax.ppermute(value, axis, [(i, (i + step) % size) for i in range(size)])]
    unnamed x36 -> x34, local copies, waits for them, and re-layouts: 4.42 us -> 6.85 us
    pallas_call x1, Pallas kernels: 5.57 us -> 6.98 us  [attended_rows(): pl.pallas_call(attention_kernel, out_shape=pltpu.VMEM((SLOT, HEAD_SIZE),...]
    all_to_all x1, blocking collectives: 19.7 us -> 18.3 us  [block(): arrived = lax.all_to_all(summed, CHIPS, 0, 0, tiled=True)]
  transfers between devices with their start and end apart: 8 -> 4, of which waited for: 3 -> 3; matrix products, arithmetic and copies ran while one was open for 0% -> 0% of each run, Pallas kernels for 19% -> 21%
where the time goes in v3:
time: 109 us; the launch traced here: 108 us
  blocking collectives  42.9 us (39%)
  Pallas kernels  29.1 us (27%)
  starting transfers between devices  14.6 us (13%)
  waiting for transfers between devices  12.1 us (11%)
  local copies, waits for them, and re-layouts  7.62 us (7%)
    all_to_all x1, blocking collectives, block(): held = lax.all_to_all(copies, CHIPS, 0, 0, tiled=True)  24.6 us
    all_to_all x1, blocking collectives, block(): arrived = lax.all_to_all(summed, CHIPS, 0, 0, tiled=True)  18.3 us
    pallas_call x2, Pallas kernels, window_rows(): pl.pallas_call(functools.partial(window_kernel, begin=begin), out_shape=(...  14.2 us
    all_to_all x1, starting transfers between devices, block(): packed = lax.all_to_all(packed, GRP_SEQ, 0, 0, tiled=True)  9.94 us
    all_to_all x1, waiting for transfers between devices, block(): packed = lax.all_to_all(packed, GRP_SEQ, 0, 0, tiled=True)  8.31 us
    pallas_call x5, Pallas kernels, vmem_call(): pl.pallas_call(kernel, out_shape=tuple(((pltpu.VMEM if inner else pltpu.H...  7.91 us
    pallas_call x1, Pallas kernels, attended_rows(): pl.pallas_call(attention_kernel, out_shape=pltpu.VMEM((SLOT, HEAD_SIZE),...  6.98 us
    unnamed x34, local copies, waits for them, and re-layouts  6.85 us
  transfers between devices with their start and end apart: 4, of which 3 were waited for; matrix products, arithmetic and copies ran while one was open for 0% of the time, Pallas kernels for 21%

profile of v3, /device:TPU:0, one launch (start us, length us, event | category | flops | bytes accessed | tf_op | source)
XLA Modules:
  0.0 108.0 jit_solution(18177746659980858243)
XLA Ops:
  0.6 0.8 broadcast_in_dim.15
  1.4 24.6 %all_to_all.20.near = bf16[64,32,96]{2,1,0:T(8,128)(2,1)S(1)} all-to-all(bf16[64,32,96]{2,1,0:T(8,128)(2,1)S(1)} %broadcast_in_dim.15), channel_id=1, replica_groups=mesh['grp'=4,'seq_0'=4,'seq_1'=4,'seq_2'=2] {'grp','seq_0','seq_1'}, dimensions={0} | all-to-all | bytes 786432 | tf_op jit(solution)/shard_map/all_to_all | solution.py:517
  26.0 1.9 %collective-permute-done.far = bf16[64,32,96]{2,1,0:T(8,128)(2,1)S(1)} collective-permute-done((bf16[64,32,96]{2,1,0:T(8,128)(2,1)S(1)}, bf16[64,32,96]{2,1,0:T(8,128)(2,1)S(1)}, u32[]{:S(2)}, u32[]{:S(2)}) %collective-permute-start) | collective-permute-done | bytes 393248 | tf_op jit(solution)/shard_map/ppermute | solution.py:45
  27.9 0.8 copy-done.6
  28.7 0.8 copy-done.7
  29.5 0.7 copy-done.9
  30.2 0.7 copy-done.11
  30.9 0.7 copy-done.12
  31.6 2.5 %shard_map.248 = (bf16[4096,96]{1,0:T(8,128)(2,1)}, f32[64,96]{1,0:T(8,128)}, f32[128,4,128]{2,1,0:T(4,128)}) custom-call(bf16[64,32,96]{2,1,0:T(8,128)(2,1)S(1)} %all_to_all.20.near, bf16[64,32,96]{2,1,0:T(8,128)(2,1)S(1)} %collective-permute-done.far, f32[32,128]{1,0:T(8,128)S(1)} %bitcast.22, bf16[64,4096]{1,0:T(8,128)(2,1)} %bitcast.26, ...), custom_call_target="tpu_custom_call" | custom-call | tf_op jit(solution)/shard_map/pallas_call | solution.py:68
  34.1 4.6 %all-to-all-start.1 = ((f32[128,4,128]{2,1,0:T(4,128)}), f32[128,4,128]{2,1,0:T(4,128)S(1)}, u32[]{:S(2)}, u32[]{:S(2)}) async-start(f32[128,4,128]{2,1,0:T(4,128)} %get-tuple-element.14), calls=%async_computation.1 | async-start | bytes 524288 | tf_op jit(solution)/shard_map/all_to_all | solution.py:544
  38.7 6.0 %shard_map.249 = (bf16[1,512,256]{2,1,0:T(8,128)(2,1)}, bf16[1,512,256]{2,1,0:T(8,128)(2,1)}) custom-call(bf16[3,512,4096]{2,1,0:T(8,128)(2,1)} %cached.3, bf16[4096,256]{1,0:T(8,128)(2,1)} %w_key.5, bf16[4096,256]{1,0:T(8,128)(2,1)} %w_value.5, f32[520,128]{1,0:T(8,128)} %constant.6.clone.cosines, f32[520,128]{1,0:T(8,128)} %constant.7.clone.sines), custom_call_target="tpu_custom_call" | custom-call | tf_op jit(solution)/shard_map/pallas_call | solution.py:158
  44.7 8.2 %shard_map.250 = (bf16[2,512,256]{2,1,0:T(8,128)(2,1)}, bf16[2,512,256]{2,1,0:T(8,128)(2,1)}) custom-call(bf16[3,512,4096]{2,1,0:T(8,128)(2,1)} %cached.3, bf16[4096,256]{1,0:T(8,128)(2,1)} %w_key.5, bf16[4096,256]{1,0:T(8,128)(2,1)} %w_value.5, f32[520,128]{1,0:T(8,128)} %constant.6.clone.cosines, f32[520,128]{1,0:T(8,128)} %constant.7.clone.sines), custom_call_target="tpu_custom_call" | custom-call | tf_op jit(solution)/shard_map/pallas_call | solution.py:158
  52.9 7.0 %shard_map.251.attended = f32[16,128]{1,0:T(8,128)S(1)} custom-call(s32[96]{0:T(128)S(1)} %copy-done.13, bf16[4096,96]{1,0:T(8,128)(2,1)} %get-tuple-element.15.normed_hbm.normed, bf16[4096,512]{1,0:T(8,128)(2,1)} %w_query.1, bf16[4096,256]{1,0:T(8,128)(2,1)} %w_key.5, bf16[4096,256]{1,0:T(8,128)(2,1)} %w_value.5, ...), custom_call_target="tpu_custom_call" | custom-call | tf_op jit(solution)/shard_map/pallas_call | solution.py:378
  60.0 1.0 shard_map.252
  60.9 9.9 %all-to-all-start.2 = ((bf16[128,16,128]{2,1,0:T(8,128)(2,1)}), bf16[128,16,128]{2,1,0:T(8,128)(2,1)S(1)}, u32[]{:S(2)}, u32[]{:S(2)}) async-start(bf16[128,16,128]{2,1,0:T(8,128)(2,1)} %shard_map.252), calls=%async_computation.2 | async-start | bytes 1048576 | tf_op jit(solution)/shard_map/all_to_all | solution.py:558
  70.9 1.2 %copy-done.2 = bf16[4096,112]{0,1:T(8,128)(2,1)S(1)} copy-done((bf16[4096,112]{0,1:T(8,128)(2,1)S(1)}, bf16[4096,112]{0,1:T(8,128)(2,1)}, u32[]{:S(2)}) %copy-start.2) | copy-done | bytes 917528
  72.1 1.2 %copy-done.3 = bf16[4096,112]{0,1:T(8,128)(2,1)S(1)} copy-done((bf16[4096,112]{0,1:T(8,128)(2,1)S(1)}, bf16[4096,112]{0,1:T(8,128)(2,1)}, u32[]{:S(2)}) %copy-start.3) | copy-done | bytes 917528
  73.3 1.4 %shard_map.253 = (f32[64,96]{1,0:T(8,128)}, bf16[112,96]{1,0:T(8,128)(2,1)}) custom-call(bf16[4096,96]{1,0:T(8,128)(2,1)S(1)} %copy-done, bf16[64,4096]{1,0:T(8,128)(2,1)S(1)} %bitcast.20, bf16[112,4096]{1,0:T(8,128)(2,1)S(1)} %bitcast.17, bf16[112,4096]{1,0:T(8,128)(2,1)S(1)} %bitcast.18), custom_call_target="tpu_custom_call" | custom-call | tf_op jit(solution)/shard_map/pallas_call | solution.py:68
  74.7 0.8 copy-done.8
  75.9 8.3 %all-to-all-done.2.packed = bf16[128,16,128]{2,1,0:T(8,128)(2,1)S(1)} async-done(((bf16[128,16,128]{2,1,0:T(8,128)(2,1)}), bf16[128,16,128]{2,1,0:T(8,128)(2,1)S(1)}, u32[]{:S(2)}, u32[]{:S(2)}) %all-to-all-start.2) | async-done | bytes 524320 | tf_op jit(solution)/shard_map/all_to_all | solution.py:558
  84.2 2.6 %shard_map.255 = (f32[16,64,96]{2,1,0:T(8,128)}, bf16[64,32,96]{2,1,0:T(8,128)(2,1)S(1)}, bf16[64,32,96]{2,1,0:T(8,128)(2,1)S(1)}) custom-call(bf16[128,16,128]{2,1,0:T(8,128)(2,1)S(1)} %all-to-all-done.2.packed, bf16[64,256]{1,0:T(8,128)(2,1)} %bitcast.27, f32[16,64]{1,0:T(8,128)S(1)} %copy-done.10, f32[1,64]{1,0:T(1,128)S(1)} %bitcast.24, ...), custom_call_target="tpu_custom_call" | custom-call | tf_op jit(solution)/shard_map/pallas_call | solution.py:68
  86.9 1.9 %collective-permute-done.1 = bf16[64,32,96]{2,1,0:T(8,128)(2,1)S(1)} collective-permute-done((bf16[64,32,96]{2,1,0:T(8,128)(2,1)S(1)}, bf16[64,32,96]{2,1,0:T(8,128)(2,1)S(1)}, u32[]{:S(2)}, u32[]{:S(2)}) %collective-permute-start.1) | collective-permute-done | bytes 393248 | tf_op jit(solution)/shard_map/ppermute | solution.py:45
  89.0 18.3 %all_to_all.21 = bf16[64,32,96]{2,1,0:T(8,128)(2,1)S(1)} all-to-all(bf16[64,32,96]{2,1,0:T(8,128)(2,1)S(1)} %add_convert_fusion), channel_id=1, replica_groups=mesh['grp'=4,'seq_0'=4,'seq_1'=4,'seq_2'=2] {'grp','seq_0','seq_1'}, dimensions={0} | all-to-all | bytes 786432 | tf_op jit(solution)/shard_map/all_to_all | solution.py:582
  107.4 0.6 fusion
  (32 shorter events, 0.8 us)
Async XLA Ops:
  26.0 1.9 %collective-permute-start = (bf16[64,32,96]{2,1,0:T(8,128)(2,1)S(1)}, bf16[64,32,96]{2,1,0:T(8,128)(2,1)S(1)}, u32[]{:S(2)}, u32[]{:S(2)}) collective-permute-start(bf16[64,32,96]{2,1,0:T(8,128)(2,1)S(1)} %all_to_all.20.near), channel_id=1, source_target_pairs={{0,1},{1,0},{2,3},{3,2},{4,5},{5,4},{6,7},{7,6},{8,9},{9,8},{10,11... | collective-permute-start | bytes 1179656 | tf_op jit(solution)/shard_map/ppermute | solution.py:45
  27.9 0.8 copy-start.6
  28.7 0.8 copy-start.7
  29.5 0.7 copy-start.9
  30.2 0.7 copy-start.11
  30.9 0.7 copy-start.12
  34.1 25.8 %all-to-all-start.1 = ((f32[128,4,128]{2,1,0:T(4,128)}), f32[128,4,128]{2,1,0:T(4,128)S(1)}, u32[]{:S(2)}, u32[]{:S(2)}) async-start(f32[128,4,128]{2,1,0:T(4,128)} %get-tuple-element.14), calls=%async_computation.1 | async-start | bytes 524288 | tf_op jit(solution)/shard_map/all_to_all | solution.py:544
  44.7 8.2 %copy-start.13 = (s32[96]{0:T(128)S(1)}, s32[96]{0:T(128)}, u32[]{:S(2)}) copy-start(s32[96]{0:T(128)} %lengths.1) | copy-start | bytes 1156
  52.9 17.9 %copy-start.5 = (bf16[4096,64]{0,1:T(8,128)(2,1)S(1)}, bf16[4096,64]{0,1:T(8,128)(2,1)}, u32[]{:S(2)}) copy-start(bf16[4096,64]{0,1:T(8,128)(2,1)} %param.28) | copy-start | bytes 1572868
  59.9 10.9 %copy-start = (bf16[4096,96]{1,0:T(8,128)(2,1)S(1)}, bf16[4096,96]{1,0:T(8,128)(2,1)}, u32[]{:S(2)}) copy-start(bf16[4096,96]{1,0:T(8,128)(2,1)} %get-tuple-element.15.normed_hbm.normed) | copy-start | bytes 2359300
  60.9 13.7 %copy-start.1 = (bf16[112,4096]{1,0:T(8,128)(2,1)S(1)}, bf16[112,4096]{1,0:T(8,128)(2,1)}, u32[]{:S(2)}) copy-start(bf16[112,4096]{1,0:T(8,128)(2,1)} %w_mlp_down.1) | copy-start | bytes 2752516
  60.9 23.3 %all-to-all-start.2 = ((bf16[128,16,128]{2,1,0:T(8,128)(2,1)}), bf16[128,16,128]{2,1,0:T(8,128)(2,1)S(1)}, u32[]{:S(2)}, u32[]{:S(2)}) async-start(bf16[128,16,128]{2,1,0:T(8,128)(2,1)} %shard_map.252), calls=%async_computation.2 | async-start | bytes 1048576 | tf_op jit(solution)/shard_map/all_to_all | solution.py:558
  70.9 1.2 %copy-start.2 = (bf16[4096,112]{0,1:T(8,128)(2,1)S(1)}, bf16[4096,112]{0,1:T(8,128)(2,1)}, u32[]{:S(2)}) copy-start(bf16[4096,112]{0,1:T(8,128)(2,1)} %param.43) | copy-start | bytes 2752516
  72.1 1.2 %copy-start.3 = (bf16[4096,112]{0,1:T(8,128)(2,1)S(1)}, bf16[4096,112]{0,1:T(8,128)(2,1)}, u32[]{:S(2)}) copy-start(bf16[4096,112]{0,1:T(8,128)(2,1)} %param.44) | copy-start | bytes 2752516
  74.6 9.5 %copy-start.4 = (f32[96,16,64]{0,2,1:T(8,128)S(1)}, f32[96,16,64]{0,2,1:T(8,128)}, u32[]{:S(2)}) copy-start(f32[96,16,64]{0,2,1:T(8,128)} %param.37) | copy-start | bytes 1179652
  74.7 0.8 copy-start.8
  75.5 8.7 %copy-start.10 = (f32[16,64]{1,0:T(8,128)S(1)}, f32[16,64]{1,0:T(8,128)}, u32[]{:S(2)}) copy-start(f32[16,64]{1,0:T(8,128)} %log_decay.1) | copy-start | bytes 12292
  75.5 8.7 %copy-start.14 = (f32[64]{0:T(128)S(1)}, f32[64]{0:T(128)}, u32[]{:S(2)}) copy-start(f32[64]{0:T(128)} %param.34) | copy-start | bytes 772
  75.5 8.7 %copy-start.15 = (f32[64]{0:T(128)S(1)}, f32[64]{0:T(128)}, u32[]{:S(2)}) copy-start(f32[64]{0:T(128)} %param.36) | copy-start | bytes 772
  86.8 20.6 %copy-start.16 = (bf16[96,32]{0,1:T(8,128)(2,1)S(1)}, bf16[96,32]{0,1:T(8,128)(2,1)}, u32[]{:S(2)}) copy-start(bf16[96,32]{0,1:T(8,128)(2,1)} %param.25) | copy-start | bytes 18436
  86.8 2.0 %collective-permute-start.1 = (bf16[64,32,96]{2,1,0:T(8,128)(2,1)S(1)}, bf16[64,32,96]{2,1,0:T(8,128)(2,1)S(1)}, u32[]{:S(2)}, u32[]{:S(2)}) collective-permute-start(bf16[64,32,96]{2,1,0:T(8,128)(2,1)S(1)} %get-tuple-element.24), channel_id=1, source_target_pairs={{0,1},{1,0},{2,3},{3,2},{4,5},{5,4},{6,7},{7,6},{8,9},{9,8},{10,11... | collective-permute-start | bytes 1179656 | tf_op jit(solution)/shard_map/ppermute | solution.py:45

commit v4 on v2

--- a/solution.py
+++ b/solution.py
@@ -1,3 +1,5 @@
+import functools
+
 import jax
 import jax.numpy as jnp
 import numpy as np
@@ -23,6 +25,9 @@
 ROWS = 144
 SLOT = 16
 WEIGHT_PIECES = 4
+WINDOW_SIZES = (256, 384, 512)
+MAIN = 112
+TAIL = 32
 
 
 def rotary_tables(count):
@@ -86,8 +91,9 @@
 
 
 def window_kernel(
-    lengths, cached, w_key, w_value, cosines, sines, key_out, value_out,
-    rows, weights, cos, sin, turned, plain, row_sem, first_sem, key_sem, value_sem, table_sem, out_sem,
+    lengths_hbm, cached, w_key, w_value, cosines, sines, key_out, value_out,
+    rows, weights, cos, sin, turned, plain, lengths,
+    row_sem, first_sem, key_sem, value_sem, table_sem, out_sem, length_sem,
 ):
     seqs, window, width = cached.shape
     columns = w_key.shape[1]
@@ -114,6 +120,8 @@
     later = [
         pltpu.make_async_copy(cached.at[b], rows.at[b], row_sem.at[b]) for b in range(1, seqs)
     ]
+    fetch = pltpu.make_async_copy(lengths_hbm, lengths, length_sem)
+    fetch.start()
     for p in range(pieces):
         for copy in piece_copies(p):
             copy.start()
@@ -121,15 +129,33 @@
         copy.start()
     for copy in later:
         copy.start()
+    fetch.wait()
 
     def finish(b, both):
+        live = both.shape[0]
         for head in range(columns // HEAD_SIZE):
             lanes = slice(head * HEAD_SIZE, (head + 1) * HEAD_SIZE)
             part = both[:, lanes]
-            turned[b, :, lanes] = (
-                part * cos[...] + pltpu.roll(part, HEAD_SIZE // 2, 1) * sin[...]
+            turned[b, 0:live, lanes] = (
+                part * cos[0:live, :] + pltpu.roll(part, HEAD_SIZE // 2, 1) * sin[0:live, :]
             ).astype(BF16)
-        plain[b] = both[:, columns:].astype(BF16)
+        plain[b, 0:live, :] = both[:, columns:].astype(BF16)
+        if live < window:
+            turned[b, live:, :] = jnp.zeros((window - live, columns), BF16)
+            plain[b, live:, :] = jnp.zeros((window - live, columns), BF16)
+
+    def by_length(b, work):
+        length = lengths[first + b]
+        low = 0
+        for size in WINDOW_SIZES:
+            if size == WINDOW_SIZES[0]:
+                chosen = length <= size
+            elif size == WINDOW_SIZES[-1]:
+                chosen = length > low
+            else:
+                chosen = (length > low) & (length <= size)
+            pl.when(chosen)(functools.partial(work, size))
+            low = size
 
     def out_copies(b):
         return (
@@ -137,21 +163,31 @@
             pltpu.make_async_copy(plain.at[b], value_out.at[b], out_sem.at[1, b]),
         )
 
-    total = None
-    for p in range(pieces):
-        for copy in piece_copies(p):
-            copy.wait()
-        span = slice(p * step, (p + 1) * step)
-        part = dot(rows[0, :, span], weights[span, :])
-        total = part if total is None else total + part
     for copy in tables:
         copy.wait()
-    finish(0, total)
+
+    def first_rows(size):
+        total = None
+        for p in range(pieces):
+            for copy in piece_copies(p):
+                copy.wait()
+            span = slice(p * step, (p + 1) * step)
+            part = dot(rows[0, 0:size, span], weights[span, :])
+            total = part if total is None else total + part
+        finish(0, total)
+
+    by_length(0, first_rows)
     for copy in out_copies(0):
         copy.start()
+    for copy in later:
+        copy.wait()
+
+    def later_rows(b, carry):
+        by_length(b, lambda size: finish(b, dot(rows[b, 0:size, :], weights[...])))
+        return carry
+
+    lax.fori_loop(1, seqs, later_rows, 0)
     for b in range(1, seqs):
-        later[b - 1].wait()
-        finish(b, dot(rows[b], weights[...]))
         for copy in out_copies(b):
             copy.start()
     for b in range(seqs):
@@ -168,7 +204,7 @@
     return pl.pallas_call(
         window_kernel,
         out_shape=(out, out),
-        in_specs=[pl.BlockSpec(memory_space=pltpu.SMEM)] + [anywhere] * 5,
+        in_specs=[anywhere] * 6,
         out_specs=(anywhere, anywhere),
         scratch_shapes=[
             pltpu.VMEM((seqs, window, width), BF16),
@@ -177,15 +213,17 @@
             pltpu.VMEM((window, HEAD_SIZE), F32),
             pltpu.VMEM((seqs, window, columns), BF16),
             pltpu.VMEM((seqs, window, columns), BF16),
+            pltpu.SMEM(lengths.shape, jnp.int32),
             dma((seqs,)),
             dma((WEIGHT_PIECES,)),
             dma((WEIGHT_PIECES,)),
             dma((WEIGHT_PIECES,)),
             dma((2,)),
             dma((2, seqs)),
+            dma,
         ],
         compiler_params=pltpu.CompilerParams(vmem_limit_bytes=40 << 20),
-    )(lengths, *(in_hbm(v) for v in (cached, w_key, w_value, cosines, sines)))
+    )(*(in_hbm(v) for v in (lengths, cached, w_key, w_value, cosines, sines)))
 
 
 def inner_kernel(
@@ -240,9 +278,11 @@
 
 
 def attention_kernel(
-    lengths, normed, w_query, w_key, w_value, key_rows, value_rows, cosines, sines, out,
-    weights, keys, values, cos_rows, sin_rows, weight_sem, row_sem, table_sem,
+    lengths_hbm, normed, w_query, w_key, w_value, key_rows, value_rows, cosines, sines, out,
+    weights, keys, values, cos_rows, sin_rows, lengths, weight_sem, row_sem, table_sem, length_sem,
 ):
+    fetch = pltpu.make_async_copy(lengths_hbm, lengths, length_sem)
+    fetch.start()
     seqs, window = keys.shape[0], keys.shape[1]
     columns = keys.shape[2]
     queries = w_query.shape[1]
@@ -273,6 +313,12 @@
         pltpu.make_async_copy(key_rows, keys, row_sem.at[0]),
         pltpu.make_async_copy(value_rows, values, row_sem.at[1]),
     )
+    for p in range(pieces):
+        for copy in piece_copies(p):
+            copy.start()
+    for copy in row_copies:
+        copy.start()
+    fetch.wait()
     table_copies = []
     for b in range(seqs):
         at = pl.ds(lengths[first + b], 1)
@@ -282,10 +328,7 @@
         table_copies.append(
             pltpu.make_async_copy(sines.at[at], sin_rows.at[pl.ds(b, 1)], table_sem.at[1, b])
         )
-    for p in range(pieces):
-        for copy in piece_copies(p):
-            copy.start()
-    for copy in (*table_copies, *row_copies):
+    for copy in table_copies:
         copy.start()
     row = lax.broadcasted_iota(jnp.int32, (8, batch), 0)
     column = lax.broadcasted_iota(jnp.int32, (8, batch), 1)
@@ -375,7 +418,7 @@
     return pl.pallas_call(
         attention_kernel,
         out_shape=pltpu.VMEM((SLOT, HEAD_SIZE), F32),
-        in_specs=[pl.BlockSpec(memory_space=pltpu.SMEM), vmem] + [anywhere] * 7,
+        in_specs=[anywhere, vmem] + [anywhere] * 7,
         out_specs=vmem,
         scratch_shapes=[
             pltpu.VMEM((width, w_query.shape[1] + 2 * w_key.shape[1]), BF16),
@@ -383,33 +426,46 @@
             pltpu.VMEM(values.shape, BF16),
             pltpu.VMEM((8, HEAD_SIZE), F32),
             pltpu.VMEM((8, HEAD_SIZE), F32),
+            pltpu.SMEM(lengths.shape, jnp.int32),
             dma((3, WEIGHT_PIECES)),
             dma((2,)),
             dma((2, keys.shape[0])),
+            dma,
         ],
         compiler_params=pltpu.CompilerParams(vmem_limit_bytes=20 << 20),
     )(
-        lengths,
+        in_hbm(lengths),
         in_vmem(normed),
         *(in_hbm(v) for v in (w_query, w_key, w_value, keys, values, cosines, sines)),
     )
 
 
 def pack_kernel(s0, s1, s2, s3, attended, out):
-    low = ((s0[...] + s1[...]) + (s2[...] + s3[...])).astype(BF16)
+    low = (s0[...] + s1[...]) + (s2[...] + s3[...])
+    tail = low[MAIN:, :]
+    moved = [pltpu.roll(tail, 96 - TAIL * p, 1) for p in range(3)]
+    moved.append(jnp.zeros((MAIN - 3 * TAIL, HEAD_SIZE), F32))
+    lane = lax.broadcasted_iota(jnp.int32, (MAIN, HEAD_SIZE), 1)
+    low = jnp.where(lane < 96, low[0:MAIN, :], jnp.concatenate(moved, axis=0)).astype(BF16)
     rows = attended[...].astype(BF16)
     for k in range(out.shape[0]):
-        out[k, 0:ROWS, :] = low
-        out[k, ROWS:, :] = rows
+        out[k, 0:MAIN, :] = low
+        out[k, MAIN:, :] = rows
 
 
 def combine_kernel(arrived, low_out, rows_out):
-    total = arrived[0, 0:ROWS, :].astype(F32)
-    rows_out[0:SLOT, :] = arrived[0, ROWS:, :]
+    total = arrived[0, 0:MAIN, :].astype(F32)
+    rows_out[0:SLOT, :] = arrived[0, MAIN:, :]
     for k in range(1, arrived.shape[0]):
-        total = total + arrived[k, 0:ROWS, :].astype(F32)
-        rows_out[k * SLOT : (k + 1) * SLOT, :] = arrived[k, ROWS:, :]
-    low_out[...] = total
+        total = total + arrived[k, 0:MAIN, :].astype(F32)
+        rows_out[k * SLOT : (k + 1) * SLOT, :] = arrived[k, MAIN:, :]
+    low_out[0:MAIN, :] = total
+    lane = lax.broadcasted_iota(jnp.int32, (TAIL, HEAD_SIZE), 1)
+    tail = jnp.zeros((TAIL, HEAD_SIZE), F32)
+    for p in range(3):
+        back = pltpu.roll(total[TAIL * p : TAIL * (p + 1), :], HEAD_SIZE - 96 + TAIL * p, 1)
+        tail = jnp.where(lane // TAIL == p, back, tail)
+    low_out[MAIN:, :] = tail
 
 
 def outer_kernel(
@@ -542,7 +598,7 @@
     )
     (term,) = vmem_call(down_kernel, (((batch, width), F32, True),), (act, w_mlp_down))
     (packed,) = vmem_call(
-        pack_kernel, (((16, ROWS + SLOT, HEAD_SIZE), BF16, True),), (*arrived, attended)
+        pack_kernel, (((16, MAIN + SLOT, HEAD_SIZE), BF16, True),), (*arrived, attended)
     )
     packed = lax.all_to_all(packed, PLANE, 0, 0, tiled=True)
     near_low, near_rows = vmem_call(

time: 99 us -> 96.6 us (0.976)
  Pallas kernels: 22.1 us -> 20.8 us
  blocking collectives: 60.3 us -> 59.3 us
    unnamed x36 -> x34, local copies, waits for them, and re-layouts: 4.42 us -> 4.42 us
  transfers between devices with their start and end apart: 8 -> 8, of which waited for: 3 -> 3; matrix products, arithmetic and copies ran while one was open for 0% -> 0% of each run, Pallas kernels for 19% -> 18%
where the time goes in v4:
time: 96.6 us; the launch traced here: 96.1 us
  blocking collectives  59.3 us (61%)
  Pallas kernels  20.8 us (22%)
  local copies, waits for them, and re-layouts  5.19 us (5%)
  waiting for transfers between devices  4.88 us (5%)
  starting transfers between devices  4.21 us (4%)
    all_to_all x1, blocking collectives, block(): held = lax.all_to_all(copies, CHIPS, 0, 0, tiled=True)  24.6 us
    all_to_all x1, blocking collectives, block(): arrived = lax.all_to_all(summed, CHIPS, 0, 0, tiled=True)  19.1 us
    all_to_all x1, blocking collectives, block(): packed = lax.all_to_all(packed, PLANE, 0, 0, tiled=True)  15.6 us
    pallas_call x1, Pallas kernels, window_rows(): pl.pallas_call(window_kernel, out_shape=(out, out), in_specs=[anywhere] *...  11.4 us
    ppermute x8, waiting for transfers between devices, shifted(): lax.ppermute(value, axis, [(i, (i + step) % size) for i in range(size)])  4.88 us
    pallas_call x1, Pallas kernels, attended_rows(): pl.pallas_call(attention_kernel, out_shape=pltpu.VMEM((SLOT, HEAD_SIZE),...  4.77 us
    pallas_call x6, Pallas kernels, vmem_call(): pl.pallas_call(kernel, out_shape=tuple((pltpu.VMEM(shape, dtype) if inner...  4.68 us
    unnamed x34, local copies, waits for them, and re-layouts  4.42 us
  transfers between devices with their start and end apart: 8, of which 3 were waited for; matrix products, arithmetic and copies ran while one was open for 0% of the time, Pallas kernels for 18%

profile of v4, /device:TPU:0, one launch (start us, length us, event | category | flops | bytes accessed | tf_op | source)
XLA Modules:
  0.0 96.1 jit_solution(1891387990759454474)
XLA Ops:
  0.6 0.8 broadcast_in_dim.15
  1.4 24.6 %all_to_all.15.near = bf16[64,32,96]{2,1,0:T(8,128)(2,1)S(1)} all-to-all(bf16[64,32,96]{2,1,0:T(8,128)(2,1)S(1)} %broadcast_in_dim.15), channel_id=1, replica_groups=mesh['grp'=4,'seq_0'=4,'seq_1'=4,'seq_2'=2] {'grp','seq_0','seq_1'}, dimensions={0} | all-to-all | bytes 786432 | tf_op jit(solution)/shard_map/all_to_all | solution.py:566
  26.0 1.9 %collective-permute-done.far = bf16[64,32,96]{2,1,0:T(8,128)(2,1)S(1)} collective-permute-done((bf16[64,32,96]{2,1,0:T(8,128)(2,1)S(1)}, bf16[64,32,96]{2,1,0:T(8,128)(2,1)S(1)}, u32[]{:S(2)}, u32[]{:S(2)}) %collective-permute-start) | collective-permute-done | bytes 393248 | tf_op jit(solution)/shard_map/ppermute | solution.py:49
  27.9 0.8 copy-done.7
  28.7 0.8 copy-done.8
  29.5 0.7 copy-done.10
  30.2 0.7 copy-done.12
  30.9 0.7 copy-done.13
  31.6 1.5 %shard_map.248 = (bf16[4096,96]{1,0:T(8,128)(2,1)S(1)}, f32[64,96]{1,0:T(8,128)S(1)}, f32[2,144,128]{2,1,0:T(8,128)S(1)}) custom-call(bf16[64,32,96]{2,1,0:T(8,128)(2,1)S(1)} %all_to_all.15.near, bf16[64,32,96]{2,1,0:T(8,128)(2,1)S(1)} %collective-permute-done.far, f32[32,128]{1,0:T(8,128)S(1)} %bitcast.27, bf16[64,4096]{1,0:T(8,128)(2,1)} %bitcast.31, ...), custom_call_target="tpu_custom_call" | custom-call | tf_op jit(solution)/shard_map/pallas_call | solution.py:83
  33.3 1.1 %collective-permute-done.1 = f32[144,128]{1,0:T(8,128)S(1)} collective-permute-done((f32[144,128]{1,0:T(8,128)S(1)}, f32[144,128]{1,0:T(8,128)S(1)}, u32[]{:S(2)}, u32[]{:S(2)}) %collective-permute-start.1) | collective-permute-done | bytes 73760 | tf_op jit(solution)/shard_map/ppermute | solution.py:49
  34.5 0.2 collective-permute-start.2
  34.7 2.1 %collective-permute-start.3 = (f32[144,128]{1,0:T(8,128)S(1)}, f32[144,128]{1,0:T(8,128)S(1)}, u32[]{:S(2)}, u32[]{:S(2)}) collective-permute-start(f32[144,128]{1,0:T(8,128)S(1)} %bitcast_add_fusion.s0), channel_id=1, source_target_pairs={{0,64},{32,96},{64,0},{96,32},{1,65},{33,97},{65,1},{97,33},{2,66}... | collective-permute-start | bytes 221192 | tf_op jit(solution)/shard_map/ppermute | solution.py:49
  36.8 1.1 %collective-permute-start.4 = (f32[144,128]{1,0:T(8,128)S(1)}, f32[144,128]{1,0:T(8,128)S(1)}, u32[]{:S(2)}, u32[]{:S(2)}) collective-permute-start(f32[144,128]{1,0:T(8,128)S(1)} %bitcast_add_fusion.s0), channel_id=1, source_target_pairs={{0,96},{32,0},{64,32},{96,64},{1,97},{33,1},{65,33},{97,65},{2,98}... | collective-permute-start | bytes 221192 | tf_op jit(solution)/shard_map/ppermute | solution.py:49
  37.8 11.4 %shard_map.249 = (bf16[3,512,256]{2,1,0:T(8,128)(2,1)}, bf16[3,512,256]{2,1,0:T(8,128)(2,1)}) custom-call(s32[96]{0:T(128)} %lengths_hbm.3, bf16[3,512,4096]{2,1,0:T(8,128)(2,1)} %cached.1, bf16[4096,256]{1,0:T(8,128)(2,1)} %w_key.3, bf16[4096,256]{1,0:T(8,128)(2,1)} %w_value.3, f32[520,128]{1,0:T(8,128)} %constant.6.clone.cosines, ...), custom_call_target="tpu_custom_call" | custom-call | tf_op jit(solution)/shard_map/pallas_call | solution.py:204
  49.2 4.8 %shard_map.250.attended = f32[16,128]{1,0:T(8,128)S(1)} custom-call(s32[96]{0:T(128)} %lengths_hbm.3, bf16[4096,96]{1,0:T(8,128)(2,1)S(1)} %get-tuple-element.15.normed, bf16[4096,512]{1,0:T(8,128)(2,1)} %w_query.1, bf16[4096,256]{1,0:T(8,128)(2,1)} %w_key.3, bf16[4096,256]{1,0:T(8,128)(2,1)} %w_value.3, bf16[3,512,256]{2,1,0:T(8,128)(2,1)} %get-tuple-element.16.key_rows, ...), custom_call_target="tpu_custom_call" | custom-call | tf_op jit(solution)/shard_map/pallas_call | solution.py:418
  54.2 15.6 %all_to_all.16.arrived = bf16[16,128,128]{2,1,0:T(8,128)(2,1)S(1)} all-to-all(bf16[16,128,128]{2,1,0:T(8,128)(2,1)S(1)} %shard_map.251), channel_id=1, replica_groups=mesh['grp'=4,'seq_0'=4,'seq_1'=4,'seq_2'=2] {'seq_0','seq_1'}, dimensions={0} | all-to-all | bytes 1048576 | tf_op jit(solution)/shard_map/all_to_all | solution.py:603
  70.0 0.5 collective-permute-start.6
  70.5 0.8 shard_map.253
  71.4 0.4 shard_map.254.term
  71.8 0.5 copy-done.4
  72.5 1.7 %shard_map.255 = (f32[16,64,96]{2,1,0:T(8,128)}, bf16[64,32,96]{2,1,0:T(8,128)(2,1)S(1)}, bf16[64,32,96]{2,1,0:T(8,128)(2,1)S(1)}) custom-call(f32[144,128]{1,0:T(8,128)S(1)} %get-tuple-element.18.near, f32[144,128]{1,0:T(8,128)S(1)} %collective-permute-done.5.far, bf16[256,128]{1,0:T(8,128)(2,1)S(1)} %get-tuple-element.19.near_rows, ...), custom_call_target="tpu_custom_call" | custom-call | tf_op jit(solution)/shard_map/pallas_call | solution.py:83
  74.3 1.8 %collective-permute-done.7 = bf16[64,32,96]{2,1,0:T(8,128)(2,1)S(1)} collective-permute-done((bf16[64,32,96]{2,1,0:T(8,128)(2,1)S(1)}, bf16[64,32,96]{2,1,0:T(8,128)(2,1)S(1)}, u32[]{:S(2)}, u32[]{:S(2)}) %collective-permute-start.7) | collective-permute-done | bytes 393248 | tf_op jit(solution)/shard_map/ppermute | solution.py:49
  76.3 19.1 %all_to_all.17 = bf16[64,32,96]{2,1,0:T(8,128)(2,1)S(1)} all-to-all(bf16[64,32,96]{2,1,0:T(8,128)(2,1)S(1)} %add_convert_fusion), channel_id=1, replica_groups=mesh['grp'=4,'seq_0'=4,'seq_1'=4,'seq_2'=2] {'grp','seq_0','seq_1'}, dimensions={0} | all-to-all | bytes 786432 | tf_op jit(solution)/shard_map/all_to_all | solution.py:624
  95.5 0.6 fusion
  (43 shorter events, 1.2 us)
Async XLA Ops:
  26.0 1.9 %collective-permute-start = (bf16[64,32,96]{2,1,0:T(8,128)(2,1)S(1)}, bf16[64,32,96]{2,1,0:T(8,128)(2,1)S(1)}, u32[]{:S(2)}, u32[]{:S(2)}) collective-permute-start(bf16[64,32,96]{2,1,0:T(8,128)(2,1)S(1)} %all_to_all.15.near), channel_id=1, source_target_pairs={{0,1},{1,0},{2,3},{3,2},{4,5},{5,4},{6,7},{7,6},{8,9},{9,8},{10,11... | collective-permute-start | bytes 1179656 | tf_op jit(solution)/shard_map/ppermute | solution.py:49
  27.9 0.8 copy-start.7
  28.7 0.8 copy-start.8
  29.5 0.7 copy-start.10
  30.2 0.7 copy-start.12
  33.1 1.3 %collective-permute-start.1 = (f32[144,128]{1,0:T(8,128)S(1)}, f32[144,128]{1,0:T(8,128)S(1)}, u32[]{:S(2)}, u32[]{:S(2)}) collective-permute-start(f32[144,128]{1,0:T(8,128)S(1)} %slice_bitcast_fusion), channel_id=1, source_target_pairs={{0,1},{1,0},{2,3},{3,2},{4,5},{5,4},{6,7},{7,6},{8,9},{9,8},{10,11... | collective-permute-start | bytes 221192 | tf_op jit(solution)/shard_map/ppermute | solution.py:49
  34.5 19.5 %collective-permute-start.2 = (f32[144,128]{1,0:T(8,128)S(1)}, f32[144,128]{1,0:T(8,128)S(1)}, u32[]{:S(2)}, u32[]{:S(2)}) collective-permute-start(f32[144,128]{1,0:T(8,128)S(1)} %bitcast_add_fusion.s0), channel_id=1, source_target_pairs={{0,32},{32,64},{64,96},{96,0},{1,33},{33,65},{65,97},{97,1},{2,34}... | collective-permute-start | bytes 221192 | tf_op jit(solution)/shard_map/ppermute | solution.py:49
  34.7 19.3 %collective-permute-start.3 = (f32[144,128]{1,0:T(8,128)S(1)}, f32[144,128]{1,0:T(8,128)S(1)}, u32[]{:S(2)}, u32[]{:S(2)}) collective-permute-start(f32[144,128]{1,0:T(8,128)S(1)} %bitcast_add_fusion.s0), channel_id=1, source_target_pairs={{0,64},{32,96},{64,0},{96,32},{1,65},{33,97},{65,1},{97,33},{2,66}... | collective-permute-start | bytes 221192 | tf_op jit(solution)/shard_map/ppermute | solution.py:49
  36.8 17.3 %collective-permute-start.4 = (f32[144,128]{1,0:T(8,128)S(1)}, f32[144,128]{1,0:T(8,128)S(1)}, u32[]{:S(2)}, u32[]{:S(2)}) collective-permute-start(f32[144,128]{1,0:T(8,128)S(1)} %bitcast_add_fusion.s0), channel_id=1, source_target_pairs={{0,96},{32,0},{64,32},{96,64},{1,97},{33,1},{65,33},{97,65},{2,98}... | collective-permute-start | bytes 221192 | tf_op jit(solution)/shard_map/ppermute | solution.py:49
  54.0 16.5 %copy-start.1 = (bf16[4096,112]{0,1:T(8,128)(2,1)S(1)}, bf16[4096,112]{0,1:T(8,128)(2,1)}, u32[]{:S(2)}) copy-start(bf16[4096,112]{0,1:T(8,128)(2,1)} %param.43) | copy-start | bytes 2752516
  54.0 16.5 %copy-start.2 = (bf16[4096,112]{0,1:T(8,128)(2,1)S(1)}, bf16[4096,112]{0,1:T(8,128)(2,1)}, u32[]{:S(2)}) copy-start(bf16[4096,112]{0,1:T(8,128)(2,1)} %param.44) | copy-start | bytes 2752516
  54.0 16.5 %copy-start.3 = (bf16[4096,64]{0,1:T(8,128)(2,1)S(1)}, bf16[4096,64]{0,1:T(8,128)(2,1)}, u32[]{:S(2)}) copy-start(bf16[4096,64]{0,1:T(8,128)(2,1)} %param.28) | copy-start | bytes 1572868
  69.8 1.6 %copy-start = (bf16[112,4096]{1,0:T(8,128)(2,1)S(1)}, bf16[112,4096]{1,0:T(8,128)(2,1)}, u32[]{:S(2)}) copy-start(bf16[112,4096]{1,0:T(8,128)(2,1)} %w_mlp_down.1) | copy-start | bytes 2752516
  69.9 1.9 %collective-permute-start.5 = (f32[144,128]{1,0:T(8,128)S(1)}, f32[144,128]{1,0:T(8,128)S(1)}, u32[]{:S(2)}, u32[]{:S(2)}) collective-permute-start(f32[144,128]{1,0:T(8,128)S(1)} %get-tuple-element.18.near), channel_id=1, source_target_pairs={{0,1},{1,0},{2,3},{3,2},{4,5},{5,4},{6,7},{7,6},{8,9},{9,8},{10,11... | collective-permute-start | bytes 221192 | tf_op jit(solution)/shard_map/ppermute | solution.py:49
  70.0 1.8 %collective-permute-start.6 = (bf16[256,128]{1,0:T(8,128)(2,1)S(1)}, bf16[256,128]{1,0:T(8,128)(2,1)S(1)}, u32[]{:S(2)}, u32[]{:S(2)}) collective-permute-start(bf16[256,128]{1,0:T(8,128)(2,1)S(1)} %get-tuple-element.19.near_rows), channel_id=1, source_target_pairs={{0,1},{1,0},{2,3},{3,2},{4,5},{5,4},{6,7},{7,6},{8,9},{9,8},{10,11... | collective-permute-start | bytes 196616 | tf_op jit(solution)/shard_map/ppermute | solution.py:49
  71.3 1.0 %copy-start.4 = (f32[96,16,64]{0,2,1:T(8,128)S(1)}, f32[96,16,64]{0,2,1:T(8,128)}, u32[]{:S(2)}) copy-start(f32[96,16,64]{0,2,1:T(8,128)} %param.37) | copy-start | bytes 1179652
  71.3 1.2 %copy-start.5 = (bf16[64,4096]{1,0:T(8,128)(2,1)S(1)}, bf16[64,4096]{1,0:T(8,128)(2,1)}, u32[]{:S(2)}) copy-start(bf16[64,4096]{1,0:T(8,128)(2,1)} %w_out.1) | copy-start | bytes 1572868
  71.3 1.2 %copy-start.6 = (bf16[512,128]{1,0:T(8,128)(2,1)S(1)}, bf16[512,128]{1,0:T(8,128)(2,1)}, u32[]{:S(2)}) copy-start(bf16[512,128]{1,0:T(8,128)(2,1)} %w_attn.1) | copy-start | bytes 393220
  71.3 1.2 %copy-start.9 = (bf16[256,64]{0,1:T(8,128)(2,1)S(1)}, bf16[256,64]{0,1:T(8,128)(2,1)}, u32[]{:S(2)}) copy-start(bf16[256,64]{0,1:T(8,128)(2,1)} %param.33) | copy-start | bytes 98308
  71.3 1.2 %copy-start.11 = (f32[16,64]{1,0:T(8,128)S(1)}, f32[16,64]{1,0:T(8,128)}, u32[]{:S(2)}) copy-start(f32[16,64]{1,0:T(8,128)} %log_decay.1) | copy-start | bytes 12292
  71.3 1.2 %copy-start.14 = (f32[64]{0:T(128)S(1)}, f32[64]{0:T(128)}, u32[]{:S(2)}) copy-start(f32[64]{0:T(128)} %param.34) | copy-start | bytes 772
  71.4 1.2 %copy-start.15 = (f32[64]{0:T(128)S(1)}, f32[64]{0:T(128)}, u32[]{:S(2)}) copy-start(f32[64]{0:T(128)} %param.36) | copy-start | bytes 772
  74.2 21.3 %copy-start.16 = (bf16[96,32]{0,1:T(8,128)(2,1)S(1)}, bf16[96,32]{0,1:T(8,128)(2,1)}, u32[]{:S(2)}) copy-start(bf16[96,32]{0,1:T(8,128)(2,1)} %param.25) | copy-start | bytes 18436
  74.2 1.9 %collective-permute-start.7 = (bf16[64,32,96]{2,1,0:T(8,128)(2,1)S(1)}, bf16[64,32,96]{2,1,0:T(8,128)(2,1)S(1)}, u32[]{:S(2)}, u32[]{:S(2)}) collective-permute-start(bf16[64,32,96]{2,1,0:T(8,128)(2,1)S(1)} %get-tuple-element.24), channel_id=1, source_target_pairs={{0,1},{1,0},{2,3},{3,2},{4,5},{5,4},{6,7},{7,6},{8,9},{9,8},{10,11... | collective-permute-start | bytes 1179656 | tf_op jit(solution)/shard_map/ppermute | solution.py:49
  (1 other events, 0.7 us)

commit v5 on v4

--- a/solution.py
+++ b/solution.py
@@ -27,6 +27,7 @@
 WEIGHT_PIECES = 4
 WINDOW_SIZES = (256, 384, 512)
 MAIN = 112
+COST = 8_000_000_000
 TAIL = 32
 
 
@@ -77,7 +78,7 @@
     return pltpu.with_memory_space_constraint(value, pltpu.VMEM)
 
 
-def vmem_call(kernel, outs, operands, fetched=(), scratch=(), limit=12 << 20):
+def vmem_call(kernel, outs, operands, fetched=(), scratch=(), limit=12 << 20, cost=None):
     vmem = pl.BlockSpec(memory_space=pltpu.VMEM)
     anywhere = pl.BlockSpec(memory_space=pl.ANY)
     return pl.pallas_call(
@@ -87,6 +88,7 @@
         out_specs=tuple(vmem for _ in outs),
         scratch_shapes=list(scratch),
         compiler_params=pltpu.CompilerParams(vmem_limit_bytes=limit),
+        cost_estimate=cost,
     )(*((in_hbm if k in fetched else in_vmem)(v) for k, v in enumerate(operands)))
 
 
@@ -163,9 +165,6 @@
             pltpu.make_async_copy(plain.at[b], value_out.at[b], out_sem.at[1, b]),
         )
 
-    for copy in tables:
-        copy.wait()
-
     def first_rows(size):
         total = None
         for p in range(pieces):
@@ -174,6 +173,8 @@
             span = slice(p * step, (p + 1) * step)
             part = dot(rows[0, 0:size, span], weights[span, :])
             total = part if total is None else total + part
+        for copy in tables:
+            copy.wait()
         finish(0, total)
 
     by_length(0, first_rows)
@@ -184,12 +185,11 @@
 
     def later_rows(b, carry):
         by_length(b, lambda size: finish(b, dot(rows[b, 0:size, :], weights[...])))
-        return carry
-
-    lax.fori_loop(1, seqs, later_rows, 0)
-    for b in range(1, seqs):
         for copy in out_copies(b):
             copy.start()
+        return carry
+
+    lax.fori_loop(1, seqs, later_rows, 0)
     for b in range(seqs):
         for copy in out_copies(b):
             copy.wait()
@@ -279,7 +279,7 @@
 
 def attention_kernel(
     lengths_hbm, normed, w_query, w_key, w_value, key_rows, value_rows, cosines, sines, out,
-    weights, keys, values, cos_rows, sin_rows, lengths, weight_sem, row_sem, table_sem, length_sem,
+    keys, values, cos_rows, sin_rows, lengths, row_sem, table_sem, length_sem,
 ):
     fetch = pltpu.make_async_copy(lengths_hbm, lengths, length_sem)
     fetch.start()
@@ -288,34 +288,12 @@
     queries = w_query.shape[1]
     kv_heads = columns // HEAD_SIZE
     group = queries // columns
-    width, batch = normed.shape
+    batch = normed.shape[1]
     first = own_seq() * seqs
-    pieces = WEIGHT_PIECES
-    step = width // pieces
-
-    def piece_copies(p):
-        span = pl.ds(p * step, step)
-        return (
-            pltpu.make_async_copy(
-                w_query.at[span], weights.at[span, pl.ds(0, queries)], weight_sem.at[0, p]
-            ),
-            pltpu.make_async_copy(
-                w_key.at[span], weights.at[span, pl.ds(queries, columns)], weight_sem.at[1, p]
-            ),
-            pltpu.make_async_copy(
-                w_value.at[span],
-                weights.at[span, pl.ds(queries + columns, columns)],
-                weight_sem.at[2, p],
-            ),
-        )
-
     row_copies = (
         pltpu.make_async_copy(key_rows, keys, row_sem.at[0]),
         pltpu.make_async_copy(value_rows, values, row_sem.at[1]),
     )
-    for p in range(pieces):
-        for copy in piece_copies(p):
-            copy.start()
     for copy in row_copies:
         copy.start()
     fetch.wait()
@@ -334,16 +312,9 @@
     column = lax.broadcasted_iota(jnp.int32, (8, batch), 1)
     pick = jnp.where((column == first + row) & (row < seqs), 1.0, 0.0).astype(BF16)
     own = lax.dot_general(pick, normed[...], NT, preferred_element_type=F32).astype(BF16)
-    projected = None
-    for p in range(pieces):
-        for copy in piece_copies(p):
-            copy.wait()
-        span = slice(p * step, (p + 1) * step)
-        part = dot(own[:, span], weights[span, :])
-        projected = part if projected is None else projected + part
-    query = projected[:, 0:queries]
-    fresh_key = projected[:, queries : queries + columns]
-    fresh_value = projected[:, queries + columns :].astype(BF16).astype(F32)
+    query = dot(own, w_query[...])
+    fresh_key = dot(own, w_key[...])
+    fresh_value = dot(own, w_value[...]).astype(BF16).astype(F32)
     for copy in (*table_copies, *row_copies):
         copy.wait()
     scale = HEAD_SIZE ** (-0.5)
@@ -414,29 +385,26 @@
     anywhere = pl.BlockSpec(memory_space=pl.ANY)
     vmem = pl.BlockSpec(memory_space=pltpu.VMEM)
     dma = pltpu.SemaphoreType.DMA
-    width = normed.shape[0]
     return pl.pallas_call(
         attention_kernel,
         out_shape=pltpu.VMEM((SLOT, HEAD_SIZE), F32),
-        in_specs=[anywhere, vmem] + [anywhere] * 7,
+        in_specs=[anywhere] + [vmem] * 4 + [anywhere] * 4,
         out_specs=vmem,
         scratch_shapes=[
-            pltpu.VMEM((width, w_query.shape[1] + 2 * w_key.shape[1]), BF16),
             pltpu.VMEM(keys.shape, BF16),
             pltpu.VMEM(values.shape, BF16),
             pltpu.VMEM((8, HEAD_SIZE), F32),
             pltpu.VMEM((8, HEAD_SIZE), F32),
             pltpu.SMEM(lengths.shape, jnp.int32),
-            dma((3, WEIGHT_PIECES)),
             dma((2,)),
             dma((2, keys.shape[0])),
             dma,
         ],
-        compiler_params=pltpu.CompilerParams(vmem_limit_bytes=20 << 20),
+        compiler_params=pltpu.CompilerParams(vmem_limit_bytes=12 << 20),
     )(
         in_hbm(lengths),
-        in_vmem(normed),
-        *(in_hbm(v) for v in (w_query, w_key, w_value, keys, values, cosines, sines)),
+        *(in_vmem(v) for v in (normed, w_query, w_key, w_value)),
+        *(in_hbm(v) for v in (keys, values, cosines, sines)),
     )
 
 
@@ -583,6 +551,7 @@
         ),
         fetched=(3,),
         scratch=(pltpu.VMEM((channels, width), BF16), pltpu.SemaphoreType.DMA),
+        cost=pl.CostEstimate(flops=COST, bytes_accessed=0, transcendentals=0),
     )
     paired = shifted(low[1], "seq_2", 1)
     half = low[0] + paired

time: 96.6 us -> 94.4 us (0.977)
  Pallas kernels: 20.8 us -> 19.1 us
    pallas_call x1, Pallas kernels: 4.77 us -> 3.5 us  [attended_rows(): pl.pallas_call(attention_kernel, out_shape=pltpu.VMEM((SLOT, HEAD_SIZE),...]
    unnamed x34 -> x40, local copies, waits for them, and re-layouts: 4.42 us -> 4.44 us
  transfers between devices with their start and end apart: 8 -> 8, of which waited for: 3 -> 3; matrix products, arithmetic and copies ran while one was open for 0% -> 0% of each run, Pallas kernels for 18% -> 17%
where the time goes in v5:
time: 94.4 us; the launch traced here: 93.8 us
  blocking collectives  58.7 us (62%)
  Pallas kernels  19.1 us (20%)
  local copies, waits for them, and re-layouts  5.21 us (6%)
  waiting for transfers between devices  4.86 us (5%)
  starting transfers between devices  4.23 us (4%)
    all_to_all x1, blocking collectives, block(): held = lax.all_to_all(copies, CHIPS, 0, 0, tiled=True)  24.6 us
    all_to_all x1, blocking collectives, block(): arrived = lax.all_to_all(summed, CHIPS, 0, 0, tiled=True)  19.3 us
    all_to_all x1, blocking collectives, block(): packed = lax.all_to_all(packed, PLANE, 0, 0, tiled=True)  14.8 us
    pallas_call x1, Pallas kernels, window_rows(): pl.pallas_call(window_kernel, out_shape=(out, out), in_specs=[anywhere] *...  10.9 us
    ppermute x8, waiting for transfers between devices, shifted(): lax.ppermute(value, axis, [(i, (i + step) % size) for i in range(size)])  4.86 us
    pallas_call x6, Pallas kernels, vmem_call(): pl.pallas_call(kernel, out_shape=tuple((pltpu.VMEM(shape, dtype) if inner...  4.68 us
    unnamed x40, local copies, waits for them, and re-layouts  4.44 us
    ppermute x8, starting transfers between devices, shifted(): lax.ppermute(value, axis, [(i, (i + step) % size) for i in range(size)])  4.23 us
  transfers between devices with their start and end apart: 8, of which 3 were waited for; matrix products, arithmetic and copies ran while one was open for 0% of the time, Pallas kernels for 17%

profile of v5, /device:TPU:0, one launch (start us, length us, event | category | flops | bytes accessed | tf_op | source)
XLA Modules:
  0.0 93.8 jit_solution(9788457078748866239)
XLA Ops:
  0.6 0.8 broadcast_in_dim.15
  1.4 24.6 %all_to_all.15.near = bf16[64,32,96]{2,1,0:T(8,128)(2,1)S(1)} all-to-all(bf16[64,32,96]{2,1,0:T(8,128)(2,1)S(1)} %broadcast_in_dim.15), channel_id=1, replica_groups=mesh['grp'=4,'seq_0'=4,'seq_1'=4,'seq_2'=2] {'grp','seq_0','seq_1'}, dimensions={0} | all-to-all | bytes 786432 | tf_op jit(solution)/shard_map/all_to_all | solution.py:534
  26.0 1.9 %collective-permute-done.far = bf16[64,32,96]{2,1,0:T(8,128)(2,1)S(1)} collective-permute-done((bf16[64,32,96]{2,1,0:T(8,128)(2,1)S(1)}, bf16[64,32,96]{2,1,0:T(8,128)(2,1)S(1)}, u32[]{:S(2)}, u32[]{:S(2)}) %collective-permute-start) | collective-permute-done | bytes 393248 | tf_op jit(solution)/shard_map/ppermute | solution.py:50
  27.9 0.8 copy-done.14
  28.7 0.8 copy-done.15
  29.5 0.7 copy-done.16
  30.2 0.7 copy-done.17
  30.9 0.7 copy-done.18
  31.6 1.5 %shard_map.248 = (bf16[4096,96]{1,0:T(8,128)(2,1)S(1)}, f32[64,96]{1,0:T(8,128)S(1)}, f32[2,144,128]{2,1,0:T(8,128)S(1)}) custom-call(bf16[64,32,96]{2,1,0:T(8,128)(2,1)S(1)} %all_to_all.15.near, bf16[64,32,96]{2,1,0:T(8,128)(2,1)S(1)} %collective-permute-done.far, f32[32,128]{1,0:T(8,128)S(1)} %bitcast.29, bf16[64,4096]{1,0:T(8,128)(2,1)} %bitcast.32, ...), custom_call_target="tpu_custom_call" | custom-call | flops 8000000000 | tf_op jit(solution)/shard_map/pallas_call | solution.py:84
  33.3 1.1 %collective-permute-done.1 = f32[144,128]{1,0:T(8,128)S(1)} collective-permute-done((f32[144,128]{1,0:T(8,128)S(1)}, f32[144,128]{1,0:T(8,128)S(1)}, u32[]{:S(2)}, u32[]{:S(2)}) %collective-permute-start.1) | collective-permute-done | bytes 73760 | tf_op jit(solution)/shard_map/ppermute | solution.py:50
  34.5 0.2 collective-permute-start.2
  34.7 2.1 %collective-permute-start.3 = (f32[144,128]{1,0:T(8,128)S(1)}, f32[144,128]{1,0:T(8,128)S(1)}, u32[]{:S(2)}, u32[]{:S(2)}) collective-permute-start(f32[144,128]{1,0:T(8,128)S(1)} %bitcast_add_fusion.s0), channel_id=1, source_target_pairs={{0,64},{32,96},{64,0},{96,32},{1,65},{33,97},{65,1},{97,33},{2,66}... | collective-permute-start | bytes 221192 | tf_op jit(solution)/shard_map/ppermute | solution.py:50
  36.8 1.1 %collective-permute-start.4 = (f32[144,128]{1,0:T(8,128)S(1)}, f32[144,128]{1,0:T(8,128)S(1)}, u32[]{:S(2)}, u32[]{:S(2)}) collective-permute-start(f32[144,128]{1,0:T(8,128)S(1)} %bitcast_add_fusion.s0), channel_id=1, source_target_pairs={{0,96},{32,0},{64,32},{96,64},{1,97},{33,1},{65,33},{97,65},{2,98}... | collective-permute-start | bytes 221192 | tf_op jit(solution)/shard_map/ppermute | solution.py:50
  37.9 10.9 %shard_map.249 = (bf16[3,512,256]{2,1,0:T(8,128)(2,1)}, bf16[3,512,256]{2,1,0:T(8,128)(2,1)}) custom-call(s32[96]{0:T(128)} %lengths_hbm.3, bf16[3,512,4096]{2,1,0:T(8,128)(2,1)} %cached.1, bf16[4096,256]{1,0:T(8,128)(2,1)} %w_key.3, bf16[4096,256]{1,0:T(8,128)(2,1)} %w_value.3, f32[520,128]{1,0:T(8,128)} %constant.6.clone.cosines, ...), custom_call_target="tpu_custom_call" | custom-call | tf_op jit(solution)/shard_map/pallas_call | solution.py:204
  48.8 3.5 %shard_map.250.attended = f32[16,128]{1,0:T(8,128)S(1)} custom-call(s32[96]{0:T(128)} %lengths_hbm.3, bf16[4096,96]{1,0:T(8,128)(2,1)S(1)} %get-tuple-element.15.normed, bf16[4096,512]{1,0:T(8,128)(2,1)S(1)} %copy-done.2, bf16[4096,256]{1,0:T(8,128)(2,1)S(1)} %copy-done, bf16[4096,256]{1,0:T(8,128)(2,1)S(1)} %copy-done.1, ...), custom_call_target="tpu_custom_call" | custom-call | tf_op jit(solution)/shard_map/pallas_call | solution.py:388
  52.5 14.8 %all_to_all.16.arrived = bf16[16,128,128]{2,1,0:T(8,128)(2,1)S(1)} all-to-all(bf16[16,128,128]{2,1,0:T(8,128)(2,1)S(1)} %shard_map.251), channel_id=1, replica_groups=mesh['grp'=4,'seq_0'=4,'seq_1'=4,'seq_2'=2] {'seq_0','seq_1'}, dimensions={0} | all-to-all | bytes 1048576 | tf_op jit(solution)/shard_map/all_to_all | solution.py:572
  67.5 0.5 collective-permute-start.6
  68.0 0.8 shard_map.253
  68.9 0.4 shard_map.254.term
  69.3 0.5 copy-done.7
  70.0 1.7 %shard_map.255 = (f32[16,64,96]{2,1,0:T(8,128)}, bf16[64,32,96]{2,1,0:T(8,128)(2,1)S(1)}, bf16[64,32,96]{2,1,0:T(8,128)(2,1)S(1)}) custom-call(f32[144,128]{1,0:T(8,128)S(1)} %get-tuple-element.18.near, f32[144,128]{1,0:T(8,128)S(1)} %collective-permute-done.5.far, bf16[256,128]{1,0:T(8,128)(2,1)S(1)} %get-tuple-element.19.near_rows, ...), custom_call_target="tpu_custom_call" | custom-call | tf_op jit(solution)/shard_map/pallas_call | solution.py:84
  71.8 1.8 %collective-permute-done.7 = bf16[64,32,96]{2,1,0:T(8,128)(2,1)S(1)} collective-permute-done((bf16[64,32,96]{2,1,0:T(8,128)(2,1)S(1)}, bf16[64,32,96]{2,1,0:T(8,128)(2,1)S(1)}, u32[]{:S(2)}, u32[]{:S(2)}) %collective-permute-start.7) | collective-permute-done | bytes 393248 | tf_op jit(solution)/shard_map/ppermute | solution.py:50
  73.8 19.3 %all_to_all.17 = bf16[64,32,96]{2,1,0:T(8,128)(2,1)S(1)} all-to-all(bf16[64,32,96]{2,1,0:T(8,128)(2,1)S(1)} %add_convert_fusion), channel_id=1, replica_groups=mesh['grp'=4,'seq_0'=4,'seq_1'=4,'seq_2'=2] {'grp','seq_0','seq_1'}, dimensions={0} | all-to-all | bytes 786432 | tf_op jit(solution)/shard_map/all_to_all | solution.py:593
  93.2 0.6 fusion
  (49 shorter events, 1.2 us)
Async XLA Ops:
  26.0 1.9 %collective-permute-start = (bf16[64,32,96]{2,1,0:T(8,128)(2,1)S(1)}, bf16[64,32,96]{2,1,0:T(8,128)(2,1)S(1)}, u32[]{:S(2)}, u32[]{:S(2)}) collective-permute-start(bf16[64,32,96]{2,1,0:T(8,128)(2,1)S(1)} %all_to_all.15.near), channel_id=1, source_target_pairs={{0,1},{1,0},{2,3},{3,2},{4,5},{5,4},{6,7},{7,6},{8,9},{9,8},{10,11... | collective-permute-start | bytes 1179656 | tf_op jit(solution)/shard_map/ppermute | solution.py:50
  27.9 0.8 copy-start.14
  33.1 1.3 %collective-permute-start.1 = (f32[144,128]{1,0:T(8,128)S(1)}, f32[144,128]{1,0:T(8,128)S(1)}, u32[]{:S(2)}, u32[]{:S(2)}) collective-permute-start(f32[144,128]{1,0:T(8,128)S(1)} %slice_bitcast_fusion), channel_id=1, source_target_pairs={{0,1},{1,0},{2,3},{3,2},{4,5},{5,4},{6,7},{7,6},{8,9},{9,8},{10,11... | collective-permute-start | bytes 221192 | tf_op jit(solution)/shard_map/ppermute | solution.py:50
  34.5 14.3 %copy-start = (bf16[4096,256]{1,0:T(8,128)(2,1)S(1)}, bf16[4096,256]{1,0:T(8,128)(2,1)}, u32[]{:S(2)}) copy-start(bf16[4096,256]{1,0:T(8,128)(2,1)} %w_key.3) | copy-start | bytes 6291460
  34.5 14.3 %copy-start.1 = (bf16[4096,256]{1,0:T(8,128)(2,1)S(1)}, bf16[4096,256]{1,0:T(8,128)(2,1)}, u32[]{:S(2)}) copy-start(bf16[4096,256]{1,0:T(8,128)(2,1)} %w_value.3) | copy-start | bytes 6291460
  34.5 17.8 %collective-permute-start.2 = (f32[144,128]{1,0:T(8,128)S(1)}, f32[144,128]{1,0:T(8,128)S(1)}, u32[]{:S(2)}, u32[]{:S(2)}) collective-permute-start(f32[144,128]{1,0:T(8,128)S(1)} %bitcast_add_fusion.s0), channel_id=1, source_target_pairs={{0,32},{32,64},{64,96},{96,0},{1,33},{33,65},{65,97},{97,1},{2,34}... | collective-permute-start | bytes 221192 | tf_op jit(solution)/shard_map/ppermute | solution.py:50
  34.7 17.6 %collective-permute-start.3 = (f32[144,128]{1,0:T(8,128)S(1)}, f32[144,128]{1,0:T(8,128)S(1)}, u32[]{:S(2)}, u32[]{:S(2)}) collective-permute-start(f32[144,128]{1,0:T(8,128)S(1)} %bitcast_add_fusion.s0), channel_id=1, source_target_pairs={{0,64},{32,96},{64,0},{96,32},{1,65},{33,97},{65,1},{97,33},{2,66}... | collective-permute-start | bytes 221192 | tf_op jit(solution)/shard_map/ppermute | solution.py:50
  36.8 15.6 %collective-permute-start.4 = (f32[144,128]{1,0:T(8,128)S(1)}, f32[144,128]{1,0:T(8,128)S(1)}, u32[]{:S(2)}, u32[]{:S(2)}) collective-permute-start(f32[144,128]{1,0:T(8,128)S(1)} %bitcast_add_fusion.s0), channel_id=1, source_target_pairs={{0,96},{32,0},{64,32},{96,64},{1,97},{33,1},{65,33},{97,65},{2,98}... | collective-permute-start | bytes 221192 | tf_op jit(solution)/shard_map/ppermute | solution.py:50
  37.9 11.0 %copy-start.2 = (bf16[4096,512]{1,0:T(8,128)(2,1)S(1)}, bf16[4096,512]{1,0:T(8,128)(2,1)}, u32[]{:S(2)}) copy-start(bf16[4096,512]{1,0:T(8,128)(2,1)} %w_query.1) | copy-start | bytes 12582916
  52.3 15.7 %copy-start.4 = (bf16[4096,112]{0,1:T(8,128)(2,1)S(1)}, bf16[4096,112]{0,1:T(8,128)(2,1)}, u32[]{:S(2)}) copy-start(bf16[4096,112]{0,1:T(8,128)(2,1)} %param.43) | copy-start | bytes 2752516
  52.3 15.6 %copy-start.5 = (bf16[4096,112]{0,1:T(8,128)(2,1)S(1)}, bf16[4096,112]{0,1:T(8,128)(2,1)}, u32[]{:S(2)}) copy-start(bf16[4096,112]{0,1:T(8,128)(2,1)} %param.44) | copy-start | bytes 2752516
  52.3 15.6 %copy-start.6 = (bf16[4096,64]{0,1:T(8,128)(2,1)S(1)}, bf16[4096,64]{0,1:T(8,128)(2,1)}, u32[]{:S(2)}) copy-start(bf16[4096,64]{0,1:T(8,128)(2,1)} %param.28) | copy-start | bytes 1572868
  67.3 1.6 %copy-start.3 = (bf16[112,4096]{1,0:T(8,128)(2,1)S(1)}, bf16[112,4096]{1,0:T(8,128)(2,1)}, u32[]{:S(2)}) copy-start(bf16[112,4096]{1,0:T(8,128)(2,1)} %w_mlp_down.1) | copy-start | bytes 2752516
  67.4 1.9 %collective-permute-start.5 = (f32[144,128]{1,0:T(8,128)S(1)}, f32[144,128]{1,0:T(8,128)S(1)}, u32[]{:S(2)}, u32[]{:S(2)}) collective-permute-start(f32[144,128]{1,0:T(8,128)S(1)} %get-tuple-element.18.near), channel_id=1, source_target_pairs={{0,1},{1,0},{2,3},{3,2},{4,5},{5,4},{6,7},{7,6},{8,9},{9,8},{10,11... | collective-permute-start | bytes 221192 | tf_op jit(solution)/shard_map/ppermute | solution.py:50
  67.5 1.8 %collective-permute-start.6 = (bf16[256,128]{1,0:T(8,128)(2,1)S(1)}, bf16[256,128]{1,0:T(8,128)(2,1)S(1)}, u32[]{:S(2)}, u32[]{:S(2)}) collective-permute-start(bf16[256,128]{1,0:T(8,128)(2,1)S(1)} %get-tuple-element.19.near_rows), channel_id=1, source_target_pairs={{0,1},{1,0},{2,3},{3,2},{4,5},{5,4},{6,7},{7,6},{8,9},{9,8},{10,11... | collective-permute-start | bytes 196616 | tf_op jit(solution)/shard_map/ppermute | solution.py:50
  68.8 1.0 %copy-start.7 = (f32[96,16,64]{0,2,1:T(8,128)S(1)}, f32[96,16,64]{0,2,1:T(8,128)}, u32[]{:S(2)}) copy-start(f32[96,16,64]{0,2,1:T(8,128)} %param.37) | copy-start | bytes 1179652
  68.8 1.2 %copy-start.8 = (bf16[64,4096]{1,0:T(8,128)(2,1)S(1)}, bf16[64,4096]{1,0:T(8,128)(2,1)}, u32[]{:S(2)}) copy-start(bf16[64,4096]{1,0:T(8,128)(2,1)} %w_out.1) | copy-start | bytes 1572868
  68.8 1.2 %copy-start.9 = (bf16[512,128]{1,0:T(8,128)(2,1)S(1)}, bf16[512,128]{1,0:T(8,128)(2,1)}, u32[]{:S(2)}) copy-start(bf16[512,128]{1,0:T(8,128)(2,1)} %w_attn.1) | copy-start | bytes 393220
  68.8 1.2 %copy-start.10 = (bf16[256,64]{0,1:T(8,128)(2,1)S(1)}, bf16[256,64]{0,1:T(8,128)(2,1)}, u32[]{:S(2)}) copy-start(bf16[256,64]{0,1:T(8,128)(2,1)} %param.33) | copy-start | bytes 98308
  68.8 1.2 %copy-start.11 = (f32[16,64]{1,0:T(8,128)S(1)}, f32[16,64]{1,0:T(8,128)}, u32[]{:S(2)}) copy-start(f32[16,64]{1,0:T(8,128)} %log_decay.1) | copy-start | bytes 12292
  68.9 1.2 %copy-start.12 = (f32[64]{0:T(128)S(1)}, f32[64]{0:T(128)}, u32[]{:S(2)}) copy-start(f32[64]{0:T(128)} %param.34) | copy-start | bytes 772
  68.9 1.2 %copy-start.13 = (f32[64]{0:T(128)S(1)}, f32[64]{0:T(128)}, u32[]{:S(2)}) copy-start(f32[64]{0:T(128)} %param.36) | copy-start | bytes 772
  71.7 21.5 %copy-start.19 = (bf16[96,32]{0,1:T(8,128)(2,1)S(1)}, bf16[96,32]{0,1:T(8,128)(2,1)}, u32[]{:S(2)}) copy-start(bf16[96,32]{0,1:T(8,128)(2,1)} %param.25) | copy-start | bytes 18436
  71.7 1.9 %collective-permute-start.7 = (bf16[64,32,96]{2,1,0:T(8,128)(2,1)S(1)}, bf16[64,32,96]{2,1,0:T(8,128)(2,1)S(1)}, u32[]{:S(2)}, u32[]{:S(2)}) collective-permute-start(bf16[64,32,96]{2,1,0:T(8,128)(2,1)S(1)} %get-tuple-element.24), channel_id=1, source_target_pairs={{0,1},{1,0},{2,3},{3,2},{4,5},{5,4},{6,7},{7,6},{8,9},{9,8},{10,11... | collective-permute-start | bytes 1179656 | tf_op jit(solution)/shard_map/ppermute | solution.py:50
  (4 other events, 2.9 us)

commit v6 on v5

--- a/solution.py
+++ b/solution.py
@@ -78,14 +78,14 @@
     return pltpu.with_memory_space_constraint(value, pltpu.VMEM)
 
 
-def vmem_call(kernel, outs, operands, fetched=(), scratch=(), limit=12 << 20, cost=None):
+def vmem_call(kernel, outs, operands, fetched=(), stored=(), scratch=(), limit=12 << 20, cost=None):
     vmem = pl.BlockSpec(memory_space=pltpu.VMEM)
     anywhere = pl.BlockSpec(memory_space=pl.ANY)
     return pl.pallas_call(
         kernel,
         out_shape=tuple(pltpu.VMEM(shape, dtype) if inner else jax.ShapeDtypeStruct(shape, dtype) for shape, dtype, inner in outs),
         in_specs=[anywhere if k in fetched else vmem for k in range(len(operands))],
-        out_specs=tuple(vmem for _ in outs),
+        out_specs=tuple(anywhere if k in stored else vmem for k in range(len(outs))),
         scratch_shapes=list(scratch),
         compiler_params=pltpu.CompilerParams(vmem_limit_bytes=limit),
         cost_estimate=cost,
@@ -93,8 +93,8 @@
 
 
 def window_kernel(
-    lengths_hbm, cached, w_key, w_value, cosines, sines, key_out, value_out,
-    rows, weights, cos, sin, turned, plain, lengths,
+    lengths_hbm, cached, w_key, w_value, cosines, sines, key_out, value_out, last_key, last_value,
+    rows, weights, cos, sin, early_key, early_value, lengths,
     row_sem, first_sem, key_sem, value_sem, table_sem, out_sem, length_sem,
 ):
     seqs, window, width = cached.shape
@@ -135,16 +135,18 @@
 
     def finish(b, both):
         live = both.shape[0]
+        at = b if b < seqs - 1 else 0
+        turned, plain = (early_key, early_value) if b < seqs - 1 else (last_key, last_value)
         for head in range(columns // HEAD_SIZE):
             lanes = slice(head * HEAD_SIZE, (head + 1) * HEAD_SIZE)
             part = both[:, lanes]
-            turned[b, 0:live, lanes] = (
+            turned[at, 0:live, lanes] = (
                 part * cos[0:live, :] + pltpu.roll(part, HEAD_SIZE // 2, 1) * sin[0:live, :]
             ).astype(BF16)
-        plain[b, 0:live, :] = both[:, columns:].astype(BF16)
+        plain[at, 0:live, :] = both[:, columns:].astype(BF16)
         if live < window:
-            turned[b, live:, :] = jnp.zeros((window - live, columns), BF16)
-            plain[b, live:, :] = jnp.zeros((window - live, columns), BF16)
+            turned[at, live:, :] = jnp.zeros((window - live, columns), BF16)
+            plain[at, live:, :] = jnp.zeros((window - live, columns), BF16)
 
     def by_length(b, work):
         length = lengths[first + b]
@@ -161,8 +163,8 @@
 
     def out_copies(b):
         return (
-            pltpu.make_async_copy(turned.at[b], key_out.at[b], out_sem.at[0, b]),
-            pltpu.make_async_copy(plain.at[b], value_out.at[b], out_sem.at[1, b]),
+            pltpu.make_async_copy(early_key.at[b], key_out.at[b], out_sem.at[0, b]),
+            pltpu.make_async_copy(early_value.at[b], value_out.at[b], out_sem.at[1, b]),
         )
 
     def first_rows(size):
@@ -180,17 +182,13 @@
     by_length(0, first_rows)
     for copy in out_copies(0):
         copy.start()
-    for copy in later:
-        copy.wait()
-
-    def later_rows(b, carry):
-        by_length(b, lambda size: finish(b, dot(rows[b, 0:size, :], weights[...])))
-        for copy in out_copies(b):
-            copy.start()
-        return carry
-
-    lax.fori_loop(1, seqs, later_rows, 0)
-    for b in range(seqs):
+    for b in range(1, seqs):
+        later[b - 1].wait()
+        by_length(b, lambda size, b=b: finish(b, dot(rows[b, 0:size, :], weights[...])))
+        if b < seqs - 1:
+            for copy in out_copies(b):
+                copy.start()
+    for b in range(seqs - 1):
         for copy in out_copies(b):
             copy.wait()
 
@@ -199,27 +197,31 @@
     seqs, window, width = cached.shape
     columns = w_key.shape[1]
     anywhere = pl.BlockSpec(memory_space=pl.ANY)
-    out = pltpu.HBM((seqs, window, columns), BF16)
+    early = (seqs - 1, window, columns)
+    last = (1, window, columns)
+    vmem = pl.BlockSpec(memory_space=pltpu.VMEM)
     dma = pltpu.SemaphoreType.DMA
     return pl.pallas_call(
         window_kernel,
-        out_shape=(out, out),
+        out_shape=(
+            pltpu.HBM(early, BF16), pltpu.HBM(early, BF16), pltpu.VMEM(last, BF16), pltpu.VMEM(last, BF16)
+        ),
         in_specs=[anywhere] * 6,
-        out_specs=(anywhere, anywhere),
+        out_specs=(anywhere, anywhere, vmem, vmem),
         scratch_shapes=[
             pltpu.VMEM((seqs, window, width), BF16),
             pltpu.VMEM((width, 2 * columns), BF16),
             pltpu.VMEM((window, HEAD_SIZE), F32),
             pltpu.VMEM((window, HEAD_SIZE), F32),
-            pltpu.VMEM((seqs, window, columns), BF16),
-            pltpu.VMEM((seqs, window, columns), BF16),
+            pltpu.VMEM(early, BF16),
+            pltpu.VMEM(early, BF16),
             pltpu.SMEM(lengths.shape, jnp.int32),
             dma((seqs,)),
             dma((WEIGHT_PIECES,)),
             dma((WEIGHT_PIECES,)),
             dma((WEIGHT_PIECES,)),
             dma((2,)),
-            dma((2, seqs)),
+            dma((2, seqs - 1)),
             dma,
         ],
         compiler_params=pltpu.CompilerParams(vmem_limit_bytes=40 << 20),
@@ -278,12 +280,13 @@
 
 
 def attention_kernel(
-    lengths_hbm, normed, w_query, w_key, w_value, key_rows, value_rows, cosines, sines, out,
+    lengths_hbm, normed, w_query, w_key, w_value, last_key, last_value, key_rows, value_rows,
+    cosines, sines, out,
     keys, values, cos_rows, sin_rows, lengths, row_sem, table_sem, length_sem,
 ):
     fetch = pltpu.make_async_copy(lengths_hbm, lengths, length_sem)
     fetch.start()
-    seqs, window = keys.shape[0], keys.shape[1]
+    seqs, window = keys.shape[0] + 1, keys.shape[1]
     columns = keys.shape[2]
     queries = w_query.shape[1]
     kv_heads = columns // HEAD_SIZE
@@ -340,11 +343,15 @@
 
     q = turned(jnp.concatenate(stacked, axis=0))
     k_new = turned(jnp.concatenate(new_key, axis=0))
+
+    def row_of(early, last, b):
+        return early.at[b] if b < seqs - 1 else last.at[0]
+
     scores = jnp.concatenate(
         [
             lax.dot_general(
                 q[n * 8 : n * 8 + 8],
-                keys[b, :, g * HEAD_SIZE : (g + 1) * HEAD_SIZE],
+                row_of(keys, last_key, b)[:, g * HEAD_SIZE : (g + 1) * HEAD_SIZE],
                 NT,
                 preferred_element_type=F32,
             )
@@ -369,7 +376,7 @@
     rounded = shares.astype(BF16)
     summed = jnp.concatenate(
         [
-            dot(rounded[n * 8 : n * 8 + 8], values[b, :, g * HEAD_SIZE : (g + 1) * HEAD_SIZE])
+            dot(rounded[n * 8 : n * 8 + 8], row_of(values, last_value, b)[:, g * HEAD_SIZE : (g + 1) * HEAD_SIZE])
             for n, (b, g) in enumerate(blocks)
         ],
         axis=0,
@@ -381,14 +388,16 @@
         out[n * group : (n + 1) * group, :] = result[n * 8 : n * 8 + group, :]
 
 
-def attended_rows(lengths, normed, w_query, w_key, w_value, keys, values, cosines, sines):
+def attended_rows(
+    lengths, normed, w_query, w_key, w_value, keys, values, last_key, last_value, cosines, sines
+):
     anywhere = pl.BlockSpec(memory_space=pl.ANY)
     vmem = pl.BlockSpec(memory_space=pltpu.VMEM)
     dma = pltpu.SemaphoreType.DMA
     return pl.pallas_call(
         attention_kernel,
         out_shape=pltpu.VMEM((SLOT, HEAD_SIZE), F32),
-        in_specs=[anywhere] + [vmem] * 4 + [anywhere] * 4,
+        in_specs=[anywhere] + [vmem] * 6 + [anywhere] * 4,
         out_specs=vmem,
         scratch_shapes=[
             pltpu.VMEM(keys.shape, BF16),
@@ -397,13 +406,13 @@
             pltpu.VMEM((8, HEAD_SIZE), F32),
             pltpu.SMEM(lengths.shape, jnp.int32),
             dma((2,)),
-            dma((2, keys.shape[0])),
+            dma((2, keys.shape[0] + 1)),
             dma,
         ],
         compiler_params=pltpu.CompilerParams(vmem_limit_bytes=12 << 20),
     )(
         in_hbm(lengths),
-        *(in_vmem(v) for v in (normed, w_query, w_key, w_value)),
+        *(in_vmem(v) for v in (normed, w_query, w_key, w_value, last_key, last_value)),
         *(in_hbm(v) for v in (keys, values, cosines, sines)),
     )
 
@@ -438,7 +447,7 @@
 
 def outer_kernel(
     near, far, near_rows, far_rows, w_step, log_decay, step_bias, skip, conv, gate, state, w_out, term, w_attn,
-    state_out, keep_out, send_out, total,
+    state_hbm, keep_out, send_out, total, state_out, state_sem,
 ):
     c = lax.axis_index("seq_2").astype(jnp.int32)
     seq = own_seq()
@@ -466,6 +475,8 @@
         fresh = decay * state[n] + driven * low[rank + n : rank + n + 1]
         state_out[n] = fresh
         mixed = mixed + fresh * low[rank + states + n : rank + states + n + 1]
+    store = pltpu.make_async_copy(state_out, state_hbm, state_sem)
+    store.start()
     gated = (mixed * gate[...]).astype(BF16)
     total[...] = term[...] + lax.dot_general(gated, w_out[...], TN, preferred_element_type=F32)
 
@@ -495,6 +506,7 @@
             odd = block[(q + 1) * rows : (q + 2) * rows, :]
             keep_out[slot] = jnp.where(mine, even, odd)
             send_out[slot] = jnp.where(mine, odd, even)
+    store.wait()
 
 
 def block(
@@ -534,7 +546,7 @@
     held = lax.all_to_all(copies, CHIPS, 0, 0, tiled=True)
     other = shifted(held, "seq_2", 1)
 
-    keys, values = window_rows(
+    window_parts = window_rows(
         window_lengths, cached_inputs, key_projection, value_projection, cosines, sines
     )
 
@@ -557,7 +569,7 @@
     half = low[0] + paired
     arrived = from_ring(half, "grp")
     attended = attended_rows(
-        window_lengths, normed, w_query, key_projection, value_projection, keys, values,
+        window_lengths, normed, w_query, key_projection, value_projection, *window_parts,
         cosines, sines,
     )
     gate, act = vmem_call(
@@ -586,7 +598,12 @@
             near_low, far_low, near_rows, far_rows, w_step.T, log_decay, step_bias[None], skip_gain[None], conv, gate,
             jnp.transpose(ssm_state, (1, 2, 0)), w_ssm_out, term, w_attn_out,
         ),
-        scratch=(pltpu.VMEM((batch, width), F32),),
+        stored=(0,),
+        scratch=(
+            pltpu.VMEM((batch, width), F32),
+            pltpu.VMEM((states, channels, batch), F32),
+            pltpu.SemaphoreType.DMA,
+        ),
     )
     came = shifted(send, "seq_2", 1)
     summed = (keep.astype(F32) + came.astype(F32)).astype(BF16)

time: 94.4 us -> 93.1 us (0.986)
  Pallas kernels: 19.1 us -> 17.6 us
    pallas_call x1, Pallas kernels: 10.9 us -> 9.5 us  [window_rows(): pl.pallas_call(window_kernel, out_shape=(pltpu.HBM(early, BF16), pltpu.HB...]
  transfers between devices with their start and end apart: 8 -> 8, of which waited for: 3 -> 3; matrix products, arithmetic and copies ran while one was open for 0% -> 0% of each run, Pallas kernels for 17% -> 15%
where the time goes in v6:
time: 93.1 us; the launch traced here: 92.6 us
  blocking collectives  58.8 us (63%)
  Pallas kernels  17.6 us (19%)
  local copies, waits for them, and re-layouts  5.21 us (6%)
  waiting for transfers between devices  4.87 us (5%)
  starting transfers between devices  4.29 us (5%)
    all_to_all x1, blocking collectives, block(): held = lax.all_to_all(copies, CHIPS, 0, 0, tiled=True)  24.6 us
    all_to_all x1, blocking collectives, block(): arrived = lax.all_to_all(summed, CHIPS, 0, 0, tiled=True)  19.4 us
    all_to_all x1, blocking collectives, block(): packed = lax.all_to_all(packed, PLANE, 0, 0, tiled=True)  14.8 us
    pallas_call x1, Pallas kernels, window_rows(): pl.pallas_call(window_kernel, out_shape=(pltpu.HBM(early, BF16), pltpu.HB...  9.5 us
    ppermute x8, waiting for transfers between devices, shifted(): lax.ppermute(value, axis, [(i, (i + step) % size) for i in range(size)])  4.87 us
    pallas_call x6, Pallas kernels, vmem_call(): pl.pallas_call(kernel, out_shape=tuple((pltpu.VMEM(shape, dtype) if inner...  4.56 us
    unnamed x40, local copies, waits for them, and re-layouts  4.44 us
    ppermute x8, starting transfers between devices, shifted(): lax.ppermute(value, axis, [(i, (i + step) % size) for i in range(size)])  4.29 us
  transfers between devices with their start and end apart: 8, of which 3 were waited for; matrix products, arithmetic and copies ran while one was open for 0% of the time, Pallas kernels for 15%

profile of v6, /device:TPU:0, one launch (start us, length us, event | category | flops | bytes accessed | tf_op | source)
XLA Modules:
  0.0 92.6 jit_solution(7141490768303020445)
XLA Ops:
  0.6 0.8 broadcast_in_dim.15
  1.4 24.6 %all_to_all.15.near = bf16[64,32,96]{2,1,0:T(8,128)(2,1)S(1)} all-to-all(bf16[64,32,96]{2,1,0:T(8,128)(2,1)S(1)} %broadcast_in_dim.15), channel_id=1, replica_groups=mesh['grp'=4,'seq_0'=4,'seq_1'=4,'seq_2'=2] {'grp','seq_0','seq_1'}, dimensions={0} | all-to-all | bytes 786432 | tf_op jit(solution)/shard_map/all_to_all | solution.py:546
  26.0 1.9 %collective-permute-done.far = bf16[64,32,96]{2,1,0:T(8,128)(2,1)S(1)} collective-permute-done((bf16[64,32,96]{2,1,0:T(8,128)(2,1)S(1)}, bf16[64,32,96]{2,1,0:T(8,128)(2,1)S(1)}, u32[]{:S(2)}, u32[]{:S(2)}) %collective-permute-start) | collective-permute-done | bytes 393248 | tf_op jit(solution)/shard_map/ppermute | solution.py:50
  27.9 0.8 copy-done.14
  28.7 0.8 copy-done.15
  29.5 0.7 copy-done.16
  30.2 0.7 copy-done.17
  30.9 0.7 copy-done.18
  31.6 1.5 %shard_map.248 = (bf16[4096,96]{1,0:T(8,128)(2,1)S(1)}, f32[64,96]{1,0:T(8,128)S(1)}, f32[2,144,128]{2,1,0:T(8,128)S(1)}) custom-call(bf16[64,32,96]{2,1,0:T(8,128)(2,1)S(1)} %all_to_all.15.near, bf16[64,32,96]{2,1,0:T(8,128)(2,1)S(1)} %collective-permute-done.far, f32[32,128]{1,0:T(8,128)S(1)} %bitcast.29, bf16[64,4096]{1,0:T(8,128)(2,1)} %bitcast.32, ...), custom_call_target="tpu_custom_call" | custom-call | flops 8000000000 | tf_op jit(solution)/shard_map/pallas_call | solution.py:84
  33.3 1.1 %collective-permute-done.1 = f32[144,128]{1,0:T(8,128)S(1)} collective-permute-done((f32[144,128]{1,0:T(8,128)S(1)}, f32[144,128]{1,0:T(8,128)S(1)}, u32[]{:S(2)}, u32[]{:S(2)}) %collective-permute-start.1) | collective-permute-done | bytes 73760 | tf_op jit(solution)/shard_map/ppermute | solution.py:50
  34.5 0.2 collective-permute-start.2
  34.7 2.1 %collective-permute-start.3 = (f32[144,128]{1,0:T(8,128)S(1)}, f32[144,128]{1,0:T(8,128)S(1)}, u32[]{:S(2)}, u32[]{:S(2)}) collective-permute-start(f32[144,128]{1,0:T(8,128)S(1)} %bitcast_add_fusion.s0), channel_id=1, source_target_pairs={{0,64},{32,96},{64,0},{96,32},{1,65},{33,97},{65,1},{97,33},{2,66}... | collective-permute-start | bytes 221192 | tf_op jit(solution)/shard_map/ppermute | solution.py:50
  36.8 1.1 %collective-permute-start.4 = (f32[144,128]{1,0:T(8,128)S(1)}, f32[144,128]{1,0:T(8,128)S(1)}, u32[]{:S(2)}, u32[]{:S(2)}) collective-permute-start(f32[144,128]{1,0:T(8,128)S(1)} %bitcast_add_fusion.s0), channel_id=1, source_target_pairs={{0,96},{32,0},{64,32},{96,64},{1,97},{33,1},{65,33},{97,65},{2,98}... | collective-permute-start | bytes 221192 | tf_op jit(solution)/shard_map/ppermute | solution.py:50
  37.9 9.5 %shard_map.249 = (bf16[2,512,256]{2,1,0:T(8,128)(2,1)}, bf16[2,512,256]{2,1,0:T(8,128)(2,1)}, bf16[1,512,256]{2,1,0:T(8,128)(2,1)S(1)}, bf16[1,512,256]{2,1,0:T(8,128)(2,1)S(1)}) custom-call(s32[96]{0:T(128)} %lengths_hbm.3, bf16[3,512,4096]{2,1,0:T(8,128)(2,1)} %cached.1, bf16[4096,256]{1,0:T(8,128)(2,1)} %w_key.3, bf16[4096,256]{1,0:T(8,128)(2,1)} %w_value.3, ...), custom_call_target="tpu_custom_call" | custom-call | tf_op jit(solution)/shard_map/pallas_call | solution.py:204
  47.4 3.5 %shard_map.250.attended = f32[16,128]{1,0:T(8,128)S(1)} custom-call(s32[96]{0:T(128)} %lengths_hbm.3, bf16[4096,96]{1,0:T(8,128)(2,1)S(1)} %get-tuple-element.17.normed, bf16[4096,512]{1,0:T(8,128)(2,1)S(1)} %copy-done.2, bf16[4096,256]{1,0:T(8,128)(2,1)S(1)} %copy-done, bf16[4096,256]{1,0:T(8,128)(2,1)S(1)} %copy-done.1, ...), custom_call_target="tpu_custom_call" | custom-call | tf_op jit(solution)/shard_map/pallas_call | solution.py:397
  51.1 14.8 %all_to_all.16.arrived = bf16[16,128,128]{2,1,0:T(8,128)(2,1)S(1)} all-to-all(bf16[16,128,128]{2,1,0:T(8,128)(2,1)S(1)} %shard_map.251), channel_id=1, replica_groups=mesh['grp'=4,'seq_0'=4,'seq_1'=4,'seq_2'=2] {'seq_0','seq_1'}, dimensions={0} | all-to-all | bytes 1048576 | tf_op jit(solution)/shard_map/all_to_all | solution.py:584
  66.1 0.5 collective-permute-start.6
  66.6 0.8 shard_map.253
  67.5 0.4 shard_map.254.term
  68.0 0.5 copy-done.7
  68.7 1.6 %shard_map.255 = (f32[16,64,96]{2,1,0:T(8,128)}, bf16[64,32,96]{2,1,0:T(8,128)(2,1)S(1)}, bf16[64,32,96]{2,1,0:T(8,128)(2,1)S(1)}) custom-call(f32[144,128]{1,0:T(8,128)S(1)} %get-tuple-element.22.near, f32[144,128]{1,0:T(8,128)S(1)} %collective-permute-done.5.far, bf16[256,128]{1,0:T(8,128)(2,1)S(1)} %get-tuple-element.23.near_rows, ...), custom_call_target="tpu_custom_call" | custom-call | tf_op jit(solution)/shard_map/pallas_call | solution.py:84
  70.4 1.8 %collective-permute-done.7 = bf16[64,32,96]{2,1,0:T(8,128)(2,1)S(1)} collective-permute-done((bf16[64,32,96]{2,1,0:T(8,128)(2,1)S(1)}, bf16[64,32,96]{2,1,0:T(8,128)(2,1)S(1)}, u32[]{:S(2)}, u32[]{:S(2)}) %collective-permute-start.7) | collective-permute-done | bytes 393248 | tf_op jit(solution)/shard_map/ppermute | solution.py:50
  72.4 19.4 %all_to_all.17 = bf16[64,32,96]{2,1,0:T(8,128)(2,1)S(1)} all-to-all(bf16[64,32,96]{2,1,0:T(8,128)(2,1)S(1)} %add_convert_fusion), channel_id=1, replica_groups=mesh['grp'=4,'seq_0'=4,'seq_1'=4,'seq_2'=2] {'grp','seq_0','seq_1'}, dimensions={0} | all-to-all | bytes 786432 | tf_op jit(solution)/shard_map/all_to_all | solution.py:610
  92.0 0.6 fusion
  (49 shorter events, 1.3 us)
Async XLA Ops:
  26.0 1.9 %collective-permute-start = (bf16[64,32,96]{2,1,0:T(8,128)(2,1)S(1)}, bf16[64,32,96]{2,1,0:T(8,128)(2,1)S(1)}, u32[]{:S(2)}, u32[]{:S(2)}) collective-permute-start(bf16[64,32,96]{2,1,0:T(8,128)(2,1)S(1)} %all_to_all.15.near), channel_id=1, source_target_pairs={{0,1},{1,0},{2,3},{3,2},{4,5},{5,4},{6,7},{7,6},{8,9},{9,8},{10,11... | collective-permute-start | bytes 1179656 | tf_op jit(solution)/shard_map/ppermute | solution.py:50
  27.9 0.8 copy-start.14
  33.1 1.3 %collective-permute-start.1 = (f32[144,128]{1,0:T(8,128)S(1)}, f32[144,128]{1,0:T(8,128)S(1)}, u32[]{:S(2)}, u32[]{:S(2)}) collective-permute-start(f32[144,128]{1,0:T(8,128)S(1)} %slice_bitcast_fusion), channel_id=1, source_target_pairs={{0,1},{1,0},{2,3},{3,2},{4,5},{5,4},{6,7},{7,6},{8,9},{9,8},{10,11... | collective-permute-start | bytes 221192 | tf_op jit(solution)/shard_map/ppermute | solution.py:50
  34.5 12.9 %copy-start = (bf16[4096,256]{1,0:T(8,128)(2,1)S(1)}, bf16[4096,256]{1,0:T(8,128)(2,1)}, u32[]{:S(2)}) copy-start(bf16[4096,256]{1,0:T(8,128)(2,1)} %w_key.3) | copy-start | bytes 6291460
  34.5 12.9 %copy-start.1 = (bf16[4096,256]{1,0:T(8,128)(2,1)S(1)}, bf16[4096,256]{1,0:T(8,128)(2,1)}, u32[]{:S(2)}) copy-start(bf16[4096,256]{1,0:T(8,128)(2,1)} %w_value.3) | copy-start | bytes 6291460
  34.5 16.4 %collective-permute-start.2 = (f32[144,128]{1,0:T(8,128)S(1)}, f32[144,128]{1,0:T(8,128)S(1)}, u32[]{:S(2)}, u32[]{:S(2)}) collective-permute-start(f32[144,128]{1,0:T(8,128)S(1)} %bitcast_add_fusion.s0), channel_id=1, source_target_pairs={{0,32},{32,64},{64,96},{96,0},{1,33},{33,65},{65,97},{97,1},{2,34}... | collective-permute-start | bytes 221192 | tf_op jit(solution)/shard_map/ppermute | solution.py:50
  34.7 16.2 %collective-permute-start.3 = (f32[144,128]{1,0:T(8,128)S(1)}, f32[144,128]{1,0:T(8,128)S(1)}, u32[]{:S(2)}, u32[]{:S(2)}) collective-permute-start(f32[144,128]{1,0:T(8,128)S(1)} %bitcast_add_fusion.s0), channel_id=1, source_target_pairs={{0,64},{32,96},{64,0},{96,32},{1,65},{33,97},{65,1},{97,33},{2,66}... | collective-permute-start | bytes 221192 | tf_op jit(solution)/shard_map/ppermute | solution.py:50
  36.8 14.2 %collective-permute-start.4 = (f32[144,128]{1,0:T(8,128)S(1)}, f32[144,128]{1,0:T(8,128)S(1)}, u32[]{:S(2)}, u32[]{:S(2)}) collective-permute-start(f32[144,128]{1,0:T(8,128)S(1)} %bitcast_add_fusion.s0), channel_id=1, source_target_pairs={{0,96},{32,0},{64,32},{96,64},{1,97},{33,1},{65,33},{97,65},{2,98}... | collective-permute-start | bytes 221192 | tf_op jit(solution)/shard_map/ppermute | solution.py:50
  37.9 9.5 %copy-start.2 = (bf16[4096,512]{1,0:T(8,128)(2,1)S(1)}, bf16[4096,512]{1,0:T(8,128)(2,1)}, u32[]{:S(2)}) copy-start(bf16[4096,512]{1,0:T(8,128)(2,1)} %w_query.1) | copy-start | bytes 12582916
  50.9 15.7 %copy-start.4 = (bf16[4096,112]{0,1:T(8,128)(2,1)S(1)}, bf16[4096,112]{0,1:T(8,128)(2,1)}, u32[]{:S(2)}) copy-start(bf16[4096,112]{0,1:T(8,128)(2,1)} %param.43) | copy-start | bytes 2752516
  50.9 15.7 %copy-start.5 = (bf16[4096,112]{0,1:T(8,128)(2,1)S(1)}, bf16[4096,112]{0,1:T(8,128)(2,1)}, u32[]{:S(2)}) copy-start(bf16[4096,112]{0,1:T(8,128)(2,1)} %param.44) | copy-start | bytes 2752516
  50.9 15.7 %copy-start.6 = (bf16[4096,64]{0,1:T(8,128)(2,1)S(1)}, bf16[4096,64]{0,1:T(8,128)(2,1)}, u32[]{:S(2)}) copy-start(bf16[4096,64]{0,1:T(8,128)(2,1)} %param.28) | copy-start | bytes 1572868
  65.9 1.6 %copy-start.3 = (bf16[112,4096]{1,0:T(8,128)(2,1)S(1)}, bf16[112,4096]{1,0:T(8,128)(2,1)}, u32[]{:S(2)}) copy-start(bf16[112,4096]{1,0:T(8,128)(2,1)} %w_mlp_down.1) | copy-start | bytes 2752516
  66.1 1.9 %collective-permute-start.5 = (f32[144,128]{1,0:T(8,128)S(1)}, f32[144,128]{1,0:T(8,128)S(1)}, u32[]{:S(2)}, u32[]{:S(2)}) collective-permute-start(f32[144,128]{1,0:T(8,128)S(1)} %get-tuple-element.22.near), channel_id=1, source_target_pairs={{0,1},{1,0},{2,3},{3,2},{4,5},{5,4},{6,7},{7,6},{8,9},{9,8},{10,11... | collective-permute-start | bytes 221192 | tf_op jit(solution)/shard_map/ppermute | solution.py:50
  66.1 1.8 %collective-permute-start.6 = (bf16[256,128]{1,0:T(8,128)(2,1)S(1)}, bf16[256,128]{1,0:T(8,128)(2,1)S(1)}, u32[]{:S(2)}, u32[]{:S(2)}) collective-permute-start(bf16[256,128]{1,0:T(8,128)(2,1)S(1)} %get-tuple-element.23.near_rows), channel_id=1, source_target_pairs={{0,1},{1,0},{2,3},{3,2},{4,5},{5,4},{6,7},{7,6},{8,9},{9,8},{10,11... | collective-permute-start | bytes 196616 | tf_op jit(solution)/shard_map/ppermute | solution.py:50
  67.5 1.0 %copy-start.7 = (f32[96,16,64]{0,2,1:T(8,128)S(1)}, f32[96,16,64]{0,2,1:T(8,128)}, u32[]{:S(2)}) copy-start(f32[96,16,64]{0,2,1:T(8,128)} %param.37) | copy-start | bytes 1179652
  67.5 1.2 %copy-start.8 = (bf16[64,4096]{1,0:T(8,128)(2,1)S(1)}, bf16[64,4096]{1,0:T(8,128)(2,1)}, u32[]{:S(2)}) copy-start(bf16[64,4096]{1,0:T(8,128)(2,1)} %w_out.1) | copy-start | bytes 1572868
  67.5 1.2 %copy-start.9 = (bf16[512,128]{1,0:T(8,128)(2,1)S(1)}, bf16[512,128]{1,0:T(8,128)(2,1)}, u32[]{:S(2)}) copy-start(bf16[512,128]{1,0:T(8,128)(2,1)} %w_attn.1) | copy-start | bytes 393220
  67.5 1.2 %copy-start.10 = (bf16[256,64]{0,1:T(8,128)(2,1)S(1)}, bf16[256,64]{0,1:T(8,128)(2,1)}, u32[]{:S(2)}) copy-start(bf16[256,64]{0,1:T(8,128)(2,1)} %param.33) | copy-start | bytes 98308
  67.5 1.2 %copy-start.11 = (f32[16,64]{1,0:T(8,128)S(1)}, f32[16,64]{1,0:T(8,128)}, u32[]{:S(2)}) copy-start(f32[16,64]{1,0:T(8,128)} %log_decay.1) | copy-start | bytes 12292
  67.5 1.2 %copy-start.12 = (f32[64]{0:T(128)S(1)}, f32[64]{0:T(128)}, u32[]{:S(2)}) copy-start(f32[64]{0:T(128)} %param.34) | copy-start | bytes 772
  67.5 1.2 %copy-start.13 = (f32[64]{0:T(128)S(1)}, f32[64]{0:T(128)}, u32[]{:S(2)}) copy-start(f32[64]{0:T(128)} %param.36) | copy-start | bytes 772
  70.3 21.7 %copy-start.19 = (bf16[96,32]{0,1:T(8,128)(2,1)S(1)}, bf16[96,32]{0,1:T(8,128)(2,1)}, u32[]{:S(2)}) copy-start(bf16[96,32]{0,1:T(8,128)(2,1)} %param.25) | copy-start | bytes 18436
  70.3 2.0 %collective-permute-start.7 = (bf16[64,32,96]{2,1,0:T(8,128)(2,1)S(1)}, bf16[64,32,96]{2,1,0:T(8,128)(2,1)S(1)}, u32[]{:S(2)}, u32[]{:S(2)}) collective-permute-start(bf16[64,32,96]{2,1,0:T(8,128)(2,1)S(1)} %get-tuple-element.28), channel_id=1, source_target_pairs={{0,1},{1,0},{2,3},{3,2},{4,5},{5,4},{6,7},{7,6},{8,9},{9,8},{10,11... | collective-permute-start | bytes 1179656 | tf_op jit(solution)/shard_map/ppermute | solution.py:50
  (4 other events, 2.9 us)

commit v7 on v6

--- a/solution.py
+++ b/solution.py
@@ -93,9 +93,10 @@
 
 
 def window_kernel(
-    lengths_hbm, cached, w_key, w_value, cosines, sines, key_out, value_out, last_key, last_value,
+    lengths_hbm, cached, w_key, w_value, cosines, sines, w_in_hbm, key_out, value_out, last_key,
+    last_value, w_in,
     rows, weights, cos, sin, early_key, early_value, lengths,
-    row_sem, first_sem, key_sem, value_sem, table_sem, out_sem, length_sem,
+    row_sem, first_sem, key_sem, value_sem, table_sem, out_sem, length_sem, w_in_sem,
 ):
     seqs, window, width = cached.shape
     columns = w_key.shape[1]
@@ -131,6 +132,8 @@
         copy.start()
     for copy in later:
         copy.start()
+    ahead = pltpu.make_async_copy(w_in_hbm, w_in, w_in_sem)
+    ahead.start()
     fetch.wait()
 
     def finish(b, both):
@@ -188,12 +191,13 @@
         if b < seqs - 1:
             for copy in out_copies(b):
                 copy.start()
+    ahead.wait()
     for b in range(seqs - 1):
         for copy in out_copies(b):
             copy.wait()
 
 
-def window_rows(lengths, cached, w_key, w_value, cosines, sines):
+def window_rows(lengths, cached, w_key, w_value, cosines, sines, w_in):
     seqs, window, width = cached.shape
     columns = w_key.shape[1]
     anywhere = pl.BlockSpec(memory_space=pl.ANY)
@@ -204,10 +208,14 @@
     return pl.pallas_call(
         window_kernel,
         out_shape=(
-            pltpu.HBM(early, BF16), pltpu.HBM(early, BF16), pltpu.VMEM(last, BF16), pltpu.VMEM(last, BF16)
+            pltpu.HBM(early, BF16),
+            pltpu.HBM(early, BF16),
+            pltpu.VMEM(last, BF16),
+            pltpu.VMEM(last, BF16),
+            pltpu.VMEM(w_in.shape, BF16),
         ),
-        in_specs=[anywhere] * 6,
-        out_specs=(anywhere, anywhere, vmem, vmem),
+        in_specs=[anywhere] * 7,
+        out_specs=(anywhere, anywhere, vmem, vmem, vmem),
         scratch_shapes=[
             pltpu.VMEM((seqs, window, width), BF16),
             pltpu.VMEM((width, 2 * columns), BF16),
@@ -223,16 +231,15 @@
             dma((2,)),
             dma((2, seqs - 1)),
             dma,
+            dma,
         ],
         compiler_params=pltpu.CompilerParams(vmem_limit_bytes=40 << 20),
-    )(*(in_hbm(v) for v in (lengths, cached, w_key, w_value, cosines, sines)))
+    )(*(in_hbm(v) for v in (lengths, cached, w_key, w_value, cosines, sines, w_in)))
 
 
 def inner_kernel(
-    near, far, gain, w_in_hbm, w_proj, past, taps, bias, normed_out, conv_out, low_out, w_in, w_sem,
+    near, far, gain, w_in, w_proj, past, taps, bias, normed_out, conv_out, low_out,
 ):
-    fetch = pltpu.make_async_copy(w_in_hbm, w_in, w_sem)
-    fetch.start()
     c = lax.axis_index("seq_2").astype(jnp.int32)
     rows, batch = near.shape[1], near.shape[2]
     total = jnp.zeros((rows, batch), F32)
@@ -255,7 +262,6 @@
             at = (j % per_gain) * rows
             column = gains[at : at + rows, j // per_gain : j // per_gain + 1]
             normed_out[j * rows : (j + 1) * rows, :] = (pair[k] * scale * column).astype(BF16)
-    fetch.wait()
     fresh = dot(w_in[...], normed_out[...]).astype(BF16).astype(F32)
     params = jnp.concatenate([taps[...], bias[...], jnp.zeros((3, taps.shape[1]), F32)], axis=0).T
     mixed = params[:, 4:5] + params[:, 3:4] * fresh
@@ -418,7 +424,8 @@
 
 
 def pack_kernel(s0, s1, s2, s3, attended, out):
-    low = (s0[...] + s1[...]) + (s2[...] + s3[...])
+    parts = [s[...].astype(F32) for s in (s0, s1, s2, s3)]
+    low = (parts[0] + parts[1]) + (parts[2] + parts[3])
     tail = low[MAIN:, :]
     moved = [pltpu.roll(tail, 96 - TAIL * p, 1) for p in range(3)]
     moved.append(jnp.zeros((MAIN - 3 * TAIL, HEAD_SIZE), F32))
@@ -546,8 +553,9 @@
     held = lax.all_to_all(copies, CHIPS, 0, 0, tiled=True)
     other = shifted(held, "seq_2", 1)
 
-    window_parts = window_rows(
-        window_lengths, cached_inputs, key_projection, value_projection, cosines, sines
+    *window_parts, w_in = window_rows(
+        window_lengths, cached_inputs, key_projection, value_projection, cosines, sines,
+        w_ssm_in.T,
     )
 
     normed, conv, low = vmem_call(
@@ -558,15 +566,13 @@
             ((2, ROWS, 128), F32, True),
         ),
         (
-            held, other, norm_gain.reshape(-1, 128), w_ssm_in.T, w_state_proj,
+            held, other, norm_gain.reshape(-1, 128), w_in, w_state_proj,
             jnp.transpose(conv_state, (1, 2, 0)), conv_weight, conv_bias[None],
         ),
-        fetched=(3,),
-        scratch=(pltpu.VMEM((channels, width), BF16), pltpu.SemaphoreType.DMA),
         cost=pl.CostEstimate(flops=COST, bytes_accessed=0, transcendentals=0),
     )
     paired = shifted(low[1], "seq_2", 1)
-    half = low[0] + paired
+    half = (low[0] + paired).astype(BF16)
     arrived = from_ring(half, "grp")
     attended = attended_rows(
         window_lengths, normed, w_query, key_projection, value_projection, *window_parts,

time: 93.1 us -> 87.5 us (0.940)
  local copies, waits for them, and re-layouts: 5.21 us -> 1.59 us
    unnamed x40, local copies, waits for them, and re-layouts: 4.44 us -> 0.82 us
    all_to_all x1, blocking collectives: 14.8 us -> 13.6 us  [block(): packed = lax.all_to_all(packed, PLANE, 0, 0, tiled=True)]
  transfers between devices with their start and end apart: 8 -> 8, of which waited for: 3 -> 4; matrix products, arithmetic and copies ran while one was open for 0% -> 0% of each run, Pallas kernels for 15% -> 16%
where the time goes in v7:
time: 87.5 us; the launch traced here: 87.2 us
  blocking collectives  58.4 us (67%)
  Pallas kernels  17.2 us (20%)
  waiting for transfers between devices  4.32 us (5%)
  starting transfers between devices  3.81 us (4%)
  local copies, waits for them, and re-layouts  1.59 us (2%)
  between operations  0.94 us (1%)
  other arithmetic  0.9 us (1%)
    all_to_all x1, blocking collectives, block(): held = lax.all_to_all(copies, CHIPS, 0, 0, tiled=True)  24.6 us
    all_to_all x1, blocking collectives, block(): arrived = lax.all_to_all(summed, CHIPS, 0, 0, tiled=True)  20.2 us
    all_to_all x1, blocking collectives, block(): packed = lax.all_to_all(packed, PLANE, 0, 0, tiled=True)  13.6 us
    pallas_call x1, Pallas kernels, window_rows(): pl.pallas_call(window_kernel, out_shape=(pltpu.HBM(early, BF16), pltpu.HB...  9.42 us
    pallas_call x6, Pallas kernels, vmem_call(): pl.pallas_call(kernel, out_shape=tuple((pltpu.VMEM(shape, dtype) if inner...  4.33 us
    ppermute x8, waiting for transfers between devices, shifted(): lax.ppermute(value, axis, [(i, (i + step) % size) for i in range(size)])  4.32 us
    ppermute x8, starting transfers between devices, shifted(): lax.ppermute(value, axis, [(i, (i + step) % size) for i in range(size)])  3.81 us
    pallas_call x1, Pallas kernels, attended_rows(): pl.pallas_call(attention_kernel, out_shape=pltpu.VMEM((SLOT, HEAD_SIZE),...  3.49 us
  transfers between devices with their start and end apart: 8, of which 4 were waited for; matrix products, arithmetic and copies ran while one was open for 0% of the time, Pallas kernels for 16%

profile of v7, /device:TPU:0, one launch (start us, length us, event | category | flops | bytes accessed | tf_op | source)
XLA Modules:
  0.0 87.2 jit_solution(3212869019003436502)
XLA Ops:
  0.6 0.8 broadcast_in_dim.15
  1.4 24.6 %all_to_all.15.near = bf16[64,32,96]{2,1,0:T(8,128)(2,1)S(1)} all-to-all(bf16[64,32,96]{2,1,0:T(8,128)(2,1)S(1)} %broadcast_in_dim.15), channel_id=1, replica_groups=mesh['grp'=4,'seq_0'=4,'seq_1'=4,'seq_2'=2] {'grp','seq_0','seq_1'}, dimensions={0} | all-to-all | bytes 786432 | tf_op jit(solution)/shard_map/all_to_all | solution.py:553
  26.0 9.4 %shard_map.248 = (bf16[2,512,256]{2,1,0:T(8,128)(2,1)}, bf16[2,512,256]{2,1,0:T(8,128)(2,1)}, bf16[1,512,256]{2,1,0:T(8,128)(2,1)S(1)}, bf16[1,512,256]{2,1,0:T(8,128)(2,1)S(1)}, bf16[64,4096]{1,0:T(8,128)(2,1)S(1)}) custom-call(s32[96]{0:T(128)} %lengths_hbm.3, bf16[3,512,4096]{2,1,0:T(8,128)(2,1)} %cached.1, bf16[4096,256]{1,0:T(8,128)(2,1)} %w_key.3, ...), custom_call_target="tpu_custom_call" | custom-call | tf_op jit(solution)/shard_map/pallas_call | solution.py:208
  35.6 1.3 %shard_map.249 = (bf16[4096,96]{1,0:T(8,128)(2,1)S(1)}, f32[64,96]{1,0:T(8,128)S(1)}, f32[2,144,128]{2,1,0:T(8,128)S(1)}) custom-call(bf16[64,32,96]{2,1,0:T(8,128)(2,1)S(1)} %all_to_all.15.near, bf16[64,32,96]{2,1,0:T(8,128)(2,1)S(1)} %collective-permute-done.far, f32[32,128]{1,0:T(8,128)S(1)} %bitcast.31, bf16[64,4096]{1,0:T(8,128)(2,1)S(1)} %get-tuple-element.17.w_in, ...), custom_call_target="tpu_custom_call" | custom-call | flops 8000000000 | tf_op jit(solution)/shard_map/pallas_call | solution.py:84
  36.9 0.8 collective-permute-start.1
  37.7 0.9 %collective-permute-done.1 = f32[144,128]{1,0:T(8,128)S(1)} collective-permute-done((f32[144,128]{1,0:T(8,128)S(1)}, f32[144,128]{1,0:T(8,128)S(1)}, u32[]{:S(2)}, u32[]{:S(2)}) %collective-permute-start.1) | collective-permute-done | bytes 73760 | tf_op jit(solution)/shard_map/ppermute | solution.py:50
  38.6 0.8 collective-permute-start.4
  39.4 1.5 %collective-permute-start.3 = (bf16[144,128]{1,0:T(8,128)(2,1)S(1)}, bf16[144,128]{1,0:T(8,128)(2,1)S(1)}, u32[]{:S(2)}, u32[]{:S(2)}) collective-permute-start(bf16[144,128]{1,0:T(8,128)(2,1)S(1)} %fusion.s0), channel_id=1, source_target_pairs={{0,64},{32,96},{64,0},{96,32},{1,65},{33,97},{65,1},{97,33},{2,66}... | collective-permute-start | bytes 110600 | tf_op jit(solution)/shard_map/ppermute | solution.py:50
  40.9 3.5 %shard_map.250.attended = f32[16,128]{1,0:T(8,128)S(1)} custom-call(s32[96]{0:T(128)} %lengths_hbm.3, bf16[4096,96]{1,0:T(8,128)(2,1)S(1)} %get-tuple-element.19.normed, bf16[4096,512]{1,0:T(8,128)(2,1)S(1)} %copy-done.2, bf16[4096,256]{1,0:T(8,128)(2,1)S(1)} %copy-done, bf16[4096,256]{1,0:T(8,128)(2,1)S(1)} %copy-done.1, ...), custom_call_target="tpu_custom_call" | custom-call | tf_op jit(solution)/shard_map/pallas_call | solution.py:403
  44.5 0.5 collective-permute-done.3.s2
  44.9 1.1 %collective-permute-done.2.s1 = bf16[144,128]{1,0:T(8,128)(2,1)S(1)} collective-permute-done((bf16[144,128]{1,0:T(8,128)(2,1)S(1)}, bf16[144,128]{1,0:T(8,128)(2,1)S(1)}, u32[]{:S(2)}, u32[]{:S(2)}) %collective-permute-start.2) | collective-permute-done | bytes 36896 | tf_op jit(solution)/shard_map/ppermute | solution.py:50
  46.2 13.6 %all_to_all.16.arrived = bf16[16,128,128]{2,1,0:T(8,128)(2,1)S(1)} all-to-all(bf16[16,128,128]{2,1,0:T(8,128)(2,1)S(1)} %shard_map.251), channel_id=1, replica_groups=mesh['grp'=4,'seq_0'=4,'seq_1'=4,'seq_2'=2] {'seq_0','seq_1'}, dimensions={0} | all-to-all | bytes 1048576 | tf_op jit(solution)/shard_map/all_to_all | solution.py:590
  60.0 0.5 collective-permute-start.6
  60.5 0.8 shard_map.253
  61.4 0.4 shard_map.254.term
  61.8 0.5 copy-done.7
  62.3 0.2 copy-done.8
  62.5 1.6 %shard_map.255 = (f32[16,64,96]{2,1,0:T(8,128)}, bf16[64,32,96]{2,1,0:T(8,128)(2,1)S(1)}, bf16[64,32,96]{2,1,0:T(8,128)(2,1)S(1)}) custom-call(f32[144,128]{1,0:T(8,128)S(1)} %get-tuple-element.24.near, f32[144,128]{1,0:T(8,128)S(1)} %collective-permute-done.5.far, bf16[256,128]{1,0:T(8,128)(2,1)S(1)} %get-tuple-element.25.near_rows, ...), custom_call_target="tpu_custom_call" | custom-call | tf_op jit(solution)/shard_map/pallas_call | solution.py:84
  64.1 0.2 collective-permute-start.7
  64.3 1.8 %collective-permute-done.7 = bf16[64,32,96]{2,1,0:T(8,128)(2,1)S(1)} collective-permute-done((bf16[64,32,96]{2,1,0:T(8,128)(2,1)S(1)}, bf16[64,32,96]{2,1,0:T(8,128)(2,1)S(1)}, u32[]{:S(2)}, u32[]{:S(2)}) %collective-permute-start.7) | collective-permute-done | bytes 393248 | tf_op jit(solution)/shard_map/ppermute | solution.py:50
  66.1 0.1 add_convert_fusion
  66.2 20.2 %all_to_all.17 = bf16[64,32,96]{2,1,0:T(8,128)(2,1)S(1)} all-to-all(bf16[64,32,96]{2,1,0:T(8,128)(2,1)S(1)} %add_convert_fusion), channel_id=1, replica_groups=mesh['grp'=4,'seq_0'=4,'seq_1'=4,'seq_2'=2] {'grp','seq_0','seq_1'}, dimensions={0} | all-to-all | bytes 786432 | tf_op jit(solution)/shard_map/all_to_all | solution.py:616
  86.4 0.1 convert_reduce_fusion
  86.6 0.6 fusion.1
  (49 shorter events, 0.5 us)
Async XLA Ops:
  26.0 9.5 %collective-permute-start = (bf16[64,32,96]{2,1,0:T(8,128)(2,1)S(1)}, bf16[64,32,96]{2,1,0:T(8,128)(2,1)S(1)}, u32[]{:S(2)}, u32[]{:S(2)}) collective-permute-start(bf16[64,32,96]{2,1,0:T(8,128)(2,1)S(1)} %all_to_all.15.near), channel_id=1, source_target_pairs={{0,1},{1,0},{2,3},{3,2},{4,5},{5,4},{6,7},{7,6},{8,9},{9,8},{10,11... | collective-permute-start | bytes 1179656 | tf_op jit(solution)/shard_map/ppermute | solution.py:50
  26.0 9.5 %copy-start.14 = (bf16[64,288]{1,0:T(8,128)(2,1)S(1)}, bf16[64,288]{1,0:T(8,128)(2,1)}, u32[]{:S(2)}) copy-start(bf16[64,288]{1,0:T(8,128)(2,1)} %w_proj.1) | copy-start | bytes 110596
  26.0 9.5 %copy-start.15 = (bf16[96,3,64]{0,2,1:T(8,128)(2,1)S(1)}, bf16[96,3,64]{0,2,1:T(8,128)(2,1)}, u32[]{:S(2)}) copy-start(bf16[96,3,64]{0,2,1:T(8,128)(2,1)} %param.31) | copy-start | bytes 110596
  26.0 9.5 %copy-start.16 = (f32[4096]{0:T(1024)S(1)}, f32[4096]{0:T(1024)}, u32[]{:S(2)}) copy-start(f32[4096]{0:T(1024)} %param.26) | copy-start | bytes 49156
  26.0 9.5 %copy-start.17 = (f32[4,64]{1,0:T(4,128)S(1)}, f32[4,64]{1,0:T(4,128)}, u32[]{:S(2)}) copy-start(f32[4,64]{1,0:T(4,128)} %taps.1) | copy-start | bytes 3076
  26.0 9.5 %copy-start.18 = (f32[64]{0:T(128)S(1)}, f32[64]{0:T(128)}, u32[]{:S(2)}) copy-start(f32[64]{0:T(128)} %param.30) | copy-start | bytes 772
  35.5 5.4 %copy-start = (bf16[4096,256]{1,0:T(8,128)(2,1)S(1)}, bf16[4096,256]{1,0:T(8,128)(2,1)}, u32[]{:S(2)}) copy-start(bf16[4096,256]{1,0:T(8,128)(2,1)} %w_key.3) | copy-start | bytes 6291460
  35.5 5.4 %copy-start.1 = (bf16[4096,256]{1,0:T(8,128)(2,1)S(1)}, bf16[4096,256]{1,0:T(8,128)(2,1)}, u32[]{:S(2)}) copy-start(bf16[4096,256]{1,0:T(8,128)(2,1)} %w_value.3) | copy-start | bytes 6291460
  35.5 5.4 %copy-start.2 = (bf16[4096,512]{1,0:T(8,128)(2,1)S(1)}, bf16[4096,512]{1,0:T(8,128)(2,1)}, u32[]{:S(2)}) copy-start(bf16[4096,512]{1,0:T(8,128)(2,1)} %w_query.1) | copy-start | bytes 12582916
  36.9 1.7 %collective-permute-start.1 = (f32[144,128]{1,0:T(8,128)S(1)}, f32[144,128]{1,0:T(8,128)S(1)}, u32[]{:S(2)}, u32[]{:S(2)}) collective-permute-start(f32[144,128]{1,0:T(8,128)S(1)} %slice_bitcast_fusion), channel_id=1, source_target_pairs={{0,1},{1,0},{2,3},{3,2},{4,5},{5,4},{6,7},{7,6},{8,9},{9,8},{10,11... | collective-permute-start | bytes 221192 | tf_op jit(solution)/shard_map/ppermute | solution.py:50
  38.6 5.9 %collective-permute-start.4 = (bf16[144,128]{1,0:T(8,128)(2,1)S(1)}, bf16[144,128]{1,0:T(8,128)(2,1)S(1)}, u32[]{:S(2)}, u32[]{:S(2)}) collective-permute-start(bf16[144,128]{1,0:T(8,128)(2,1)S(1)} %fusion.s0), channel_id=1, source_target_pairs={{0,96},{32,0},{64,32},{96,64},{1,97},{33,1},{65,33},{97,65},{2,98}... | collective-permute-start | bytes 110600 | tf_op jit(solution)/shard_map/ppermute | solution.py:50
  39.4 5.5 %collective-permute-start.3 = (bf16[144,128]{1,0:T(8,128)(2,1)S(1)}, bf16[144,128]{1,0:T(8,128)(2,1)S(1)}, u32[]{:S(2)}, u32[]{:S(2)}) collective-permute-start(bf16[144,128]{1,0:T(8,128)(2,1)S(1)} %fusion.s0), channel_id=1, source_target_pairs={{0,64},{32,96},{64,0},{96,32},{1,65},{33,97},{65,1},{97,33},{2,66}... | collective-permute-start | bytes 110600 | tf_op jit(solution)/shard_map/ppermute | solution.py:50
  40.9 5.2 %collective-permute-start.2 = (bf16[144,128]{1,0:T(8,128)(2,1)S(1)}, bf16[144,128]{1,0:T(8,128)(2,1)S(1)}, u32[]{:S(2)}, u32[]{:S(2)}) collective-permute-start(bf16[144,128]{1,0:T(8,128)(2,1)S(1)} %fusion.s0), channel_id=1, source_target_pairs={{0,32},{32,64},{64,96},{96,0},{1,33},{33,65},{65,97},{97,1},{2,34}... | collective-permute-start | bytes 110600 | tf_op jit(solution)/shard_map/ppermute | solution.py:50
  40.9 19.6 %copy-start.6 = (bf16[4096,64]{0,1:T(8,128)(2,1)S(1)}, bf16[4096,64]{0,1:T(8,128)(2,1)}, u32[]{:S(2)}) copy-start(bf16[4096,64]{0,1:T(8,128)(2,1)} %param.28) | copy-start | bytes 1572868
  44.4 16.1 %copy-start.4 = (bf16[4096,112]{0,1:T(8,128)(2,1)S(1)}, bf16[4096,112]{0,1:T(8,128)(2,1)}, u32[]{:S(2)}) copy-start(bf16[4096,112]{0,1:T(8,128)(2,1)} %param.43) | copy-start | bytes 2752516
  44.4 16.0 %copy-start.5 = (bf16[4096,112]{0,1:T(8,128)(2,1)S(1)}, bf16[4096,112]{0,1:T(8,128)(2,1)}, u32[]{:S(2)}) copy-start(bf16[4096,112]{0,1:T(8,128)(2,1)} %param.44) | copy-start | bytes 2752516
  59.8 1.6 %copy-start.3 = (bf16[112,4096]{1,0:T(8,128)(2,1)S(1)}, bf16[112,4096]{1,0:T(8,128)(2,1)}, u32[]{:S(2)}) copy-start(bf16[112,4096]{1,0:T(8,128)(2,1)} %w_mlp_down.1) | copy-start | bytes 2752516
  59.9 1.9 %collective-permute-start.5 = (f32[144,128]{1,0:T(8,128)S(1)}, f32[144,128]{1,0:T(8,128)S(1)}, u32[]{:S(2)}, u32[]{:S(2)}) collective-permute-start(f32[144,128]{1,0:T(8,128)S(1)} %get-tuple-element.24.near), channel_id=1, source_target_pairs={{0,1},{1,0},{2,3},{3,2},{4,5},{5,4},{6,7},{7,6},{8,9},{9,8},{10,11... | collective-permute-start | bytes 221192 | tf_op jit(solution)/shard_map/ppermute | solution.py:50
  60.0 1.8 %collective-permute-start.6 = (bf16[256,128]{1,0:T(8,128)(2,1)S(1)}, bf16[256,128]{1,0:T(8,128)(2,1)S(1)}, u32[]{:S(2)}, u32[]{:S(2)}) collective-permute-start(bf16[256,128]{1,0:T(8,128)(2,1)S(1)} %get-tuple-element.25.near_rows), channel_id=1, source_target_pairs={{0,1},{1,0},{2,3},{3,2},{4,5},{5,4},{6,7},{7,6},{8,9},{9,8},{10,11... | collective-permute-start | bytes 196616 | tf_op jit(solution)/shard_map/ppermute | solution.py:50
  61.3 1.2 %copy-start.8 = (bf16[64,4096]{1,0:T(8,128)(2,1)S(1)}, bf16[64,4096]{1,0:T(8,128)(2,1)}, u32[]{:S(2)}) copy-start(bf16[64,4096]{1,0:T(8,128)(2,1)} %w_out.1) | copy-start | bytes 1572868
  61.3 1.2 %copy-start.9 = (bf16[512,128]{1,0:T(8,128)(2,1)S(1)}, bf16[512,128]{1,0:T(8,128)(2,1)}, u32[]{:S(2)}) copy-start(bf16[512,128]{1,0:T(8,128)(2,1)} %w_attn.1) | copy-start | bytes 393220
  61.3 1.2 %copy-start.10 = (bf16[256,64]{0,1:T(8,128)(2,1)S(1)}, bf16[256,64]{0,1:T(8,128)(2,1)}, u32[]{:S(2)}) copy-start(bf16[256,64]{0,1:T(8,128)(2,1)} %param.33) | copy-start | bytes 98308
  64.1 22.5 %copy-start.19 = (bf16[96,32]{0,1:T(8,128)(2,1)S(1)}, bf16[96,32]{0,1:T(8,128)(2,1)}, u32[]{:S(2)}) copy-start(bf16[96,32]{0,1:T(8,128)(2,1)} %param.25) | copy-start | bytes 18436
  64.1 2.0 %collective-permute-start.7 = (bf16[64,32,96]{2,1,0:T(8,128)(2,1)S(1)}, bf16[64,32,96]{2,1,0:T(8,128)(2,1)S(1)}, u32[]{:S(2)}, u32[]{:S(2)}) collective-permute-start(bf16[64,32,96]{2,1,0:T(8,128)(2,1)S(1)} %get-tuple-element.30), channel_id=1, source_target_pairs={{0,1},{1,0},{2,3},{3,2},{4,5},{5,4},{6,7},{7,6},{8,9},{9,8},{10,11... | collective-permute-start | bytes 1179656 | tf_op jit(solution)/shard_map/ppermute | solution.py:50
  (4 other events, 4.6 us)
